TPU v7x, 32 devices: a whole 2x2x4 slice. The times are simulated.
32 devices in a mesh: dp: 4 (over y, x), ctx: 4 (over z), tp: 2 (over core).
Axes of the slice: x: 2, y: 2, z: 4, core: 2. Of those that a mesh axis runs over, the one named last changes fastest.
Arguments:
- tokens: bfloat16 [4, 2048, 1024], P('dp', 'ctx'), may hold values from -6 to 6
- query_weight: bfloat16 [1024, 1024], P('dp', 'tp'), may hold values from -0.1875 to 0.1875
- key_weight: bfloat16 [1024, 512], P('dp', 'tp'), may hold values from -0.1875 to 0.1875
- value_weight: bfloat16 [1024, 512], P('dp', 'tp'), may hold values from -0.1875 to 0.1875
- output_weight: bfloat16 [1024, 1024], P('tp', 'dp'), may hold values from -4 to 4
- gain_attn: bfloat16 [1024], P('dp'), may hold values from 0.5 to 1.5
- gain_moe: bfloat16 [1024], P('dp'), may hold values from 0.5 to 1.5
- expert_weights: bfloat16 [32, 3, 1024, 512], P('dp', None, None, 'tp'), may hold values from -0.375 to 0.375
- routes: int32 [4, 2048, 8], P('dp', 'ctx'), may hold values from 0 to 31, all different within a row
- gate_values: float32 [4, 2048, 8], P('dp', 'ctx'), may hold values from 0.05 to 0.2
- documents: int32 [4, 2048], P('dp', 'ctx'), may hold values from 0 to 2, never falling along the last dimension, each value on 1 to 1024 neighbouring positions
- pic_starts: int32 [4, 4], P('dp'), may hold values from 0 to 1792, as said below
- cotangent: bfloat16 [4, 2048, 1024], P('dp', 'ctx'), may hold values from -6 to 6
Outputs:
- layer_out: bfloat16 [4, 2048, 1024], P('dp', 'ctx')
- input_grad: bfloat16 [4, 2048, 1024], P('dp', 'ctx')
- query_w_grad: float32 [1024, 1024], P(('dp', 'ctx'), 'tp')
- key_w_grad: float32 [1024, 512], P(('dp', 'ctx'), 'tp')
- value_w_grad: float32 [1024, 512], P(('dp', 'ctx'), 'tp')
- output_w_grad: float32 [1024, 1024], P('tp', ('dp', 'ctx'))
- gain_attn_grad: float32 [1024], P(('dp', 'ctx'))
- gain_moe_grad: float32 [1024], P(('dp', 'ctx'))
- expert_grad: float32 [32, 3, 1024, 512], P('dp', None, 'ctx', 'tp')
Inputs may be any that keep to these rules, and one draw needn't show every extreme that they name: `routes`: each token names 8 different experts. `documents`: document numbers never fall along a sequence; a document holds at most 1024 positions. `pic_starts`: span j of a sequence lies inside positions j * (512) to (j + 1) (512) - 1.
All inputs are finite; a program needn't handle non-finite values.
Results may differ from a plain program's by a relative error of at most 0.02.
Values may be sent and summed in bfloat16 or wider, within the bound.
A program may use at most 448 MiB of HBM per device.

v0:
```python
import jax
import jax.numpy as jnp
from jax import lax
from jax.sharding import PartitionSpec as P

HEAD_DIM = 64
EXPERTS = 32
TOP = 8
PIC = 256
CAP = 144


EPSILON = 1e-06
THETA = 10000.0
NEG_FILL = -1e30


def rms_norm(tensor, gain_vec):
    return (
        tensor * lax.rsqrt(jnp.mean(tensor * tensor, axis=-1, keepdims=True) + EPSILON) * gain_vec
    )


def apply_rotary(tensor, token_positions):
    half_dim = tensor.shape[-1] // 2
    inverse = THETA ** (-(jnp.arange(half_dim, dtype=jnp.float32) * 2.0 / tensor.shape[-1]))
    angles = token_positions.astype(jnp.float32)[:, None] * inverse[None, :]
    cosine = jnp.cos(angles)[:, None, :]
    sine_of = jnp.sin(angles)[:, None, :]
    first_half = tensor[..., :half_dim]
    second_half = tensor[..., half_dim:]
    return jnp.concatenate(
        [first_half * cosine - second_half * sine_of, second_half * cosine + first_half * sine_of],
        axis=-1,
    )


def picture_of(starts, token_positions):
    inside = (token_positions[:, None] >= starts[None, :]) & (
        token_positions[:, None] < starts[None, :] + PIC
    )
    labels = jnp.arange(starts.shape[0], dtype=jnp.int32) + 1
    return jnp.sum(jnp.where(inside, labels[None, :], 0), axis=-1) - 1


def permitted(q_doc, q_pic, q_place, k_doc, k_pic, k_place):
    same_doc = q_doc[:, None] == k_doc[None, :]
    earlier = k_place[None, :] <= q_place[:, None]
    picture = (q_pic[:, None] >= 0) & (q_pic[:, None] == k_pic[None, :])
    return same_doc & (earlier | picture)


def dispatch(chosen):
    onehot = (chosen[:, None] == jnp.arange(EXPERTS, dtype=jnp.int32)[None, :]).astype(jnp.int32)
    before = jnp.cumsum(onehot, axis=0) - onehot
    position = jnp.sum(before * onehot, axis=-1)
    return jnp.where(position < CAP, chosen * CAP + position, EXPERTS * CAP)


def slot_table(slot_ids, tok_count):
    owners = jnp.arange(slot_ids.shape[0], dtype=jnp.int32) // TOP
    slot_owner = jnp.full((EXPERTS * CAP + 1,), tok_count, jnp.int32).at[slot_ids].set(owners)
    return slot_owner[: EXPERTS * CAP]


def expert_forward(weight_rows, slot_rows):
    gate_pre = jnp.einsum(
        "ecd,edf->ecf", slot_rows, weight_rows[:, 0], preferred_element_type=jnp.float32
    )
    up_pre = jnp.einsum(
        "ecd,edf->ecf", slot_rows, weight_rows[:, 1], preferred_element_type=jnp.float32
    )
    activation = (jax.nn.silu(gate_pre) * up_pre).astype(jnp.bfloat16)
    return jnp.einsum(
        "ecf,edf->ecd", activation, weight_rows[:, 2], preferred_element_type=jnp.float32
    )


def gated_product(gate_pre, up_pre):
    return jax.nn.silu(gate_pre) * up_pre


def expert_backward(weight_rows, slot_rows, slot_grads):
    gate_pre = jnp.einsum(
        "ecd,edf->ecf", slot_rows, weight_rows[:, 0], preferred_element_type=jnp.float32
    )
    up_pre = jnp.einsum(
        "ecd,edf->ecf", slot_rows, weight_rows[:, 1], preferred_element_type=jnp.float32
    )
    activation, pullback = jax.vjp(gated_product, gate_pre, up_pre)
    act_grad = jnp.einsum(
        "ecd,edf->ecf", slot_grads, weight_rows[:, 2], preferred_element_type=jnp.float32
    )
    gate_grad, up_grad = pullback(act_grad)
    gate_low = gate_grad.astype(jnp.bfloat16)
    up_low = up_grad.astype(jnp.bfloat16)
    act_low = activation.astype(jnp.bfloat16)
    input_back = jnp.einsum(
        "ecf,edf->ecd", gate_low, weight_rows[:, 0], preferred_element_type=jnp.float32
    )
    input_back = input_back + jnp.einsum(
        "ecf,edf->ecd", up_low, weight_rows[:, 1], preferred_element_type=jnp.float32
    )
    return (input_back, gate_low, up_low, act_low)


def expert_weight_grads(slot_rows, slot_grads, gate_low, up_low, act_low):
    gate_part = jnp.einsum("ecd,ecf->edf", slot_rows, gate_low, preferred_element_type=jnp.float32)
    up_part = jnp.einsum("ecd,ecf->edf", slot_rows, up_low, preferred_element_type=jnp.float32)
    down_part = jnp.einsum("ecd,ecf->edf", slot_grads, act_low, preferred_element_type=jnp.float32)
    return jnp.stack([gate_part, up_part, down_part], axis=1)


def body(
    tokens,
    query_weight,
    key_weight,
    value_weight,
    output_weight,
    gain_attn,
    gain_moe,
    expert_weights,
    routes,
    gate_values,
    documents,
    pic_starts,
    cotangent,
):
    seq_dev, block_len, model_width = tokens.shape
    ctx_size = lax.axis_size("ctx")
    length = block_len * ctx_size
    tok_rows = seq_dev * block_len
    offset = lax.axis_index("ctx") * block_len
    query_full, key_full, value_full, output_full, gain_one, gain_two = (
        lax.all_gather(query_weight, "dp", axis=0, tiled=True),
        lax.all_gather(key_weight, "dp", axis=0, tiled=True),
        lax.all_gather(value_weight, "dp", axis=0, tiled=True),
        lax.all_gather(output_weight, "dp", axis=1, tiled=True),
        lax.all_gather(gain_attn, "dp", axis=0, tiled=True),
        lax.all_gather(gain_moe, "dp", axis=0, tiled=True),
    )
    q_heads = query_full.shape[1] // HEAD_DIM
    kv_heads = key_full.shape[1] // HEAD_DIM
    query_groups = q_heads // kv_heads
    kv_width = kv_heads * HEAD_DIM
    score_scale = HEAD_DIM ** (-0.5)
    local_places = offset + jnp.arange(block_len, dtype=jnp.int32)
    all_places = jnp.arange(length, dtype=jnp.int32)
    pictures = jax.vmap(picture_of, in_axes=(0, None))(pic_starts, all_places)
    local_pics = lax.dynamic_slice_in_dim(pictures, offset, block_len, 1)

    def sum_heads(partial_sum):
        return lax.psum(partial_sum, "tp")

    x_flat = tokens.reshape(tok_rows, model_width).astype(jnp.float32)
    gain_first = gain_one.astype(jnp.float32)
    gain_second = gain_two.astype(jnp.float32)
    normed_one = rms_norm(x_flat, gain_first).astype(jnp.bfloat16)
    query_projected = jnp.dot(normed_one, query_full, preferred_element_type=jnp.float32).reshape(
        seq_dev, block_len, q_heads, HEAD_DIM
    )
    key_projected = jnp.dot(normed_one, key_full, preferred_element_type=jnp.float32).reshape(
        seq_dev, block_len, kv_heads, HEAD_DIM
    )
    value_low = jnp.dot(normed_one, value_full, preferred_element_type=jnp.float32).astype(
        jnp.bfloat16
    )
    query_rotated = apply_rotary(query_projected, local_places).astype(jnp.bfloat16)
    key_rotated = apply_rotary(key_projected, local_places).astype(jnp.bfloat16)
    q_group = query_rotated.reshape(seq_dev, block_len, kv_heads, query_groups, HEAD_DIM)
    kv_local = jnp.concatenate(
        [
            key_rotated.reshape(seq_dev, block_len, kv_width),
            value_low.reshape(seq_dev, block_len, kv_width),
        ],
        axis=-1,
    )
    kv_all, doc_all = (
        lax.all_gather(kv_local, "ctx", axis=1, tiled=True),
        lax.all_gather(documents.astype(jnp.bfloat16), "ctx", axis=1, tiled=True),
    )
    doc_keys = doc_all.astype(jnp.int32)
    starts = jnp.arange(ctx_size, dtype=jnp.int32) * block_len
    stat_shape = (seq_dev, kv_heads, query_groups, block_len)
    acc_shape = (seq_dev, block_len, kv_heads, query_groups, HEAD_DIM)

    def key_block(first_row, row_count):
        kv_part = lax.dynamic_slice_in_dim(kv_all, first_row, row_count, 1)
        key_rows = kv_part[..., :kv_width].reshape(seq_dev, row_count, kv_heads, HEAD_DIM)
        val_rows = kv_part[..., kv_width:].reshape(seq_dev, row_count, kv_heads, HEAD_DIM)
        raw_scores = jnp.einsum(
            "sqhgd,skhd->shgqk", q_group, key_rows, preferred_element_type=jnp.float32
        )
        k_places = first_row + jnp.arange(row_count, dtype=jnp.int32)
        k_docs = lax.dynamic_slice_in_dim(doc_keys, first_row, row_count, 1)
        k_pics = lax.dynamic_slice_in_dim(pictures, first_row, row_count, 1)
        allowed = jax.vmap(permitted, in_axes=(0, 0, None, 0, 0, None))(
            documents, local_pics, local_places, k_docs, k_pics, k_places
        )
        scores = jnp.where(allowed[:, None, None], raw_scores * score_scale, -jnp.inf)
        return (scores, key_rows, val_rows)

    def stat_step(stat_carry, first_row):
        run_max, run_sum = stat_carry
        scores = key_block(first_row, block_len)[0]
        new_max = jnp.maximum(run_max, jnp.max(scores, axis=-1))
        run_sum = run_sum * jnp.exp(run_max - new_max) + jnp.sum(
            jnp.exp(scores - new_max[..., None]), axis=-1
        )
        return ((new_max, run_sum), None)

    stats = lax.scan(
        stat_step,
        (jnp.full(stat_shape, NEG_FILL, jnp.float32), jnp.zeros(stat_shape, jnp.float32)),
        starts,
    )[0]
    log_total = stats[0] + jnp.log(stats[1])

    def mix_step(running, first_row):
        scores, key_rows, val_rows = key_block(first_row, block_len)
        probs_low = jnp.exp(scores - log_total[..., None]).astype(jnp.bfloat16)
        return (
            running
            + jnp.einsum(
                "shgqk,skhd->sqhgd", probs_low, val_rows, preferred_element_type=jnp.float32
            ),
            None,
        )

    expert_mixture = lax.scan(mix_step, jnp.zeros(acc_shape, jnp.float32), starts)[0]
    mixture_low = expert_mixture.reshape(tok_rows, q_heads * HEAD_DIM).astype(jnp.bfloat16)
    attention_output = sum_heads(
        jnp.dot(mixture_low, output_full, preferred_element_type=jnp.float32)
    )
    hidden = x_flat + attention_output
    normed_two = rms_norm(hidden, gain_second).astype(jnp.bfloat16)
    chosen = routes.reshape(tok_rows * TOP)
    pair_gates = gate_values.reshape(tok_rows * TOP)
    slot_ids = dispatch(chosen)
    slot_owner = slot_table(slot_ids, tok_rows)
    slot_gate = (
        jnp.zeros((EXPERTS * CAP + 1,), jnp.float32).at[slot_ids].set(pair_gates)[: EXPERTS * CAP]
    )
    padded_two = jnp.concatenate([normed_two, jnp.zeros((1, model_width), jnp.bfloat16)], axis=0)
    slot_rows = padded_two[slot_owner].reshape(EXPERTS, CAP, model_width)

    def sweep(piece_fn):
        return piece_fn(lax.all_gather(expert_weights, "dp", axis=0, tiled=True), jnp.int32(0))

    def forward_piece(weight_rows, first_row):
        return expert_forward(weight_rows, slot_rows)

    slot_out = sweep(forward_piece)
    flat_out = jnp.concatenate(
        [slot_out.reshape(EXPERTS * CAP, model_width), jnp.zeros((1, model_width), jnp.float32)],
        axis=0,
    )
    moe_part = jnp.sum(
        flat_out[slot_ids].reshape(tok_rows, TOP, model_width)
        * pair_gates.reshape(tok_rows, TOP)[:, :, None],
        axis=1,
    )
    layer_out = hidden + sum_heads(moe_part)
    out_grad = cotangent.reshape(tok_rows, model_width).astype(jnp.float32)
    padded_grad = jnp.concatenate([out_grad, jnp.zeros((1, model_width), jnp.float32)], axis=0)
    slot_grads = (
        (padded_grad[slot_owner] * slot_gate[:, None])
        .astype(jnp.bfloat16)
        .reshape(EXPERTS, CAP, model_width)
    )
    ff_width = expert_weights.shape[3]

    def backward_piece(weight_rows, first_row):
        row_count = weight_rows.shape[0]
        pieces = expert_backward(weight_rows, slot_rows, slot_grads)
        return jnp.concatenate(
            [
                pieces[0],
                pieces[1].astype(jnp.float32),
                pieces[2].astype(jnp.float32),
                pieces[3].astype(jnp.float32),
            ],
            axis=-1,
        )

    joined = sweep(backward_piece)
    slot_back = joined[..., :model_width]
    gate_low = joined[..., model_width : model_width + ff_width].astype(jnp.bfloat16)
    up_low = joined[..., model_width + ff_width : model_width + 2 * ff_width].astype(jnp.bfloat16)
    act_low = joined[..., model_width + 2 * ff_width :].astype(jnp.bfloat16)
    expert_part = lax.psum_scatter(
        expert_weight_grads(slot_rows, slot_grads, gate_low, up_low, act_low).astype(jnp.bfloat16),
        "dp",
        scatter_dimension=0,
        tiled=True,
    )
    flat_back = jnp.concatenate(
        [slot_back.reshape(EXPERTS * CAP, model_width), jnp.zeros((1, model_width), jnp.float32)],
        axis=0,
    )
    normed_two_grad = sum_heads(
        jnp.sum(flat_back[slot_ids].reshape(tok_rows, TOP, model_width), axis=1)
    )
    hidden_pull = jax.vjp(rms_norm, hidden, gain_second)[1]
    hidden_norm_grad, gain_second_grad = hidden_pull(normed_two_grad)
    hidden_grad = out_grad + hidden_norm_grad
    hidden_low = hidden_grad.astype(jnp.bfloat16)
    output_grad = jnp.einsum(
        "re,rd->ed", mixture_low, hidden_low, preferred_element_type=jnp.float32
    )
    mix_grad = (
        jnp.einsum("rd,ed->re", hidden_low, output_full, preferred_element_type=jnp.float32)
        .astype(jnp.bfloat16)
        .reshape(acc_shape)
    )

    def delta_step(running, first_row):
        scores, key_rows, val_rows = key_block(first_row, block_len)
        attn_probs = jnp.exp(scores - log_total[..., None])
        prob_grad = jnp.einsum(
            "sqhgd,skhd->shgqk", mix_grad, val_rows, preferred_element_type=jnp.float32
        )
        return (running + jnp.sum(attn_probs * prob_grad, axis=-1), None)

    row_delta = lax.scan(delta_step, jnp.zeros(stat_shape, jnp.float32), starts)[0]

    def score_grads(scores, val_rows):
        attn_probs = jnp.exp(scores - log_total[..., None])
        prob_grad = jnp.einsum(
            "sqhgd,skhd->shgqk", mix_grad, val_rows, preferred_element_type=jnp.float32
        )
        score_low = (attn_probs * (prob_grad - row_delta[..., None]) * score_scale).astype(
            jnp.bfloat16
        )
        return (attn_probs, score_low)

    def query_step(running, first_row):
        scores, key_rows, val_rows = key_block(first_row, block_len)
        score_low = score_grads(scores, val_rows)[1]
        return (
            running
            + jnp.einsum(
                "shgqk,skhd->sqhgd", score_low, key_rows, preferred_element_type=jnp.float32
            ),
            None,
        )

    q_rot_grad = lax.scan(query_step, jnp.zeros(acc_shape, jnp.float32), starts)[0]
    row_count = block_len * lax.axis_size("ctx")
    scores, key_rows, val_rows = key_block(jnp.int32(0), row_count)
    attn_probs, score_low = score_grads(scores, val_rows)
    val_grad = jnp.einsum(
        "shgqk,sqhgd->skhd",
        attn_probs.astype(jnp.bfloat16),
        mix_grad,
        preferred_element_type=jnp.float32,
    )
    key_grad = jnp.einsum(
        "shgqk,sqhgd->skhd", score_low, q_group, preferred_element_type=jnp.float32
    )
    joined_kv = jnp.concatenate(
        [
            key_grad.reshape(seq_dev, row_count, kv_width),
            val_grad.reshape(seq_dev, row_count, kv_width),
        ],
        axis=-1,
    )
    kv_term = lax.psum_scatter(
        jnp.transpose(joined_kv, (1, 0, 2)), "ctx", scatter_dimension=0, tiled=True
    )
    kv_back = jnp.transpose(kv_term, (1, 0, 2))
    k_rot_grad = kv_back[..., :kv_width].reshape(seq_dev, block_len, kv_heads, HEAD_DIM)
    value_grad_low = kv_back[..., kv_width:].reshape(tok_rows, kv_width).astype(jnp.bfloat16)

    def rotate_here(tensor):
        return apply_rotary(tensor, local_places)

    query_grad_low = (
        jax.vjp(rotate_here, query_projected)[1](
            q_rot_grad.reshape(seq_dev, block_len, q_heads, HEAD_DIM)
        )[0]
        .reshape(tok_rows, q_heads * HEAD_DIM)
        .astype(jnp.bfloat16)
    )
    key_grad_low = (
        jax.vjp(rotate_here, key_projected)[1](k_rot_grad)[0]
        .reshape(tok_rows, kv_width)
        .astype(jnp.bfloat16)
    )
    query_w_grad = jnp.einsum(
        "rd,re->de", normed_one, query_grad_low, preferred_element_type=jnp.float32
    )
    key_w_grad = jnp.einsum(
        "rd,re->de", normed_one, key_grad_low, preferred_element_type=jnp.float32
    )
    value_w_grad = jnp.einsum(
        "rd,re->de", normed_one, value_grad_low, preferred_element_type=jnp.float32
    )
    normed_one_part = jnp.einsum(
        "re,de->rd", query_grad_low, query_full, preferred_element_type=jnp.float32
    )
    normed_one_part = normed_one_part + jnp.einsum(
        "re,de->rd", key_grad_low, key_full, preferred_element_type=jnp.float32
    )
    normed_one_part = normed_one_part + jnp.einsum(
        "re,de->rd", value_grad_low, value_full, preferred_element_type=jnp.float32
    )
    normed_one_grad = sum_heads(normed_one_part)
    x_pull = jax.vjp(rms_norm, x_flat, gain_first)[1]
    x_norm_grad, gain_first_grad = x_pull(normed_one_grad)
    input_grad = (
        (hidden_grad + x_norm_grad).astype(jnp.bfloat16).reshape(seq_dev, block_len, model_width)
    )
    attn_sums = (
        lax.psum_scatter(
            query_w_grad.astype(jnp.bfloat16), "dp", scatter_dimension=0, tiled=True
        ).astype(jnp.float32),
        lax.psum_scatter(
            key_w_grad.astype(jnp.bfloat16), "dp", scatter_dimension=0, tiled=True
        ).astype(jnp.float32),
        lax.psum_scatter(
            value_w_grad.astype(jnp.bfloat16), "dp", scatter_dimension=0, tiled=True
        ).astype(jnp.float32),
        lax.psum_scatter(
            output_grad.astype(jnp.bfloat16), "dp", scatter_dimension=1, tiled=True
        ).astype(jnp.float32),
        lax.psum_scatter(
            gain_first_grad.astype(jnp.bfloat16), "dp", scatter_dimension=0, tiled=True
        ).astype(jnp.float32),
        lax.psum_scatter(
            gain_second_grad.astype(jnp.bfloat16), "dp", scatter_dimension=0, tiled=True
        ).astype(jnp.float32),
    )
    owned = (
        lax.psum_scatter(
            attn_sums[0].astype(jnp.bfloat16), "ctx", scatter_dimension=0, tiled=True
        ).astype(jnp.float32),
        lax.psum_scatter(
            attn_sums[1].astype(jnp.bfloat16), "ctx", scatter_dimension=0, tiled=True
        ).astype(jnp.float32),
        lax.psum_scatter(
            attn_sums[2].astype(jnp.bfloat16), "ctx", scatter_dimension=0, tiled=True
        ).astype(jnp.float32),
        lax.psum_scatter(
            attn_sums[3].astype(jnp.bfloat16), "ctx", scatter_dimension=1, tiled=True
        ).astype(jnp.float32),
        lax.psum_scatter(
            attn_sums[4].astype(jnp.bfloat16), "ctx", scatter_dimension=0, tiled=True
        ).astype(jnp.float32),
        lax.psum_scatter(
            attn_sums[5].astype(jnp.bfloat16), "ctx", scatter_dimension=0, tiled=True
        ).astype(jnp.float32),
        lax.psum_scatter(expert_part, "ctx", scatter_dimension=2, tiled=True).astype(jnp.float32),
    )
    return (
        layer_out.astype(jnp.bfloat16).reshape(seq_dev, block_len, model_width),
        input_grad,
        owned[0],
        owned[1],
        owned[2],
        owned[3],
        owned[4],
        owned[5],
        owned[6],
    )


def solution(mesh):
    return jax.shard_map(
        body,
        mesh=mesh,
        in_specs=(
            P("dp", "ctx", None),
            P("dp", "tp"),
            P("dp", "tp"),
            P("dp", "tp"),
            P("tp", "dp"),
            P("dp"),
            P("dp"),
            P("dp", None, None, "tp"),
            P("dp", "ctx", None),
            P("dp", "ctx", None),
            P("dp", "ctx"),
            P("dp", None),
            P("dp", "ctx", None),
        ),
        out_specs=(
            P("dp", "ctx", None),
            P("dp", "ctx", None),
            P(("dp", "ctx"), "tp"),
            P(("dp", "ctx"), "tp"),
            P(("dp", "ctx"), "tp"),
            P("tp", ("dp", "ctx")),
            P(("dp", "ctx")),
            P(("dp", "ctx")),
            P("dp", None, "ctx", "tp"),
        ),
        check_vma=False,
    )
```

profile of v0, /device:TPU:0, one launch (start us, length us, event | category | flops | bytes accessed | tf_op | source)
XLA Modules:
  0.0 2297.8 jit_solution(4786808142977648415)
XLA Ops:
  8.0 11.9 all_gather.30
  19.9 11.5 all_gather.29
  46.6 12.6 all_gather.32
  61.9 29.6 %all-gather.7.cloned.1.call-done = bf16[1,2048,512]{1,2,0:T(8,128)(2,1)} async-done(((bf16[1,512,512]{1,2,0:T(8,128)(2,1)}), bf16[1,2048,512]{1,2,0:T(8,128)(2,1)}) %all-gather.7.cloned.1.call-update) | async-done | bytes 2097168 | tf_op jit(solution)/shard_map/all_gather | solution.py:179
  91.6 61.7 %while.46 = (s32[]{:T(128)}, f32[1,4,2,512]{3,2,1,0:T(2,128)S(1)}, f32[1,4,2,512]{3,2,1,0:T(2,128)S(1)}, s32[1,512]{1,0:T(1,128)S(1)}, s32[4]{0:T(128)}, /*index...) while((s32[]{:T(128)}, f32[1,4,2,512]{3,2,1,0:T(2,128)S(1)}, ...), condition=%wide.region_5.6_spmd.clone, body=%wide.region_2.5_spmd.clone.sunk | while | flops 284710400 | bytes 19115220 | solution.py:212
  153.3 41.9 %while.47 = (s32[]{:T(128)}, f32[1,512,4,2,64]{1,4,3,2,0:T(8,128)}, s32[4]{0:T(128)}, bf16[1,2048,512]{1,2,0:T(8,128)(2,1)}, s32[1,512]{1,0:T(1,128)S(1)}, /*ind...) while((s32[]{:T(128)}, f32[1,512,4,2,64]{1,4,3,2,0:T(8,128)}, ...), condition=%wide.region_7.8_spmd.clone, body=%wide.region_6.7_spmd.clone.sunk | while | flops 547358208 | bytes 4762861 | solution.py:230
  200.3 10.6 copy.67
  212.1 8.4 all-gather.1
  220.6 9.2 reduce-window.6
  232.1 15.5 scatter_custom_fusion
  248.2 15.5 scatter_custom_fusion.1
  263.9 15.2 gather_fusion.2
  285.5 14.9 gather_fusion
  300.4 360.0 %all-gather.13.cloned.1.call-done = bf16[32,3,1024,256]{3,2,0,1:T(8,128)(2,1)} async-done(((bf16[8,3,1024,256]{3,2,0,1:T(8,128)(2,1)}), bf16[32,3,1024,256]{3,2,0,1:T(8,128)(2,1)}) %all-gather.13.cloned.1.call-update) | async-done | bytes 50331664 | tf_op jit(solution)/shard_map/all_gather | solution.py:248
  660.4 13.3 fusion.73
  673.7 13.3 fusion.75
  687.0 20.6 multiply_convert_fusion.1
  707.5 13.6 fusion.72
  721.2 19.0 fusion.78
  740.2 15.1 concatenate.58
  755.3 28.6 %gather_fusion.3 = f32[4096,1024]{1,0:T(8,128)} fusion(f32[4609,1024]{1,0:T(8,128)} %concatenate.58, s32[4096]{0:T(1024)S(1)} %broadcast_clamp_fusion), kind=kCustom, calls=%fused_computation.3 | custom fusion | bytes 33570816 | tf_op jit(solution)/shard_map/gather | solution.py:302
  783.9 9.5 bitcast_reduce_fusion
  794.7 14.1 fusion.118
  822.6 39.2 %while.48 = (s32[]{:T(128)}, f32[1,4,2,512]{3,2,1,0:T(2,128)S(1)}, s32[1,512]{1,0:T(1,128)S(1)}, s32[4]{0:T(128)}, s32[1,2048]{1,0:T(1,128)}, /*index=5*/s32[1,5...) while((s32[]{:T(128)}, f32[1,4,2,512]{3,2,1,0:T(2,128)S(1)}, ...), condition=%wide.region_22.23_spmd.clone, body=%wide.region_20.22_spmd.clone.sunk | while | flops 548935168 | bytes 20032756 | solution.py:325
  861.7 16.3 fusion.69
  878.1 20.4 fusion.66
  903.3 11.7 convert_bitcast_fusion.1
  918.6 78.3 %while.49 = (s32[]{:T(128)}, f32[1,512,4,2,64]{1,4,3,2,0:T(8,128)}, s32[4]{0:T(128)}, bf16[1,2048,512]{1,2,0:T(8,128)(2,1)S(1)}, s32[1,512]{1,0:T(1,128)S(1)}, /...) while((s32[]{:T(128)}, f32[1,512,4,2,64]{1,4,3,2,0:T(8,128)}, ...), condition=%wide.region_24.25_spmd.clone, body=%wide.region_23.24_spmd.clone.sunk | while | flops 822085120 | bytes 22342908 | solution.py:348
  949.4 8.3 fusion.226
  968.9 8.3 fusion.226
  988.5 8.4 fusion.226
  1002.6 16.2 convert_bitcast_fusion
  1022.4 11.2 convert_bitcast_fusion.2
  1036.2 34.3 %pad_maximum_fusion = bf16[32,3,1024,256]{3,2,0,1:T(8,128)(2,1)} fusion(bf16[32,1,1024,256]{3,2,0,1:T(8,128)(2,1)} %convert_bitcast_fusion, bf16[32,1,1024,256]{3,2,0,1:T(8,128)(2,1)} %convert_bitcast_fusion.1, bf16[32,1,1024,256]{3,2,0,1:T(8,128)(2,1)} %convert_bitcast_fusion.2), kind=kLoop, calls=%fused_computation.90 | loop fusion | flops 50331648 | bytes 100663296 | tf_op jit(solution)/shard_map/stack | solution.py:111
  1074.0 12.9 fusion.77
  1086.9 15.2 concatenate.56
  1102.1 28.8 %gather_fusion.1 = f32[4096,1024]{1,0:T(8,128)} fusion(f32[4609,1024]{1,0:T(8,128)} %concatenate.56, s32[4096]{0:T(1024)S(1)} %copy-done.48), kind=kCustom, calls=%fused_computation.1 | custom fusion | bytes 33570816 | tf_op jit(solution)/shard_map/gather | solution.py:259
  1131.0 9.9 fusion.68
  1149.9 805.3 %all-reduce.25.cloned.1.call-done = bf16[32,3,1024,256]{3,2,0,1:T(8,128)(2,1)} async-done(((bf16[32,3,1024,256]{3,2,0,1:T(8,128)(2,1)}), bf16[32,3,1024,256]{3,2,0,1:T(8,128)(2,1)}) %all-reduce.25.cloned.1.call-update) | async-done | bytes 50331664
  1955.2 10.5 constant_dynamic-slice_fusion.15
  1967.8 12.6 reduce-scatter.34.cloned.1.call-done
  1982.1 18.6 reduce-scatter.20.cloned.1.call-done
  2002.3 18.3 reduce-scatter.24.cloned.1.call-done
  2021.9 18.4 reduce-scatter.28.cloned.1.call-done
  2041.7 28.1 %all-reduce.27.cloned.1.call-done = (f32[512,1024]{1,0:T(8,128)}, f32[512,1024]{1,0:T(8,128)}) async-done(((f32[512,1024]{1,0:T(8,128)}, f32[512,1024]{1,0:T(8,128)}), (f32[512,1024]{1,0:T(8,128)}, f32[512,1024]{1,0:T(8,128)})) %all-reduce.27.cloned.1.call-update) | async-done | bytes 4194320 | tf_op jit(solution)/shard_map/psum | solution.py:153
  2072.2 10.1 all-reduce.15
  2082.4 12.3 all-reduce.14
  2100.4 185.0 %reduce-scatter.32.cloned.1.call-done = bf16[8,3,256,256]{3,2,0,1:T(8,128)(2,1)} async-done(((bf16[8,3,1024,256]{3,2,0,1:T(8,128)(2,1)}), bf16[8,3,256,256]{3,2,0,1:T(8,128)(2,1)}) %reduce-scatter.32.cloned.1.call-update) | async-done | bytes 3145744 | tf_op jit(solution)/shard_map/reduce_scatter | solution.py:453
  (422 shorter events, 265.1 us)
Async XLA Ops:
  7.2 36.6 %copy-start.12 = (bf16[1,512,1024]{2,1,0:T(8,128)(2,1)S(1)}, bf16[1,512,1024]{2,1,0:T(8,128)(2,1)}, u32[]{:S(2)}) copy-start(bf16[1,512,1024]{2,1,0:T(8,128)(2,1)} %param.21) | copy-start | bytes 3145732
  7.2 52.2 %all-gather.9.cloned.1.call-start = ((), (), s32[]{:S(2)}) async-start(), calls=%async_computation.11 | async-start | bytes 1310720 | tf_op jit(solution)/shard_map/all_gather | solution.py:135
  7.9 83.7 %all-gather.7.cloned.1.call-start = ((), (), s32[]{:S(2)}) async-start(), calls=%async_computation.10 | async-start | bytes 2621440 | tf_op jit(solution)/shard_map/all_gather | solution.py:179
  19.9 24.5 %copy-start.28 = (bf16[1024,256]{1,0:T(8,128)(2,1)}, bf16[1024,256]{1,0:T(8,128)(2,1)S(1)}, u32[]{:S(2)}) copy-start(bf16[1024,256]{1,0:T(8,128)(2,1)S(1)} %all_gather.30) | copy-start | bytes 1572868
  38.8 22.0 copy-start.54
  41.3 19.5 copy-start.62
  41.3 17.8 copy-start.67
  43.6 18.1 copy-start.31
  43.6 18.1 copy-start.33
  45.2 151.6 %all-gather.11.cloned.1.call-start = ((), (), s32[]{:S(2)}) async-start(), calls=%async_computation.12 | async-start | bytes 1310720 | tf_op jit(solution)/shard_map/all_gather | solution.py:138
  46.0 235.9 %all-reduce.21.cloned.1.call-start = ((), (), s32[]{:S(2)}) async-start(), calls=%async_computation.13 | async-start | bytes 4194304 | tf_op jit(solution)/shard_map/psum | solution.py:153
  61.9 29.7 %copy-start.23 = (bf16[1,512,8,32]{1,3,2,0:T(8,128)(2,1)}, bf16[1,512,8,32]{1,3,2,0:T(8,128)(2,1)S(1)}, u32[]{:S(2)}) copy-start(bf16[1,512,8,32]{1,3,2,0:T(8,128)(2,1)S(1)} %get-tuple-element.598) | copy-start | bytes 786436
  61.9 29.7 %copy-start.26 = (bf16[1,512,8,32]{1,3,2,0:T(8,128)(2,1)}, bf16[1,512,8,32]{1,3,2,0:T(8,128)(2,1)S(1)}, u32[]{:S(2)}) copy-start(bf16[1,512,8,32]{1,3,2,0:T(8,128)(2,1)S(1)} %get-tuple-element.599) | copy-start | bytes 786436
  195.3 83.8 %copy-start.21 = (s32[1,512]{1,0:T(1,128)}, s32[1,512]{1,0:T(1,128)S(1)}, u32[]{:S(2)}) copy-start(s32[1,512]{1,0:T(1,128)S(1)} %get-tuple-element.1181) | copy-start | bytes 6148
  195.3 83.8 %copy-start.39 = (s32[1,512]{1,0:T(1,128)}, s32[1,512]{1,0:T(1,128)S(1)}, u32[]{:S(2)}) copy-start(s32[1,512]{1,0:T(1,128)S(1)} %get-tuple-element.1195) | copy-start | bytes 6148
  195.3 83.8 %copy-start.41 = (s32[1,2048]{1,0:T(1,128)}, s32[1,2048]{1,0:T(1,128)S(1)}, u32[]{:S(2)}) copy-start(s32[1,2048]{1,0:T(1,128)S(1)} %get-tuple-element.1202) | copy-start | bytes 24580
  195.3 83.8 %copy-start.45 = (s32[1,2048]{1,0:T(1,128)}, s32[1,2048]{1,0:T(1,128)S(1)}, u32[]{:S(2)}) copy-start(s32[1,2048]{1,0:T(1,128)S(1)} %get-tuple-element.1205) | copy-start | bytes 24580
  200.3 460.1 %all-gather.13.cloned.1.call-start = ((), (), s32[]{:S(2)}) async-start(), calls=%async_computation.14 | async-start | bytes 62914560 | tf_op jit(solution)/shard_map/all_gather | solution.py:248
  211.0 20.2 copy-start.49
  211.0 36.7 %copy-start.20 = (bf16[1,512,1024]{2,1,0:T(8,128)(2,1)S(1)}, bf16[1,512,1024]{2,1,0:T(8,128)(2,1)}, u32[]{:S(2)}) copy-start(bf16[1,512,1024]{2,1,0:T(8,128)(2,1)} %param.33) | copy-start | bytes 3145732
  211.0 603.9 %all-reduce.23.cloned.1.call-start = ((), (), s32[]{:S(2)}) async-start(), calls=%async_computation.15 | async-start | bytes 4194304 | tf_op jit(solution)/shard_map/psum | solution.py:153
  220.6 63.3 %copy-start.52 = (f32[4,1,256]{2,1,0:T(1,128)}, f32[4,1,256]{2,1,0:T(1,128)S(1)}, u32[]{:S(2)}) copy-start(f32[4,1,256]{2,1,0:T(1,128)S(1)} %convert_element_type.266) | copy-start | bytes 12292
  263.8 423.1 %copy-start.46 = (f32[32,144]{1,0:T(8,128)}, f32[32,144]{1,0:T(8,128)S(1)}, u32[]{:S(2)}) copy-start(f32[32,144]{1,0:T(8,128)S(1)} %mul.467) | copy-start | bytes 55300
  279.0 476.3 %copy-start.47 = (s32[4096]{0:T(1024)}, s32[4096]{0:T(1024)S(1)}, u32[]{:S(2)}) copy-start(s32[4096]{0:T(1024)S(1)} %broadcast_clamp_fusion) | copy-start | bytes 49156
  793.4 225.4 %reduce-scatter.16.cloned.1.call-start = ((), (), s32[]{:S(2)}) async-start(), calls=%async_computation.16 | async-start | bytes 5242880 | tf_op jit(solution)/shard_map/reduce_scatter | solution.py:368
  794.7 20.2 copy-start.53
  794.7 20.2 copy-start.57
  794.7 23.8 %copy-start.61 = (f32[512]{0:T(512)S(1)}, f32[512]{0:T(512)}, u32[]{:S(2)}) copy-start(f32[512]{0:T(512)} %copy-done.60) | copy-start | bytes 6148
  903.3 168.8 %reduce-scatter.30.cloned.1.call-start = ((), (), s32[]{:S(2)}) async-start(), calls=%async_computation.23 | async-start | bytes 1310720 | tf_op jit(solution)/shard_map/reduce_scatter | solution.py:424
  918.5 212.4 %reduce-scatter.18.cloned.1.call-start = ((), (), s32[]{:S(2)}) async-start(), calls=%async_computation.17 | async-start | bytes 1310720 | tf_op jit(solution)/shard_map/reduce_scatter | solution.py:415
  918.5 78.3 %copy-start.32 = (f32[512,32]{0,1:T(8,128)S(1)}, f32[512,32]{0,1:T(8,128)}, u32[]{:S(2)}) copy-start(f32[512,32]{0,1:T(8,128)} %copy-done.31) | copy-start | bytes 196612
  918.5 78.3 %copy-start.34 = (f32[512,32]{0,1:T(8,128)S(1)}, f32[512,32]{0,1:T(8,128)}, u32[]{:S(2)}) copy-start(f32[512,32]{0,1:T(8,128)} %copy-done.33) | copy-start | bytes 196612
  1002.5 139.1 %reduce-scatter.22.cloned.1.call-start = ((), (), s32[]{:S(2)}) async-start(), calls=%async_computation.19 | async-start | bytes 655360 | tf_op jit(solution)/shard_map/reduce_scatter | solution.py:418
  1002.6 18.3 copy-start.13
  1002.6 18.3 copy-start.55
  1002.6 18.3 copy-start.63
  1022.3 122.3 %reduce-scatter.26.cloned.1.call-start = ((), (), s32[]{:S(2)}) async-start(), calls=%async_computation.21 | async-start | bytes 655360 | tf_op jit(solution)/shard_map/reduce_scatter | solution.py:421
  1036.2 919.1 %all-reduce.25.cloned.1.call-start = ((), (), s32[]{:S(2)}) async-start(), calls=%async_computation.26 | async-start | bytes 100663296
  1070.6 909.8 %reduce-scatter.34.cloned.1.call-start = ((), (), s32[]{:S(2)}) async-start(), calls=%async_computation.25 | async-start | bytes 327680
  1073.9 926.8 %reduce-scatter.20.cloned.1.call-start = ((), (), s32[]{:S(2)}) async-start(), calls=%async_computation.18 | async-start | bytes 327680 | tf_op jit(solution)/shard_map/reduce_scatter | solution.py:435
  1102.1 28.9 %copy-start.35 = (f32[512,8]{1,0:T(8,128)S(1)}, f32[512,8]{1,0:T(8,128)}, u32[]{:S(2)}) copy-start(f32[512,8]{1,0:T(8,128)} %copy.68) | copy-start | bytes 49156
  1130.9 889.6 %reduce-scatter.24.cloned.1.call-start = ((), (), s32[]{:S(2)}) async-start(), calls=%async_computation.20 | async-start | bytes 163840 | tf_op jit(solution)/shard_map/reduce_scatter | solution.py:438
  1141.7 898.7 %reduce-scatter.28.cloned.1.call-start = ((), (), s32[]{:S(2)}) async-start(), calls=%async_computation.22 | async-start | bytes 163840 | tf_op jit(solution)/shard_map/reduce_scatter | solution.py:441
  1144.6 925.2 %all-reduce.27.cloned.1.call-start = ((), (), s32[]{:S(2)}) async-start(), calls=%async_computation.27 | async-start | bytes 8388608 | tf_op jit(solution)/shard_map/psum | solution.py:153
  1148.6 1136.8 %reduce-scatter.32.cloned.1.call-start = ((), (), s32[]{:S(2)}) async-start(), calls=%async_computation.24 | async-start | bytes 15728640 | tf_op jit(solution)/shard_map/reduce_scatter | solution.py:453
  1965.7 106.4 %copy-start.66 = (bf16[1024]{0:T(1024)(128)(2,1)S(1)}, bf16[1024]{0:T(1024)(128)(2,1)}, u32[]{:S(2)}) copy-start(bf16[1024]{0:T(1024)(128)(2,1)} %get-tuple-element.459) | copy-start | bytes 6148
  1965.7 130.2 %copy-start.59 = (f32[512]{0:T(512)S(1)}, f32[512]{0:T(512)}, u32[]{:S(2)}) copy-start(f32[512]{0:T(512)} %copy-done.58) | copy-start | bytes 6148
  1965.8 130.1 %copy-start.5 = (f32[512,1024]{1,0:T(8,128)S(1)}, f32[512,1024]{1,0:T(8,128)}, u32[]{:S(2)}) copy-start(f32[512,1024]{1,0:T(8,128)} %copy-done.3) | copy-start | bytes 6291460
  (41 other events, 272.3 us)
Sparse Core Ops, SparseCore 0:
  9.8 30.1 all-gather.8
  45.3 46.1 all-gather.6
  93.4 25.1 all-gather.10
  200.4 20.1 all-reduce.20
  222.2 438.1 all-gather.12
  793.5 21.2 all-reduce.22
  903.4 77.9 reduce-scatter.15
  984.9 28.4 reduce-scatter.29
  1016.8 27.9 reduce-scatter.17
  1047.5 25.1 reduce-scatter.21
  1075.4 25.0 reduce-scatter.25
  1104.0 851.1 all-reduce.24
  1958.1 22.2 reduce-scatter.33
  1982.5 18.1 reduce-scatter.19
  2002.8 17.6 reduce-scatter.23
  2022.6 17.6 reduce-scatter.27
  2043.3 26.4 all-reduce.26
  2072.0 213.3 reduce-scatter.31
where the time goes:
time: 2300 us
  waiting for transfers between devices  1480 us (64%)
  matrix products  315 us (14%)
  local copies, waits for them, and re-layouts  236 us (10%)
  other arithmetic  140 us (6%)
  blocking collectives  73.5 us (3%)
  loops' own time  31.9 us (1%)
    unnamed x20, waiting for transfers between devices  820 us
    all_gather x1, waiting for transfers between devices, sweep(): lax.all_gather(expert_weights, 'dp', axis=0, tiled=True)  360 us
    reduce_scatter x1, waiting for transfers between devices, body(): lax.psum_scatter(expert_part, 'ctx', scatter_dimension=2, tiled=True)  185 us
    dot_general x13, matrix products, key_block(): jnp.einsum('sqhgd,skhd->shgqk', q_group, key_rows, preferred_element_type...  63.5 us
  transfers between devices with their start and end apart: 18, of which 10 were waited for; matrix products, arithmetic and copies ran while one was open for 20% of the time, Pallas kernels for 0%

commit v1 on v0

--- a/solution.py
+++ b/solution.py
@@ -4,7 +4,6 @@
 from jax.sharding import PartitionSpec as P
 
 HEAD_DIM = 64
-EXPERTS = 32
 TOP = 8
 PIC = 256
 CAP = 144
@@ -48,32 +47,6 @@
     earlier = k_place[None, :] <= q_place[:, None]
     picture = (q_pic[:, None] >= 0) & (q_pic[:, None] == k_pic[None, :])
     return same_doc & (earlier | picture)
-
-
-def dispatch(chosen):
-    onehot = (chosen[:, None] == jnp.arange(EXPERTS, dtype=jnp.int32)[None, :]).astype(jnp.int32)
-    before = jnp.cumsum(onehot, axis=0) - onehot
-    position = jnp.sum(before * onehot, axis=-1)
-    return jnp.where(position < CAP, chosen * CAP + position, EXPERTS * CAP)
-
-
-def slot_table(slot_ids, tok_count):
-    owners = jnp.arange(slot_ids.shape[0], dtype=jnp.int32) // TOP
-    slot_owner = jnp.full((EXPERTS * CAP + 1,), tok_count, jnp.int32).at[slot_ids].set(owners)
-    return slot_owner[: EXPERTS * CAP]
-
-
-def expert_forward(weight_rows, slot_rows):
-    gate_pre = jnp.einsum(
-        "ecd,edf->ecf", slot_rows, weight_rows[:, 0], preferred_element_type=jnp.float32
-    )
-    up_pre = jnp.einsum(
-        "ecd,edf->ecf", slot_rows, weight_rows[:, 1], preferred_element_type=jnp.float32
-    )
-    activation = (jax.nn.silu(gate_pre) * up_pre).astype(jnp.bfloat16)
-    return jnp.einsum(
-        "ecf,edf->ecd", activation, weight_rows[:, 2], preferred_element_type=jnp.float32
-    )
 
 
 def gated_product(gate_pre, up_pre):
@@ -234,73 +207,62 @@
     )
     hidden = x_flat + attention_output
     normed_two = rms_norm(hidden, gain_second).astype(jnp.bfloat16)
-    chosen = routes.reshape(tok_rows * TOP)
-    pair_gates = gate_values.reshape(tok_rows * TOP)
-    slot_ids = dispatch(chosen)
-    slot_owner = slot_table(slot_ids, tok_rows)
-    slot_gate = (
-        jnp.zeros((EXPERTS * CAP + 1,), jnp.float32).at[slot_ids].set(pair_gates)[: EXPERTS * CAP]
-    )
-    padded_two = jnp.concatenate([normed_two, jnp.zeros((1, model_width), jnp.bfloat16)], axis=0)
-    slot_rows = padded_two[slot_owner].reshape(EXPERTS, CAP, model_width)
-
-    def sweep(piece_fn):
-        return piece_fn(lax.all_gather(expert_weights, "dp", axis=0, tiled=True), jnp.int32(0))
-
-    def forward_piece(weight_rows, first_row):
-        return expert_forward(weight_rows, slot_rows)
-
-    slot_out = sweep(forward_piece)
-    flat_out = jnp.concatenate(
-        [slot_out.reshape(EXPERTS * CAP, model_width), jnp.zeros((1, model_width), jnp.float32)],
-        axis=0,
-    )
-    moe_part = jnp.sum(
-        flat_out[slot_ids].reshape(tok_rows, TOP, model_width)
-        * pair_gates.reshape(tok_rows, TOP)[:, :, None],
-        axis=1,
-    )
-    layer_out = hidden + sum_heads(moe_part)
+    own = expert_weights.shape[0]
+    chosen_all = lax.all_gather(routes.reshape(tok_rows, TOP), "dp", axis=0)
+    gates_all = lax.all_gather(gate_values.reshape(tok_rows, TOP), "dp", axis=0)
+    grad_all = lax.all_gather(cotangent.reshape(tok_rows, model_width), "dp", axis=0)
+    rows_all = lax.all_gather(normed_two, "dp", axis=0)
+    groups = rows_all.shape[0]
+    first_own = lax.axis_index("dp") * own
+    named = chosen_all[..., None] == first_own + jnp.arange(own, dtype=jnp.int32)
+    names = jnp.any(named, axis=2)
+    gate_of = jnp.sum(jnp.where(named, gates_all[..., None], 0.0), axis=2)
+    earlier = jnp.tril(jnp.ones((tok_rows, tok_rows), jnp.bfloat16), -1)
+    place = jnp.einsum(
+        "rq,gqe->gre", earlier, names.astype(jnp.bfloat16), preferred_element_type=jnp.float32
+    ).astype(jnp.int32)
+    place = jnp.where(names & (place < CAP), place, -1)
+    picks = place.transpose(0, 2, 1)[:, :, None, :] == jnp.arange(CAP, dtype=jnp.int32)[:, None]
+    slot_gate = jnp.sum(jnp.where(picks, gate_of.transpose(0, 2, 1)[:, :, None, :], 0.0), axis=-1)
+    picks = picks.astype(jnp.bfloat16)
+    slot_rows = (
+        jnp.einsum("gesr,grd->egsd", picks, rows_all, preferred_element_type=jnp.float32)
+        .astype(jnp.bfloat16)
+        .reshape(own, groups * CAP, model_width)
+    )
+    gate_col = slot_gate.transpose(1, 0, 2).reshape(own, groups * CAP, 1)
+    slot_grads = (
+        jnp.einsum("gesr,grd->egsd", picks, grad_all, preferred_element_type=jnp.float32).reshape(
+            own, groups * CAP, model_width
+        )
+        * gate_col
+    ).astype(jnp.bfloat16)
     out_grad = cotangent.reshape(tok_rows, model_width).astype(jnp.float32)
-    padded_grad = jnp.concatenate([out_grad, jnp.zeros((1, model_width), jnp.float32)], axis=0)
-    slot_grads = (
-        (padded_grad[slot_owner] * slot_gate[:, None])
-        .astype(jnp.bfloat16)
-        .reshape(EXPERTS, CAP, model_width)
-    )
-    ff_width = expert_weights.shape[3]
-
-    def backward_piece(weight_rows, first_row):
-        row_count = weight_rows.shape[0]
-        pieces = expert_backward(weight_rows, slot_rows, slot_grads)
-        return jnp.concatenate(
-            [
-                pieces[0],
-                pieces[1].astype(jnp.float32),
-                pieces[2].astype(jnp.float32),
-                pieces[3].astype(jnp.float32),
-            ],
-            axis=-1,
-        )
-
-    joined = sweep(backward_piece)
-    slot_back = joined[..., :model_width]
-    gate_low = joined[..., model_width : model_width + ff_width].astype(jnp.bfloat16)
-    up_low = joined[..., model_width + ff_width : model_width + 2 * ff_width].astype(jnp.bfloat16)
-    act_low = joined[..., model_width + 2 * ff_width :].astype(jnp.bfloat16)
-    expert_part = lax.psum_scatter(
-        expert_weight_grads(slot_rows, slot_grads, gate_low, up_low, act_low).astype(jnp.bfloat16),
-        "dp",
-        scatter_dimension=0,
-        tiled=True,
-    )
-    flat_back = jnp.concatenate(
-        [slot_back.reshape(EXPERTS * CAP, model_width), jnp.zeros((1, model_width), jnp.float32)],
-        axis=0,
-    )
-    normed_two_grad = sum_heads(
-        jnp.sum(flat_back[slot_ids].reshape(tok_rows, TOP, model_width), axis=1)
-    )
+    slot_back, gate_low, up_low, act_low = expert_backward(expert_weights, slot_rows, slot_grads)
+    slot_out = jnp.einsum(
+        "ecf,edf->ecd", act_low, expert_weights[:, 2], preferred_element_type=jnp.float32
+    )
+
+    def combine(slots):
+        part = jnp.einsum(
+            "gesr,egsd->grd",
+            picks,
+            slots.astype(jnp.bfloat16).reshape(own, groups, CAP, model_width),
+            preferred_element_type=jnp.float32,
+        )
+        mine = lax.psum_scatter(
+            part.astype(jnp.bfloat16).reshape(groups * tok_rows, model_width),
+            "dp",
+            scatter_dimension=0,
+            tiled=True,
+        )
+        return sum_heads(mine.astype(jnp.float32))
+
+    normed_two_grad = combine(slot_back)
+    expert_part = expert_weight_grads(slot_rows, slot_grads, gate_low, up_low, act_low).astype(
+        jnp.bfloat16
+    )
+    layer_out = hidden + combine(slot_out * gate_col)
     hidden_pull = jax.vjp(rms_norm, hidden, gain_second)[1]
     hidden_norm_grad, gain_second_grad = hidden_pull(normed_two_grad)
     hidden_grad = out_grad + hidden_norm_grad

time: 2300 us -> 1140 us (0.50)
  waiting for transfers between devices: 1480 us -> 508 us
  local copies, waits for them, and re-layouts: 236 us -> 83.9 us
  other arithmetic: 140 us -> 90.7 us
  blocking collectives: 73.5 us -> 106 us
    unnamed x20, waiting for transfers between devices: 820 us -> 2.18 us
    all_gather x1 -> x2, waiting for transfers between devices: 360 us -> 65.8 us  [the longest x1 34.2 us: body(): rows_all = lax.all_gather(normed_two, 'dp', axis=0)]
    gather x4 -> x0, local copies, waits for them, and re-layouts: 87.5 us -> none  [the longest x1 28.8 us: body(): flat_out[slot_ids].reshape(tok_rows, TOP, model_width)]
    reduce_scatter x0 -> x2, waiting for transfers between devices: none -> 68.8 us  [combine(): lax.psum_scatter(part.astype(jnp.bfloat16).reshape(groups * tok_rows, mod...]
    scatter x2 -> x0, local copies, waits for them, and re-layouts: 31.1 us -> none  [the longest x1 15.5 us: slot_table(): jnp.full((EXPERTS * CAP + 1,), tok_count, jnp.int32).at[slot_ids]]
    concatenate x4 -> x0, local copies, waits for them, and re-layouts: 30.6 us -> none  [the longest x1 15.2 us: body(): jnp.concatenate([slot_out.reshape(EXPERTS * CAP, model_width), jnp.zeros(...]
    reduce_scatter x1, waiting for transfers between devices: 0.01 us -> 29.5 us  [body(): lax.psum_scatter(query_w_grad.astype(jnp.bfloat16), 'dp', scatter_dimensi...]
    dot_general x3 -> x8, matrix products: 39.5 us -> 67.4 us  [the longest x2 21.7 us: combine(): jnp.einsum('gesr,egsd->grd', picks, slots.astype(jnp.bfloat16).reshape(ow...]
  transfers between devices with their start and end apart: 18 -> 19, of which waited for: 10 -> 15; matrix products, arithmetic and copies ran while one was open for 20% -> 27% of each run, Pallas kernels for 0% -> 0%
where the time goes in v1:
time: 1140 us
  waiting for transfers between devices  508 us (45%)
  matrix products  302 us (26%)
  blocking collectives  106 us (9%)
  other arithmetic  90.7 us (8%)
  local copies, waits for them, and re-layouts  83.9 us (7%)
  loops' own time  30.9 us (3%)
  between operations  16.5 us (1%)
    reduce_scatter x1, waiting for transfers between devices, body(): lax.psum_scatter(expert_part, 'ctx', scatter_dimension=2, tiled=True)  186 us
    reduce_scatter x2, waiting for transfers between devices, combine(): lax.psum_scatter(part.astype(jnp.bfloat16).reshape(groups * tok_rows, mod...  68.8 us
    dot_general x13, matrix products, key_block(): jnp.einsum('sqhgd,skhd->shgqk', q_group, key_rows, preferred_element_type...  63.5 us
    all_gather x1, waiting for transfers between devices, body(): rows_all = lax.all_gather(normed_two, 'dp', axis=0)  34.2 us
    dot_general x4, matrix products, query_step(): jnp.einsum('shgqk,skhd->sqhgd', score_low, key_rows, preferred_element_ty...  32.7 us
    psum x2, waiting for transfers between devices, sum_heads(): return lax.psum(partial_sum, 'tp')  31.8 us
    all_gather x1, waiting for transfers between devices, body(): lax.all_gather(cotangent.reshape(tok_rows, model_width), 'dp', axis=0)  31.6 us
    reduce_scatter x1, waiting for transfers between devices, body(): lax.psum_scatter(query_w_grad.astype(jnp.bfloat16), 'dp', scatter_dimensi...  29.5 us
  transfers between devices with their start and end apart: 19, of which 15 were waited for; matrix products, arithmetic and copies ran while one was open for 27% of the time, Pallas kernels for 0%

profile of v1, /device:TPU:0, one launch (start us, length us, event | category | flops | bytes accessed | tf_op | source)
XLA Modules:
  0.0 1139.3 jit_solution(12652700416432588040)
XLA Ops:
  8.0 12.0 %all_gather.40 = bf16[1024,256]{1,0:T(8,128)(2,1)S(1)} all-gather(bf16[256,256]{1,0:T(8,128)(2,1)} %param.23), channel_id=1, replica_groups=mesh['dp'=4,'ctx'=4,'tp'=2] {'dp'}, dimensions={0}, use_global_device_ids=true | all-gather | bytes 655360 | tf_op jit(solution)/shard_map/all_gather | solution.py:109
  20.0 11.2 all_gather.41
  31.9 7.1 all-gather.1
  46.0 12.5 %all_gather.43 = bf16[1,2048]{1,0:T(2,128)(2,1)S(1)} all-gather(bf16[1,512]{1,0:T(2,128)(2,1)S(1)} %convert_element_type.238), channel_id=1, replica_groups=mesh['dp'=4,'ctx'=4,'tp'=2] {'ctx'}, dimensions={1}, use_global_device_ids=true | all-gather | bytes 5120 | tf_op jit(solution)/shard_map/all_gather | solution.py:153
  64.3 26.4 %all-gather.9.cloned.1.call-done = bf16[1,2048,512]{1,2,0:T(8,128)(2,1)} async-done(((bf16[1,512,512]{1,2,0:T(8,128)(2,1)}), bf16[1,2048,512]{1,2,0:T(8,128)(2,1)}) %all-gather.9.cloned.1.call-update) | async-done | bytes 2097168 | tf_op jit(solution)/shard_map/all_gather | solution.py:152
  90.8 64.6 %while.46 = (s32[]{:T(128)}, f32[1,4,2,512]{3,2,1,0:T(2,128)S(1)}, f32[1,4,2,512]{3,2,1,0:T(2,128)S(1)}, s32[1,512]{1,0:T(1,128)S(1)}, s32[4]{0:T(128)}, /*index...) while((s32[]{:T(128)}, f32[1,4,2,512]{3,2,1,0:T(2,128)S(1)}, ...), condition=%wide.region_5.6_spmd.clone, body=%wide.region_2.5_spmd.clone.sunk | while | flops 284710400 | bytes 19115212 | solution.py:185
  155.4 37.9 %while.47 = (s32[]{:T(128)}, f32[1,512,4,2,64]{1,4,3,2,0:T(8,128)S(1)}, s32[4]{0:T(128)}, bf16[1,2048,512]{1,2,0:T(8,128)(2,1)}, s32[1,512]{1,0:T(1,128)S(1)}, /...) while((s32[]{:T(128)}, ...), condition=%wide.region_7.8_spmd.clone, body=%wide.region_6.7_spmd.clone.sunk | while | flops 547358208 | bytes 4762853 | solution.py:203
  197.7 8.0 all-gather.2
  205.7 11.5 %all-reduce.15.cloned.1.call-done = f32[512,1024]{1,0:T(8,128)} async-done(((f32[512,1024]{1,0:T(8,128)}), f32[512,1024]{1,0:T(8,128)}) %all-reduce.15.cloned.1.call-update) | async-done | bytes 2097168 | tf_op jit(solution)/shard_map/psum | solution.py:126
  221.8 8.5 all_gather.46
  230.3 9.4 all_gather.50
  241.7 31.6 %all-gather.15.cloned.1.call-done = bf16[4,512,1024]{2,1,0:T(8,128)(2,1)} async-done(((bf16[1,512,1024]{2,1,0:T(8,128)(2,1)}), bf16[4,512,1024]{2,1,0:T(8,128)(2,1)}) %all-gather.15.cloned.1.call-update) | async-done | bytes 4194320 | tf_op jit(solution)/shard_map/all_gather | solution.py:213
  293.9 34.2 %all-gather.17.cloned.1.call-done = bf16[2048,1024]{1,0:T(8,128)(2,1)} async-done(((bf16[512,1024]{1,0:T(8,128)(2,1)}), bf16[2048,1024]{1,0:T(8,128)(2,1)}) %all-gather.17.cloned.1.call-update) | async-done | bytes 4194320 | tf_op jit(solution)/shard_map/all_gather | solution.py:214
  328.1 9.6 convert_bitcast_fusion
  337.7 9.1 copy.94
  346.8 9.8 fusion.95
  356.6 11.6 %multiply_convert_fusion.2 = (bf16[8,576,256]{2,1,0:T(8,128)(2,1)}, bf16[8,576,256]{2,1,0:T(8,128)(2,1)S(1)}, bf16[8,576,256]{2,1,0:T(8,128)(2,1)S(1)}) fusion(f32[8,576,256]{2,1,0:T(8,128)} %fusion.95, f32[8,576,256]{2,1,0:T(8,128)} %fusion.87, bf16[8,576,1024]{2,1,0:T(8,128)(2,1)} %bitcast.590, bf16[8,3,1024,256]{3,2,1,0:T(8,128)(2,1)} %param.28), kind=kOutput, calls=%fused_computation.119 | convolution fusion | flops 2434793472 | bytes 30146560 | tf_op jit(solution)/shard_map/ecd,edf->ecf/dot_general | solution.py:60
  368.3 7.9 fusion.93
  376.2 11.7 %add_convert_fusion = bf16[8,576,1024]{2,1,0:T(8,128)(2,1)} fusion(f32[8,576,1024]{2,1,0:T(8,128)} %fusion.93, bf16[8,576,256]{2,1,0:T(8,128)(2,1)S(1)} %get-tuple-element.602, bf16[8,3,1024,256]{3,2,1,0:T(8,128)(2,1)} %param.28), kind=kOutput, calls=%fused_computation.94 | convolution fusion | flops 2425356288 | bytes 34865152 | tf_op jit(solution)/shard_map/ecf,edf->ecd/dot_general | solution.py:74
  387.9 10.9 bitcast_convert_fusion
  400.4 7.5 multiply_convert_fusion
  407.9 10.9 bitcast_convert_fusion.1
  424.4 13.9 %fusion.144 = f32[4,2048,512,2]{2,1,3,0:T(8,128)} fusion(bf16[2048,4,64,1]{0,2,3,1:T(8,128)(2,1)S(1)} %bitcast.605, bf16[512,4,2,32]{0,3,2,1:T(8,128)(2,1)S(1)} %bitcast.621, bf16[512,4,2,32]{0,3,2,1:T(8,128)(2,1)S(1)} %bitcast.617), kind=kOutput, calls=%fused_computation.214 | convolution fusion | flops 1074790400 | bytes 35127296 | tf_op jit(solution)/shard_map/sqhgd,skhd->shgqk/dot_general | solution.py:164
  438.3 13.2 %reduce-scatter.17.cloned.1.call-done = bf16[512,1024]{1,0:T(8,128)(2,1)} async-done(((bf16[2048,1024]{1,0:T(8,128)(2,1)}), bf16[512,1024]{1,0:T(8,128)(2,1)}) %reduce-scatter.17.cloned.1.call-update) | async-done | bytes 1048592 | tf_op jit(solution)/shard_map/reduce_scatter | solution.py:253
  451.5 55.6 %reduce-scatter.15.cloned.1.call-done = bf16[512,1024]{1,0:T(8,128)(2,1)} async-done(((bf16[2048,1024]{1,0:T(8,128)(2,1)}), bf16[512,1024]{1,0:T(8,128)(2,1)}) %reduce-scatter.15.cloned.1.call-update) | async-done | bytes 1048592 | tf_op jit(solution)/shard_map/reduce_scatter | solution.py:253
  507.1 15.0 %all-reduce.18 = (f32[512,1024]{1,0:T(8,128)}, f32[512,1024]{1,0:T(8,128)}) all-reduce(bf16[512,1024]{1,0:T(8,128)(2,1)} %reduce-scatter.17.cloned.1.call-done, bf16[512,1024]{1,0:T(8,128)(2,1)} %reduce-scatter.15.cloned.1.call-done), channel_id=1, replica_groups=mesh['dp'=4,'ctx'=4,'tp'=2] {'tp'}, use_global_device_ids=true, to_apply=%region_16.17 | all-reduce | flops 1048576 | bytes 6291456 | tf_op jit(solution)/shard_map/psum | solution.py:126
  531.5 39.1 %while.48 = (s32[]{:T(128)}, f32[1,4,2,512]{3,2,1,0:T(2,128)S(1)}, s32[1,512]{1,0:T(1,128)S(1)}, s32[4]{0:T(128)}, s32[1,2048]{1,0:T(1,128)}, /*index=5*/s32[1,5...) while((s32[]{:T(128)}, f32[1,4,2,512]{3,2,1,0:T(2,128)S(1)}, ...), condition=%wide.region_20.21_spmd.clone, body=%wide.region_18.20_spmd.clone.sunk | while | flops 548935168 | bytes 20032748 | solution.py:287
  570.7 16.4 %fusion.69 = f32[4,64,2048,1]{2,1,3,0:T(8,128)} fusion(bf16[512,4,2,64]{0,3,2,1:T(8,128)(2,1)S(1)} %bitcast.585, f32[4,2048,512,2]{2,1,3,0:T(8,128)} %fusion.144, f32[4,2,512]{2,1,0:T(2,128)S(1)} %bitcast.674, pred[512,2048]{0,1:T(8,128)(4,1)} %fusion.99), kind=kOutput, calls=%fused_computation.99 | convolution fusion | flops 1107296256 | bytes 37240832 | tf_op jit(solution)/shard_map/shgqk,sqhgd->skhd/dot_general | solution.py:314
  587.1 20.5 %fusion.67 = f32[4,64,2048,1]{2,1,3,0:T(8,128)} fusion(f32[4,2048,512,2]{2,1,3,0:T(8,128)} %fusion.144, bf16[2048,4,64,1]{0,2,3,1:T(8,128)(2,1)} %bitcast.635, bf16[512,4,2,64]{0,3,2,1:T(8,128)(2,1)S(1)} %bitcast.586, f32[4,2,512]{2,1,0:T(2,128)S(1)} %bitcast.647, f32[4,2,512]{2,1,0:T(2,128)S(1)} %bitcast.675, pred[512,2048]{0,1:T(8,128)(4,1)} %fusion.99, ...), kind=kOutput, calls=%fused_computation.97 | convolution fusion | flops 2207252480 | bytes 38830080 | tf_op jit(solution)/shard_map/shgqk,sqhgd->skhd/dot_general | solution.py:320
  616.0 76.6 %while.49 = (s32[]{:T(128)}, f32[1,512,4,2,64]{1,4,3,2,0:T(8,128)}, s32[4]{0:T(128)}, bf16[1,2048,512]{1,2,0:T(8,128)(2,1)S(1)}, s32[1,512]{1,0:T(1,128)S(1)}, /...) while((s32[]{:T(128)}, f32[1,512,4,2,64]{1,4,3,2,0:T(8,128)}, ...), condition=%wide.region_22.23_spmd.clone, body=%wide.region_21.22_spmd.clone.sunk | while | flops 822085120 | bytes 22342900 | solution.py:310
  627.0 8.0 fusion.256
  645.9 8.3 fusion.256
  665.1 8.2 fusion.256
  684.3 8.2 fusion.256
  703.0 17.5 %reduce-scatter.33.cloned.1.call-done = bf16[512,256]{1,0:T(8,128)(2,1)} async-done(((bf16[512,1024]{1,0:T(8,128)(2,1)}), bf16[512,256]{1,0:T(8,128)(2,1)}) %reduce-scatter.33.cloned.1.call-update) | async-done | bytes 262160 | tf_op jit(solution)/shard_map/reduce_scatter | solution.py:386
  722.4 29.5 %reduce-scatter.21.cloned.1.call-done = bf16[256,512]{1,0:T(8,128)(2,1)} async-done(((bf16[1024,512]{1,0:T(8,128)(2,1)}), bf16[256,512]{1,0:T(8,128)(2,1)}) %reduce-scatter.21.cloned.1.call-update) | async-done | bytes 262160 | tf_op jit(solution)/shard_map/reduce_scatter | solution.py:377
  752.0 10.5 convert_bitcast_fusion.1
  764.6 15.1 %reduce-scatter.25.cloned.1.call-done = bf16[256,256]{1,0:T(8,128)(2,1)} async-done(((bf16[1024,256]{1,0:T(8,128)(2,1)}), bf16[256,256]{1,0:T(8,128)(2,1)}) %reduce-scatter.25.cloned.1.call-update) | async-done | bytes 131088 | tf_op jit(solution)/shard_map/reduce_scatter | solution.py:380
  782.7 25.0 %reduce-scatter.29.cloned.1.call-done = bf16[256,256]{1,0:T(8,128)(2,1)} async-done(((bf16[1024,256]{1,0:T(8,128)(2,1)}), bf16[256,256]{1,0:T(8,128)(2,1)}) %reduce-scatter.29.cloned.1.call-update) | async-done | bytes 131088 | tf_op jit(solution)/shard_map/reduce_scatter | solution.py:383
  811.7 10.2 convert_bitcast_fusion.2
  821.9 10.2 convert_bitcast_fusion.3
  832.1 10.5 pad_maximum_fusion
  851.7 18.3 %reduce-scatter.27.cloned.1.call-done = bf16[64,256]{1,0:T(8,128)(2,1)} async-done(((bf16[256,256]{1,0:T(8,128)(2,1)}), bf16[64,256]{1,0:T(8,128)(2,1)}) %reduce-scatter.27.cloned.1.call-update) | async-done | bytes 32784 | tf_op jit(solution)/shard_map/reduce_scatter | solution.py:400
  871.4 18.4 %reduce-scatter.31.cloned.1.call-done = bf16[64,256]{1,0:T(8,128)(2,1)} async-done(((bf16[256,256]{1,0:T(8,128)(2,1)}), bf16[64,256]{1,0:T(8,128)(2,1)}) %reduce-scatter.31.cloned.1.call-update) | async-done | bytes 32784 | tf_op jit(solution)/shard_map/reduce_scatter | solution.py:403
  891.1 20.3 %all-reduce.17.cloned.1.call-done = f32[512,1024]{1,0:T(8,128)} async-done(((f32[512,1024]{1,0:T(8,128)}), f32[512,1024]{1,0:T(8,128)}) %all-reduce.17.cloned.1.call-update) | async-done | bytes 2097168 | tf_op jit(solution)/shard_map/psum | solution.py:126
  913.8 10.1 all-reduce.10
  924.1 12.3 %all-reduce.9 = (bf16[256]{0:T(256)(128)(2,1)S(1)}, bf16[256]{0:T(256)(128)(2,1)S(1)}) all-reduce(bf16[256]{0:T(256)(128)(2,1)S(1)} %dynamic-slice.2, bf16[256]{0:T(256)(128)(2,1)S(1)} %dynamic-slice.6), channel_id=15, replica_groups=mesh['dp'=4,'ctx'=4,'tp'=2] {'ctx'}, use_global_device_ids=true, to_apply=%region_36.37.clone | all-reduce | flops 512 | bytes 2048
  940.7 186.5 %reduce-scatter.35.cloned.1.call-done = bf16[8,3,256,256]{3,2,0,1:T(8,128)(2,1)} async-done(((bf16[8,3,1024,256]{3,2,0,1:T(8,128)(2,1)}), bf16[8,3,256,256]{3,2,0,1:T(8,128)(2,1)}) %reduce-scatter.35.cloned.1.call-update) | async-done | bytes 3145744 | tf_op jit(solution)/shard_map/reduce_scatter | solution.py:415
  (391 shorter events, 268.9 us)
Async XLA Ops:
  7.2 52.6 %all-gather.11.cloned.1.call-start = ((), (), s32[]{:S(2)}) async-start(), calls=%async_computation.13 | async-start | bytes 1310720 | tf_op jit(solution)/shard_map/all_gather | solution.py:108
  7.9 82.8 %all-gather.9.cloned.1.call-start = ((), (), s32[]{:S(2)}) async-start(), calls=%async_computation.12 | async-start | bytes 2621440 | tf_op jit(solution)/shard_map/all_gather | solution.py:152
  8.0 35.1 %copy-start.7 = (bf16[1,512,1024]{2,1,0:T(8,128)(2,1)S(1)}, bf16[1,512,1024]{2,1,0:T(8,128)(2,1)}, u32[]{:S(2)}) copy-start(bf16[1,512,1024]{2,1,0:T(8,128)(2,1)} %param.21) | copy-start | bytes 3145732
  20.0 23.7 %copy-start.13 = (bf16[1024,256]{1,0:T(8,128)(2,1)}, bf16[1024,256]{1,0:T(8,128)(2,1)S(1)}, u32[]{:S(2)}) copy-start(bf16[1024,256]{1,0:T(8,128)(2,1)S(1)} %all_gather.40) | copy-start | bytes 1572868
  31.2 12.5 %copy-start.23 = (bf16[1024,256]{1,0:T(8,128)(2,1)}, bf16[1024,256]{1,0:T(8,128)(2,1)S(1)}, u32[]{:S(2)}) copy-start(bf16[1024,256]{1,0:T(8,128)(2,1)S(1)} %all_gather.41) | copy-start | bytes 1572868
  42.9 21.2 %copy-start.25 = (f32[512,32]{0,1:T(8,128)}, f32[512,32]{0,1:T(8,128)S(1)}, u32[]{:S(2)}) copy-start(f32[512,32]{0,1:T(8,128)S(1)} %get-tuple-element.615) | copy-start | bytes 196612
  42.9 21.2 %copy-start.27 = (f32[512,32]{0,1:T(8,128)}, f32[512,32]{0,1:T(8,128)S(1)}, u32[]{:S(2)}) copy-start(f32[512,32]{0,1:T(8,128)S(1)} %get-tuple-element.616) | copy-start | bytes 196612
  44.6 148.8 %all-gather.13.cloned.1.call-start = ((), (), s32[]{:S(2)}) async-start(), calls=%async_computation.14 | async-start | bytes 1310720 | tf_op jit(solution)/shard_map/all_gather | solution.py:111
  45.3 171.9 %all-reduce.15.cloned.1.call-start = ((), (), s32[]{:S(2)}) async-start(), calls=%async_computation.15 | async-start | bytes 4194304 | tf_op jit(solution)/shard_map/psum | solution.py:126
  64.2 26.5 %copy-start.17 = (bf16[1,512,8,32]{1,3,2,0:T(8,128)(2,1)}, bf16[1,512,8,32]{1,3,2,0:T(8,128)(2,1)S(1)}, u32[]{:S(2)}) copy-start(bf16[1,512,8,32]{1,3,2,0:T(8,128)(2,1)S(1)} %get-tuple-element.609) | copy-start | bytes 786436
  64.3 26.5 %copy-start.20 = (bf16[1,512,8,32]{1,3,2,0:T(8,128)(2,1)}, bf16[1,512,8,32]{1,3,2,0:T(8,128)(2,1)S(1)}, u32[]{:S(2)}) copy-start(bf16[1,512,8,32]{1,3,2,0:T(8,128)(2,1)S(1)} %get-tuple-element.610) | copy-start | bytes 786436
  193.4 25.8 %copy-start.12 = (bf16[1,512,4,2,64]{1,4,3,2,0:T(8,128)(2,1)}, bf16[1,512,4,2,64]{1,4,3,2,0:T(8,128)(2,1)S(1)}, u32[]{:S(2)}) copy-start(bf16[1,512,4,2,64]{1,4,3,2,0:T(8,128)(2,1)S(1)} %convert_element_type.240) | copy-start | bytes 1572868
  196.9 76.3 %all-gather.15.cloned.1.call-start = ((), (), s32[]{:S(2)}) async-start(), calls=%async_computation.17 | async-start | bytes 5242880 | tf_op jit(solution)/shard_map/all_gather | solution.py:213
  197.6 130.5 %all-gather.17.cloned.1.call-start = ((), (), s32[]{:S(2)}) async-start(), calls=%async_computation.29 | async-start | bytes 5242880 | tf_op jit(solution)/shard_map/all_gather | solution.py:214
  205.7 16.0 %copy-start.37 = (f32[4,1,256]{2,1,0:T(1,128)}, f32[4,1,256]{2,1,0:T(1,128)S(1)}, u32[]{:S(2)}) copy-start(f32[4,1,256]{2,1,0:T(1,128)S(1)} %convert_element_type.288) | copy-start | bytes 12292
  205.7 16.1 %copy-start.49 = (s32[1,512,8]{1,2,0:T(8,128)S(1)}, s32[1,512,8]{1,2,0:T(8,128)}, u32[]{:S(2)}) copy-start(s32[1,512,8]{1,2,0:T(8,128)} %param.29) | copy-start | bytes 49156
  205.7 24.6 %copy-start.50 = (f32[1,512,8]{1,2,0:T(8,128)S(1)}, f32[1,512,8]{1,2,0:T(8,128)}, u32[]{:S(2)}) copy-start(f32[1,512,8]{1,2,0:T(8,128)} %param.30) | copy-start | bytes 49156
  219.2 22.4 %copy-start.45 = (f32[512]{0:T(512)}, f32[512]{0:T(512)S(1)}, u32[]{:S(2)}) copy-start(f32[512]{0:T(512)S(1)} %get-tuple-element.574) | copy-start | bytes 6148
  221.7 229.8 %reduce-scatter.17.cloned.1.call-start = ((), (), s32[]{:S(2)}) async-start(), calls=%async_computation.18 | async-start | bytes 5242880 | tf_op jit(solution)/shard_map/reduce_scatter | solution.py:253
  346.8 21.4 %slice-start = ((s8[12582912]{0:T(1024)(128)(4,1)}), s8[4194304]{0:T(1024)(128)(4,1)S(1)}, s32[]{:S(2)}) async-start(s8[12582912]{0:T(1024)(128)(4,1)} %bitcast.587), calls=%async_computation.31 | async-start | bytes 8388608
  356.6 11.6 %slice-start.1 = ((s8[12582912]{0:T(1024)(128)(4,1)}), s8[4194304]{0:T(1024)(128)(4,1)S(1)}, s32[]{:S(2)}) async-start(s8[12582912]{0:T(1024)(128)(4,1)} %bitcast.587), calls=%async_computation.32 | async-start | bytes 8388608
  356.6 11.6 %slice-start.2 = ((s8[12582912]{0:T(1024)(128)(4,1)}), s8[4194304]{0:T(1024)(128)(4,1)S(1)}, s32[]{:S(2)}) async-start(s8[12582912]{0:T(1024)(128)(4,1)} %bitcast.587), calls=%async_computation.33 | async-start | bytes 8388608
  368.2 7.9 copy-start.11
  368.2 7.9 copy-start.22
  398.7 108.4 %reduce-scatter.15.cloned.1.call-start = ((), (), s32[]{:S(2)}) async-start(), calls=%async_computation.16 | async-start | bytes 5242880 | tf_op jit(solution)/shard_map/reduce_scatter | solution.py:253
  418.8 279.2 %reduce-scatter.19.cloned.1.call-start = ((), (), s32[]{:S(2)}) async-start(), calls=%async_computation.19 | async-start | bytes 5242880 | tf_op jit(solution)/shard_map/reduce_scatter | solution.py:330
  424.4 97.7 %copy-start.38 = (f32[4,1,256]{2,1,0:T(1,128)S(1)}, f32[4,1,256]{2,1,0:T(1,128)}, u32[]{:S(2)}) copy-start(f32[4,1,256]{2,1,0:T(1,128)} %copy-done.37) | copy-start | bytes 12292
  424.4 97.7 %copy-start.42 = (f32[512]{0:T(512)S(1)}, f32[512]{0:T(512)}, u32[]{:S(2)}) copy-start(f32[512]{0:T(512)} %copy-done.41) | copy-start | bytes 6148
  438.3 87.4 %copy-start.46 = (f32[512]{0:T(512)S(1)}, f32[512]{0:T(512)}, u32[]{:S(2)}) copy-start(f32[512]{0:T(512)} %copy-done.45) | copy-start | bytes 6148
  525.7 5.8 copy-start.1
  570.6 16.4 %copy-start.36 = (f32[1,4,2,512]{3,2,1,0:T(2,128)}, f32[1,4,2,512]{3,2,1,0:T(2,128)S(1)}, u32[]{:S(2)}) copy-start(f32[1,4,2,512]{3,2,1,0:T(2,128)S(1)} %get-tuple-element.1099) | copy-start | bytes 49156
  570.7 16.4 %copy-start.19 = (bf16[1,512,8,32]{1,3,2,0:T(8,128)(2,1)S(1)}, bf16[1,512,8,32]{1,3,2,0:T(8,128)(2,1)}, u32[]{:S(2)}) copy-start(bf16[1,512,8,32]{1,3,2,0:T(8,128)(2,1)} %copy-done.17) | copy-start | bytes 786436
  612.3 108.2 %reduce-scatter.33.cloned.1.call-start = ((), (), s32[]{:S(2)}) async-start(), calls=%async_computation.27 | async-start | bytes 1310720 | tf_op jit(solution)/shard_map/reduce_scatter | solution.py:386
  615.9 136.0 %reduce-scatter.21.cloned.1.call-start = ((), (), s32[]{:S(2)}) async-start(), calls=%async_computation.21 | async-start | bytes 1310720 | tf_op jit(solution)/shard_map/reduce_scatter | solution.py:377
  615.9 76.6 %copy-start.26 = (f32[512,32]{0,1:T(8,128)S(1)}, f32[512,32]{0,1:T(8,128)}, u32[]{:S(2)}) copy-start(f32[512,32]{0,1:T(8,128)} %copy-done.25) | copy-start | bytes 196612
  616.0 76.6 %copy-start.28 = (f32[512,32]{0,1:T(8,128)S(1)}, f32[512,32]{0,1:T(8,128)}, u32[]{:S(2)}) copy-start(f32[512,32]{0,1:T(8,128)} %copy-done.27) | copy-start | bytes 196612
  698.0 81.7 %reduce-scatter.25.cloned.1.call-start = ((), (), s32[]{:S(2)}) async-start(), calls=%async_computation.23 | async-start | bytes 655360 | tf_op jit(solution)/shard_map/reduce_scatter | solution.py:380
  699.4 52.6 %copy-start.30 = (bf16[1,512,4,64]{1,3,2,0:T(8,128)(2,1)}, bf16[1,512,4,64]{1,3,2,0:T(8,128)(2,1)S(1)}, u32[]{:S(2)}) copy-start(bf16[1,512,4,64]{1,3,2,0:T(8,128)(2,1)S(1)} %add_convert_fusion.3) | copy-start | bytes 786436
  700.9 106.7 %reduce-scatter.29.cloned.1.call-start = ((), (), s32[]{:S(2)}) async-start(), calls=%async_computation.25 | async-start | bytes 655360 | tf_op jit(solution)/shard_map/reduce_scatter | solution.py:383
  703.0 142.8 %reduce-scatter.37.cloned.1.call-start = ((), (), s32[]{:S(2)}) async-start(), calls=%async_computation.30 | async-start | bytes 327680
  722.3 127.9 %reduce-scatter.23.cloned.1.call-start = ((), (), s32[]{:S(2)}) async-start(), calls=%async_computation.22 | async-start | bytes 327680 | tf_op jit(solution)/shard_map/reduce_scatter | solution.py:397
  751.9 118.1 %reduce-scatter.27.cloned.1.call-start = ((), (), s32[]{:S(2)}) async-start(), calls=%async_computation.24 | async-start | bytes 163840 | tf_op jit(solution)/shard_map/reduce_scatter | solution.py:400
  779.7 110.0 %reduce-scatter.31.cloned.1.call-start = ((), (), s32[]{:S(2)}) async-start(), calls=%async_computation.26 | async-start | bytes 163840 | tf_op jit(solution)/shard_map/reduce_scatter | solution.py:403
  807.7 103.8 %all-reduce.17.cloned.1.call-start = ((), (), s32[]{:S(2)}) async-start(), calls=%async_computation.20 | async-start | bytes 4194304 | tf_op jit(solution)/shard_map/psum | solution.py:126
  811.5 315.7 %reduce-scatter.35.cloned.1.call-start = ((), (), s32[]{:S(2)}) async-start(), calls=%async_computation.28 | async-start | bytes 15728640 | tf_op jit(solution)/shard_map/reduce_scatter | solution.py:415
  842.6 71.2 %copy-start.53 = (bf16[1024]{0:T(1024)(128)(2,1)S(1)}, bf16[1024]{0:T(1024)(128)(2,1)}, u32[]{:S(2)}) copy-start(bf16[1024]{0:T(1024)(128)(2,1)} %get-tuple-element.468) | copy-start | bytes 6148
  842.6 94.9 %copy-start.44 = (f32[512]{0:T(512)S(1)}, f32[512]{0:T(512)}, u32[]{:S(2)}) copy-start(f32[512]{0:T(512)} %copy-done.43) | copy-start | bytes 6148
  842.6 94.9 %copy-start.4 = (f32[512,1024]{1,0:T(8,128)S(1)}, f32[512,1024]{1,0:T(8,128)}, u32[]{:S(2)}) copy-start(f32[512,1024]{1,0:T(8,128)} %copy-done.3) | copy-start | bytes 6291460
  (34 other events, 114.1 us)
Sparse Core Ops, SparseCore 0:
  9.8 30.2 all-gather.10
  44.7 46.0 all-gather.8
  92.6 25.1 all-gather.12
  197.1 20.1 all-reduce.14
  218.9 54.2 all-gather.14
  275.5 52.5 all-gather.16
  398.9 52.5 reduce-scatter.16
  454.5 52.5 reduce-scatter.14
  612.4 76.8 reduce-scatter.18
  692.0 28.3 reduce-scatter.32
  723.9 27.9 reduce-scatter.20
  754.6 25.0 reduce-scatter.24
  782.5 25.0 reduce-scatter.28
  809.8 19.9 reduce-scatter.36
  831.9 18.2 reduce-scatter.22
  852.3 17.6 reduce-scatter.26
  872.1 17.6 reduce-scatter.30
  891.9 19.4 all-reduce.16
  913.8 213.3 reduce-scatter.34

commit v2 on v1

v2 whole, which is shorter than its diff:
```python
import functools

import jax
import jax.numpy as jnp
from jax import lax
from jax.experimental import pallas as pl
from jax.experimental.pallas import tpu as pltpu
from jax.sharding import PartitionSpec as P

HEAD_DIM = 64
TOP = 8
PIC = 256
CAP = 144

EPSILON = 1e-06
THETA = 10000.0
NEG_FILL = -1e30


KEY_ROWS = 256
NT = (((1,), (1,)), ((), ()))
LIMIT = 60 * 1024 * 1024


def seen_bias(flags, j, blocks, kinfo_ref, qinfo_ref):
    rows = pl.ds(pl.multiple_of(j * KEY_ROWS, KEY_ROWS), KEY_ROWS)
    q_doc, q_pic = qinfo_ref[0:1, :], qinfo_ref[1:2, :]
    k_doc, k_pic = kinfo_ref[rows, 0:1], kinfo_ref[rows, 1:2]
    q_place = flags[blocks] + lax.broadcasted_iota(jnp.int32, q_doc.shape, 1)
    k_place = j * KEY_ROWS + lax.broadcasted_iota(jnp.int32, k_doc.shape, 0)
    seen = (k_doc == q_doc) & ((k_place <= q_place) | ((k_pic == q_pic) & (q_pic >= 0)))
    return rows, jnp.where(seen, 0.0, NEG_FILL)


def attend_kernel(
    flags, q_ref, kv_ref, kinfo_ref, qinfo_ref, out_w_ref, mix_ref, full_ref, log_ref, part_ref,
    acc, top, total,
):
    blocks = kv_ref.shape[0] // KEY_ROWS
    kv_width = kv_ref.shape[1] // 2
    heads, kv_heads = q_ref.shape[1] // HEAD_DIM, kv_width // HEAD_DIM
    top[...] = jnp.full(top.shape, NEG_FILL, jnp.float32)
    total[...] = jnp.zeros(total.shape, jnp.float32)
    acc[...] = jnp.zeros(acc.shape, jnp.float32)

    def step(j, carry):
        @pl.when(flags[j] > 0)
        def _():
            rows, bias = seen_bias(flags, j, blocks, kinfo_ref, qinfo_ref)
            for g in range(kv_heads):
                key = kv_ref[rows, g * HEAD_DIM : (g + 1) * HEAD_DIM]
                val = kv_ref[rows, kv_width + g * HEAD_DIM : kv_width + (g + 1) * HEAD_DIM]
                val_t = jnp.transpose(val.astype(jnp.float32)).astype(jnp.bfloat16)
                for h in range(g * heads // kv_heads, (g + 1) * heads // kv_heads):
                    at = slice(h * HEAD_DIM, (h + 1) * HEAD_DIM)
                    scores = bias + lax.dot_general(
                        key, q_ref[:, at], NT, preferred_element_type=jnp.float32
                    )
                    old = top[h : h + 1, :]
                    new = jnp.maximum(old, jnp.max(scores, axis=0, keepdims=True))
                    probs = jnp.exp(scores - new)
                    fade = jnp.exp(old - new)
                    total[h : h + 1, :] = total[h : h + 1, :] * fade + jnp.sum(
                        probs, axis=0, keepdims=True
                    )
                    acc[at, :] = acc[at, :] * fade + jnp.dot(
                        val_t, probs.astype(jnp.bfloat16), preferred_element_type=jnp.float32
                    )
                    top[h : h + 1, :] = new

        return carry

    lax.fori_loop(0, blocks, step, 0)
    log_ref[...] = top[...] + jnp.log(total[...])
    for h in range(heads):
        at = slice(h * HEAD_DIM, (h + 1) * HEAD_DIM)
        acc[at, :] = acc[at, :] / total[h : h + 1, :]
    full = jnp.transpose(acc[...])
    full_ref[...] = full
    mix_ref[...] = full.astype(jnp.bfloat16)
    part_ref[...] = jnp.dot(
        mix_ref[...], out_w_ref[...], preferred_element_type=jnp.float32
    ).astype(jnp.bfloat16)


def attend_back_kernel(
    flags, q_ref, kv_ref, kinfo_ref, qinfo_ref, log_ref, full_ref, grad_ref, dq_ref, dkv_ref,
    acc, delta,
):
    blocks = kv_ref.shape[0] // KEY_ROWS
    kv_width = kv_ref.shape[1] // 2
    heads, kv_heads = q_ref.shape[1] // HEAD_DIM, kv_width // HEAD_DIM
    acc[...] = jnp.transpose(full_ref[...] * grad_ref[...].astype(jnp.float32))
    for h in range(heads):
        delta[h : h + 1, :] = jnp.sum(
            acc[h * HEAD_DIM : (h + 1) * HEAD_DIM, :], axis=0, keepdims=True
        )
    acc[...] = jnp.zeros(acc.shape, jnp.float32)

    def step(j, carry):
        @pl.when(flags[j] > 0)
        def _():
            rows, bias = seen_bias(flags, j, blocks, kinfo_ref, qinfo_ref)
            for g in range(kv_heads):
                k_at = slice(g * HEAD_DIM, (g + 1) * HEAD_DIM)
                v_at = slice(kv_width + g * HEAD_DIM, kv_width + (g + 1) * HEAD_DIM)
                key, val = kv_ref[rows, k_at], kv_ref[rows, v_at]
                key_t = jnp.transpose(key.astype(jnp.float32)).astype(jnp.bfloat16)
                dk = jnp.zeros((KEY_ROWS, HEAD_DIM), jnp.float32)
                dv = jnp.zeros((KEY_ROWS, HEAD_DIM), jnp.float32)
                for h in range(g * heads // kv_heads, (g + 1) * heads // kv_heads):
                    at = slice(h * HEAD_DIM, (h + 1) * HEAD_DIM)
                    q_rows, g_rows = q_ref[:, at], grad_ref[:, at]
                    scores = bias + lax.dot_general(
                        key, q_rows, NT, preferred_element_type=jnp.float32
                    )
                    probs = jnp.exp(scores - log_ref[h : h + 1, :])
                    prob_grad = lax.dot_general(
                        val, g_rows, NT, preferred_element_type=jnp.float32
                    )
                    slope = (probs * (prob_grad - delta[h : h + 1, :])).astype(jnp.bfloat16)
                    dv += jnp.dot(
                        probs.astype(jnp.bfloat16), g_rows, preferred_element_type=jnp.float32
                    )
                    dk += jnp.dot(slope, q_rows, preferred_element_type=jnp.float32)
                    acc[at, :] += jnp.dot(key_t, slope, preferred_element_type=jnp.float32)
                dkv_ref[rows, k_at] = dk.astype(dkv_ref.dtype)
                dkv_ref[rows, v_at] = dv.astype(dkv_ref.dtype)

        @pl.when(flags[j] == 0)
        def _():
            rows = pl.ds(pl.multiple_of(j * KEY_ROWS, KEY_ROWS), KEY_ROWS)
            dkv_ref[rows, :] = jnp.zeros((KEY_ROWS, dkv_ref.shape[1]), dkv_ref.dtype)

        return carry

    lax.fori_loop(0, blocks, step, 0)
    dq_ref[...] = jnp.transpose(acc[...]) * (HEAD_DIM**-0.5)


def whole_vmem(count):
    return [pl.BlockSpec(memory_space=pltpu.VMEM)] * count


def attend(flags, q, kv, kinfo, qinfo, out_w):
    rows, width = q.shape
    heads = width // HEAD_DIM
    return pl.pallas_call(
        attend_kernel,
        name="attend",
        in_specs=[pl.BlockSpec(memory_space=pltpu.SMEM)] + whole_vmem(5),
        out_specs=whole_vmem(4),
        out_shape=[
            jax.ShapeDtypeStruct((rows, width), jnp.bfloat16),
            jax.ShapeDtypeStruct((rows, width), jnp.float32),
            jax.ShapeDtypeStruct((heads, rows), jnp.float32),
            jax.ShapeDtypeStruct((rows, out_w.shape[1]), jnp.bfloat16),
        ],
        scratch_shapes=[
            pltpu.VMEM((width, rows), jnp.float32),
            pltpu.VMEM((heads, rows), jnp.float32),
            pltpu.VMEM((heads, rows), jnp.float32),
        ],
        compiler_params=pltpu.CompilerParams(vmem_limit_bytes=LIMIT),
    )(flags, q, kv, kinfo, qinfo, out_w)


def attend_back(flags, q, kv, kinfo, qinfo, log_total, full, grad):
    rows, width = q.shape
    return pl.pallas_call(
        attend_back_kernel,
        name="attend_back",
        in_specs=[pl.BlockSpec(memory_space=pltpu.SMEM)] + whole_vmem(7),
        out_specs=whole_vmem(2),
        out_shape=[
            jax.ShapeDtypeStruct((rows, width), jnp.float32),
            jax.ShapeDtypeStruct(kv.shape, jnp.bfloat16),
        ],
        scratch_shapes=[
            pltpu.VMEM((width, rows), jnp.float32),
            pltpu.VMEM((width // HEAD_DIM, rows), jnp.float32),
        ],
        compiler_params=pltpu.CompilerParams(vmem_limit_bytes=LIMIT),
    )(flags, q, kv, kinfo, qinfo, log_total, full, grad)


def block_flags(pic_starts, q_docs, k_docs, offset):
    block_len, length = q_docs.shape[0], k_docs.shape[0]
    docs = k_docs.reshape(length // KEY_ROWS, KEY_ROWS)
    first = jnp.arange(length // KEY_ROWS, dtype=jnp.int32) * KEY_ROWS
    same = (docs[:, 0] <= q_docs[-1]) & (docs[:, -1] >= q_docs[0])
    spans = (
        (pic_starts[None, :] < offset + block_len)
        & (pic_starts[None, :] + PIC > offset)
        & (pic_starts[None, :] < first[:, None] + KEY_ROWS)
        & (pic_starts[None, :] + PIC > first[:, None])
    )
    needed = same & ((first < offset + block_len) | jnp.any(spans, axis=1))
    return jnp.concatenate([needed.astype(jnp.int32), offset[None].astype(jnp.int32)])


MESH = pl.DeviceIdType.MESH


def place_on(axes):
    index, size = 0, 1
    for axis in axes:
        index = index * lax.axis_size(axis) + lax.axis_index(axis)
        size *= lax.axis_size(axis)
    return index, size


def peer_id(axes, index):
    ids = {}
    for axis in reversed(axes):
        count = lax.axis_size(axis)
        ids[axis] = lax.rem(index, count)
        index = lax.div(index, count)
    return ids


def greet(groups):
    barrier = pltpu.get_barrier_semaphore()
    count = 0
    for axes in groups:
        me, size = place_on(axes)

        def signal(k, carry, axes=axes, me=me, size=size):
            pl.semaphore_signal(
                barrier,
                inc=1,
                device_id=peer_id(axes, lax.rem(me + k, size)),
                device_id_type=MESH,
            )
            return carry

        lax.fori_loop(1, size, signal, 0)
        count += size - 1
    pl.semaphore_wait(barrier, count)


def spread_kernel(axes_of, *refs):
    count = len(axes_of)
    ins, outs, sems = refs[:count], refs[count : 2 * count], refs[2 * count :]
    groups = []
    for axes in axes_of:
        if axes not in groups:
            groups.append(axes)
    greet(groups)

    def copy(i, k):
        me, size = place_on(axes_of[i])
        return pltpu.make_async_remote_copy(
            src_ref=ins[i],
            dst_ref=outs[i].at[me],
            send_sem=sems[2 * i].at[k],
            recv_sem=sems[2 * i + 1].at[k],
            device_id=peer_id(axes_of[i], lax.rem(me + k, size)),
            device_id_type=MESH,
        )

    def start(i, k):
        copy(i, k).start()
        return 0

    def finish(i, k):
        copy(i, k).wait()
        return 0

    for i in range(count):
        lax.fori_loop(1, place_on(axes_of[i])[1], lambda k, c, i=i: start(i, k), 0)
    for i in range(count):
        outs[i][place_on(axes_of[i])[0]] = ins[i][...]
    for i in range(count):
        lax.fori_loop(1, place_on(axes_of[i])[1], lambda k, c, i=i: finish(i, k), 0)


def spread(arrays, axes_of, ident, name):
    sizes = [place_on(axes)[1] for axes in axes_of]
    scratch = []
    for size in sizes:
        scratch += [pltpu.SemaphoreType.DMA((size,)), pltpu.SemaphoreType.DMA((size,))]
    return pl.pallas_call(
        functools.partial(spread_kernel, tuple(axes_of)),
        name=name,
        in_specs=whole_vmem(len(arrays)),
        out_specs=whole_vmem(len(arrays)),
        out_shape=[
            jax.ShapeDtypeStruct((size,) + a.shape, a.dtype) for size, a in zip(sizes, arrays)
        ],
        scratch_shapes=scratch,
        compiler_params=pltpu.CompilerParams(
            collective_id=ident, has_side_effects=True, vmem_limit_bytes=LIMIT
        ),
    )(*arrays)


def swap_sum_kernel(axes, x_ref, out_ref, held, send, recv):
    me, size = place_on(axes)
    greet([axes])

    def copy(k):
        peer = lax.rem(me + k, size)
        return pltpu.make_async_remote_copy(
            src_ref=x_ref.at[peer],
            dst_ref=held.at[k],
            send_sem=send.at[k],
            recv_sem=recv.at[k],
            device_id=peer_id(axes, peer),
            device_id_type=MESH,
        )

    def start(k, carry):
        copy(k).start()
        return carry

    def finish(k, carry):
        copy(k).wait()
        out_ref[...] += held[k].astype(jnp.float32)
        return carry

    lax.fori_loop(1, size, start, 0)
    out_ref[...] = x_ref[me].astype(jnp.float32)
    lax.fori_loop(1, size, finish, 0)


def swap_sum(x, axes, ident, name):
    size = place_on(axes)[1]
    return pl.pallas_call(
        functools.partial(swap_sum_kernel, tuple(axes)),
        name=name,
        in_specs=whole_vmem(1),
        out_specs=pl.BlockSpec(memory_space=pltpu.VMEM),
        out_shape=jax.ShapeDtypeStruct(x.shape[1:], jnp.float32),
        scratch_shapes=[
            pltpu.VMEM(x.shape, x.dtype),
            pltpu.SemaphoreType.DMA((size,)),
            pltpu.SemaphoreType.DMA((size,)),
        ],
        compiler_params=pltpu.CompilerParams(
            collective_id=ident, has_side_effects=True, vmem_limit_bytes=LIMIT
        ),
    )(x)


def pair_copy(ref, dst, sems, k):
    return pltpu.make_async_remote_copy(
        src_ref=ref,
        dst_ref=dst,
        send_sem=sems[0].at[k],
        recv_sem=sems[1].at[k],
        device_id={"tp": 1 - lax.axis_index("tp")},
        device_id_type=MESH,
    )


def share_rows_kernel(
    part_ref, x_ref, gain_ref, hidden_ref, all_ref, held, normed, send, recv, up_send, up_recv
):
    me, size = place_on(("dp",))
    half = part_ref.shape[0] // 2
    core = lax.axis_index("tp")
    mine = pl.ds(pl.multiple_of(core * half, half), half)
    greet([("dp",), ("tp",)])
    swap = pair_copy(part_ref, held, (up_send, up_recv), 0)
    swap.start()
    swap.wait()

    def norm(rows):
        total = (
            x_ref[rows, :].astype(jnp.float32)
            + (part_ref[rows, :].astype(jnp.float32) + held[rows, :].astype(jnp.float32))
        )
        hidden_ref[rows, :] = total
        scale = lax.rsqrt(jnp.mean(total * total, axis=-1, keepdims=True) + EPSILON)
        normed[rows, :] = (total * scale * gain_ref[...]).astype(jnp.bfloat16)

    def copy(k):
        return pltpu.make_async_remote_copy(
            src_ref=normed.at[mine],
            dst_ref=all_ref.at[me, mine],
            send_sem=send.at[k],
            recv_sem=recv.at[k],
            device_id={"dp": lax.rem(me + k, size)},
            device_id_type=MESH,
        )

    def relay(k):
        source = lax.rem(me + size - k, size)
        return pair_copy(all_ref.at[source, mine], all_ref.at[source, mine], (up_send, up_recv), k)

    def start(k, carry):
        copy(k).start()
        return carry

    def forward(k, carry):
        copy(k).wait_recv()
        relay(k).start()
        return carry

    def finish(k, carry):
        copy(k).wait_send()
        relay(k).wait()
        return carry

    norm(mine)
    lax.fori_loop(1, size, start, 0)
    norm(pl.ds(pl.multiple_of((1 - core) * half, half), half))
    all_ref[me] = normed[...]
    lax.fori_loop(1, size, forward, 0)
    lax.fori_loop(1, size, finish, 0)


def share_rows(part, x, gain, ident):
    size = lax.axis_size("dp")
    rows, width = part.shape
    sems = pltpu.SemaphoreType.DMA((size,))
    return pl.pallas_call(
        share_rows_kernel,
        name="share_rows",
        in_specs=whole_vmem(3),
        out_specs=whole_vmem(2),
        out_shape=[
            jax.ShapeDtypeStruct((rows, width), jnp.float32),
            jax.ShapeDtypeStruct((size, rows, width), jnp.bfloat16),
        ],
        scratch_shapes=[
            pltpu.VMEM((rows, width), jnp.bfloat16),
            pltpu.VMEM((rows, width), jnp.bfloat16),
            sems,
            sems,
            sems,
            sems,
        ],
        compiler_params=pltpu.CompilerParams(
            collective_id=ident, has_side_effects=True, vmem_limit_bytes=LIMIT
        ),
    )(part, x, gain)


def return_rows_kernel(
    part_ref, out_ref, held, summed, landed, sent, send, recv, up_send, up_recv
):
    me, size = place_on(("dp",))
    half = part_ref.shape[1] // 2
    core = lax.axis_index("tp")
    mine = pl.ds(pl.multiple_of(core * half, half), half)
    theirs = pl.ds(pl.multiple_of((1 - core) * half, half), half)
    greet([("dp",), ("tp",)])

    def swap(k):
        group = lax.rem(me + k, size)
        return pair_copy(part_ref.at[group, theirs], held.at[k], (up_send, up_recv), k)

    def copy(k):
        return pltpu.make_async_remote_copy(
            src_ref=summed.at[k],
            dst_ref=landed.at[k],
            send_sem=send.at[k],
            recv_sem=recv.at[k],
            device_id={"dp": lax.rem(me + k, size)},
            device_id_type=MESH,
        )

    def total(k):
        group = lax.rem(me + k, size)
        return part_ref[group, mine].astype(jnp.float32) + held[k].astype(jnp.float32)

    def first(k, carry):
        swap(lax.rem(k, size)).start()
        return carry

    def second(k, carry):
        swap(k).wait_recv()
        summed[k] = total(k).astype(jnp.bfloat16)
        copy(k).start()
        return carry

    def third(k, carry):
        copy(k).wait_recv()
        out_ref[mine, :] += landed[k].astype(jnp.float32)
        return carry

    def finish(k, carry):
        swap(k).wait_send()
        copy(k).wait_send()
        return carry

    lax.fori_loop(1, size + 1, first, 0)
    lax.fori_loop(1, size, second, 0)
    swap(0).wait()
    out_ref[mine, :] = total(0)
    lax.fori_loop(1, size, third, 0)
    sent[...] = out_ref[mine, :].astype(jnp.bfloat16)
    out_ref[mine, :] = sent[...].astype(jnp.float32)
    last = pair_copy(sent, summed.at[0], (up_send, up_recv), size)
    last.start()
    lax.fori_loop(1, size, finish, 0)
    last.wait()
    out_ref[theirs, :] = summed[0].astype(jnp.float32)


def return_rows(part, ident, name):
    size, rows, width = part.shape
    blocks = pltpu.VMEM((size, rows // 2, width), jnp.bfloat16)
    sems, more = pltpu.SemaphoreType.DMA((size,)), pltpu.SemaphoreType.DMA((size + 1,))
    return pl.pallas_call(
        return_rows_kernel,
        name=name,
        in_specs=whole_vmem(1),
        out_specs=pl.BlockSpec(memory_space=pltpu.VMEM),
        out_shape=jax.ShapeDtypeStruct((rows, width), jnp.float32),
        scratch_shapes=[
            blocks,
            blocks,
            blocks,
            pltpu.VMEM((rows // 2, width), jnp.bfloat16),
            sems,
            sems,
            more,
            more,
        ],
        compiler_params=pltpu.CompilerParams(
            collective_id=ident, has_side_effects=True, vmem_limit_bytes=LIMIT
        ),
    )(part)


def back_blocks(ctx_size, block_len, length):
    return min(ctx_size - 1, -(-(length // 2 - 1) // block_len))


def ahead_blocks(block_len, length, spans):
    return 0 if block_len % (length // spans) == 0 else 1


def greet_line():
    me, size = lax.axis_index("ctx"), lax.axis_size("ctx")
    barrier = pltpu.get_barrier_semaphore()
    for step in (1, -1):
        other = me + step

        @pl.when((other >= 0) & (other < size))
        def _(other=other):
            pl.semaphore_signal(
                barrier, inc=1, device_id={"ctx": other}, device_id_type=MESH
            )

    inner = (me > 0) & (me < size - 1)

    @pl.when(inner)
    def _():
        pl.semaphore_wait(barrier, 2)

    @pl.when(jnp.logical_not(inner))
    def _():
        pl.semaphore_wait(barrier, 1)


def line_copy(src, dst, sems, k, other):
    return pltpu.make_async_remote_copy(
        src_ref=src,
        dst_ref=dst,
        send_sem=sems[0].at[k],
        recv_sem=sems[1].at[k],
        device_id={"ctx": other},
        device_id_type=MESH,
    )


def window_kernel(back, ahead, kv_ref, all_ref, send, recv):
    me, size = lax.axis_index("ctx"), lax.axis_size("ctx")
    greet_line()
    right, left = me + 1, me - 1
    if ahead:

        @pl.when(left >= 0)
        def _():
            line_copy(kv_ref, all_ref.at[me], (send, recv), back, left).start()

    for s in range(back):
        src = kv_ref if s == 0 else all_ref.at[lax.rem(me + size - s, size)]
        block = lax.rem(me + size - s, size)
        came = lax.rem(me + size - s - 1, size)

        @pl.when((right < size) & (me - s >= 0))
        def _(src=src, block=block, s=s):
            line_copy(src, all_ref.at[block], (send, recv), s, right).start()

        if s == 0:
            all_ref[me] = kv_ref[...]

        @pl.when(me - s - 1 >= 0)
        def _(came=came, s=s):
            line_copy(kv_ref, all_ref.at[came], (send, recv), s, right).wait_recv()

    for s in range(back):

        @pl.when((right < size) & (me - s >= 0))
        def _(s=s):
            line_copy(kv_ref, all_ref.at[me], (send, recv), s, right).wait_send()

    if ahead:

        @pl.when(left >= 0)
        def _():
            line_copy(kv_ref, all_ref.at[me], (send, recv), back, left).wait_send()

        @pl.when(right < size)
        def _():
            line_copy(kv_ref, all_ref.at[me], (send, recv), back, left).wait_recv()


def window(kv, back, ahead, ident):
    return pl.pallas_call(
        functools.partial(window_kernel, back, ahead),
        name="window",
        in_specs=whole_vmem(1),
        out_specs=pl.BlockSpec(memory_space=pltpu.VMEM),
        out_shape=jax.ShapeDtypeStruct((lax.axis_size("ctx"),) + kv.shape, kv.dtype),
        scratch_shapes=[
            pltpu.SemaphoreType.DMA((back + 1,)),
            pltpu.SemaphoreType.DMA((back + 1,)),
        ],
        compiler_params=pltpu.CompilerParams(
            collective_id=ident, has_side_effects=True, vmem_limit_bytes=LIMIT
        ),
    )(kv)


def window_sum_kernel(back, ahead, grad_ref, out_ref, going, came, send, recv):
    me, size = lax.axis_index("ctx"), lax.axis_size("ctx")
    greet_line()
    right, left = me + 1, me - 1
    if ahead:

        @pl.when(right < size)
        def _():
            line_copy(
                grad_ref.at[lax.rem(me + 1, size)], came.at[0], (send, recv), 0, right
            ).start()

    for s in range(back, 0, -1):
        piece = lax.rem(me + size - s, size)

        own = grad_ref.at[piece]
        if s == back:

            @pl.when(me - s >= 0)
            def _(own=own, s=s):
                line_copy(own, came.at[s], (send, recv), s, left).start()

        else:

            @pl.when((me - s >= 0) & (right < size))
            def _(piece=piece, s=s):
                line_copy(going.at[s], came.at[s + 1], (send, recv), s + 1, left).wait_recv()
                going[s] = (
                    grad_ref[piece].astype(jnp.float32) + came[s + 1].astype(jnp.float32)
                ).astype(going.dtype)
                line_copy(going.at[s], came.at[s], (send, recv), s, left).start()

            @pl.when((me - s >= 0) & (right >= size))
            def _(own=own, s=s):
                line_copy(own, came.at[s], (send, recv), s, left).start()

    out_ref[...] = grad_ref[me].astype(jnp.float32)

    @pl.when(right < size)
    def _():
        line_copy(going.at[1], came.at[1], (send, recv), 1, left).wait_recv()
        out_ref[...] += came[1].astype(jnp.float32)

    if ahead:

        @pl.when(left >= 0)
        def _():
            line_copy(going.at[1], came.at[0], (send, recv), 0, left).wait_recv()
            out_ref[...] += came[0].astype(jnp.float32)

        @pl.when(right < size)
        def _():
            line_copy(going.at[1], came.at[0], (send, recv), 0, right).wait_send()

    for s in range(back, 0, -1):

        @pl.when(me - s >= 0)
        def _(s=s):
            line_copy(going.at[s], came.at[s], (send, recv), s, left).wait_send()


def window_sum(grad, back, ahead, ident):
    held = pltpu.VMEM((back + 1,) + grad.shape[1:], grad.dtype)
    return pl.pallas_call(
        functools.partial(window_sum_kernel, back, ahead),
        name="window_sum",
        in_specs=whole_vmem(1),
        out_specs=pl.BlockSpec(memory_space=pltpu.VMEM),
        out_shape=jax.ShapeDtypeStruct(grad.shape[1:], jnp.float32),
        scratch_shapes=[
            held,
            held,
            pltpu.SemaphoreType.DMA((back + 1,)),
            pltpu.SemaphoreType.DMA((back + 1,)),
        ],
        compiler_params=pltpu.CompilerParams(
            collective_id=ident, has_side_effects=True, vmem_limit_bytes=LIMIT
        ),
    )(grad)


def rms_norm(tensor, gain_vec):
    return (
        tensor * lax.rsqrt(jnp.mean(tensor * tensor, axis=-1, keepdims=True) + EPSILON) * gain_vec
    )


def norm_back(x, gain, grad):
    scale = lax.rsqrt(jnp.mean(x * x, axis=-1, keepdims=True) + EPSILON)
    unit = x * scale
    pull = grad * gain
    return (
        scale * (pull - unit * jnp.mean(pull * unit, axis=-1, keepdims=True)),
        jnp.sum(grad * unit, axis=0),
    )


def rotary_tables(token_positions, heads):
    half_dim = HEAD_DIM // 2
    inverse = THETA ** (-(jnp.arange(half_dim, dtype=jnp.float32) * 2.0 / HEAD_DIM))
    angles = token_positions.astype(jnp.float32)[:, None] * inverse[None, :]
    return jnp.cos(angles)[:, None, :], jnp.sin(angles)[:, None, :]


def rotate(tensor, tables, sign):
    rows, width = tensor.shape
    parts = tensor.reshape(rows, width // HEAD_DIM, 2, HEAD_DIM // 2)
    cosine, sine = tables
    first, second = parts[:, :, 0], parts[:, :, 1]
    sine = sine * sign
    return jnp.stack([first * cosine - second * sine, second * cosine + first * sine], 2).reshape(
        rows, width
    )


def picture_of(starts, token_positions):
    inside = (token_positions[:, None] >= starts[None, :]) & (
        token_positions[:, None] < starts[None, :] + PIC
    )
    labels = jnp.arange(starts.shape[0], dtype=jnp.int32) + 1
    return jnp.sum(jnp.where(inside, labels[None, :], 0), axis=-1) - 1


def silu_parts(gate_pre):
    sig = jax.nn.sigmoid(gate_pre)
    return gate_pre * sig, sig * (1.0 + gate_pre * (1.0 - sig))


def experts(weights, chosen_all, gates_all, rows_all, grad_all):
    own, _, model_width, _ = weights.shape
    groups, tok_rows, _ = rows_all.shape
    first_own = lax.axis_index("dp") * own
    named = chosen_all[..., None] == first_own + jnp.arange(own, dtype=jnp.int32)
    names = jnp.any(named, axis=2)
    gate_of = jnp.sum(jnp.where(named, gates_all[..., None], 0.0), axis=2)
    earlier = jnp.tril(jnp.ones((tok_rows, tok_rows), jnp.bfloat16), -1)
    place = jnp.einsum(
        "rq,gqe->gre", earlier, names.astype(jnp.bfloat16), preferred_element_type=jnp.float32
    ).astype(jnp.int32)
    place = jnp.where(names & (place < CAP), place, -1)
    picks = place.transpose(0, 2, 1)[:, :, None, :] == jnp.arange(CAP, dtype=jnp.int32)[:, None]
    slot_gate = jnp.sum(jnp.where(picks, gate_of.transpose(0, 2, 1)[:, :, None, :], 0.0), axis=-1)
    picks = picks.astype(jnp.bfloat16)
    gate_col = slot_gate.transpose(1, 0, 2).reshape(own, groups * CAP, 1)

    def take(source):
        return jnp.einsum(
            "gesr,grd->egsd", picks, source, preferred_element_type=jnp.float32
        ).reshape(own, groups * CAP, model_width)

    def into(slots, matrix):
        return jnp.einsum("ecd,edf->ecf", slots, matrix, preferred_element_type=jnp.float32)

    def back(slots, matrix):
        return jnp.einsum("ecf,edf->ecd", slots, matrix, preferred_element_type=jnp.float32)

    def outer(left, right):
        return jnp.einsum("ecd,ecf->edf", left, right, preferred_element_type=jnp.float32)

    def combine(slots):
        return jnp.einsum(
            "gesr,egsd->grd",
            picks,
            slots.astype(jnp.bfloat16).reshape(own, groups, CAP, model_width),
            preferred_element_type=jnp.float32,
        ).astype(jnp.bfloat16)

    slot_rows = take(rows_all).astype(jnp.bfloat16)
    slot_grads = (take(grad_all) * gate_col).astype(jnp.bfloat16)
    gate_pre, up_pre = into(slot_rows, weights[:, 0]), into(slot_rows, weights[:, 1])
    silu, slope = silu_parts(gate_pre)
    act_grad = into(slot_grads, weights[:, 2])
    gate_low = (act_grad * up_pre * slope).astype(jnp.bfloat16)
    up_low = (act_grad * silu).astype(jnp.bfloat16)
    act_low = (silu * up_pre).astype(jnp.bfloat16)
    back_part = combine(back(gate_low, weights[:, 0]) + back(up_low, weights[:, 1]))
    out_part = combine(back(act_low, weights[:, 2]) * gate_col)
    weight_part = jnp.stack(
        [outer(slot_rows, gate_low), outer(slot_rows, up_low), outer(slot_grads, act_low)], axis=1
    ).astype(jnp.bfloat16)
    return out_part, back_part, weight_part


def body(
    tokens,
    query_weight,
    key_weight,
    value_weight,
    output_weight,
    gain_attn,
    gain_moe,
    expert_weights,
    routes,
    gate_values,
    documents,
    pic_starts,
    cotangent,
):
    _, block_len, model_width = tokens.shape
    dp_size, ctx_size = lax.axis_size("dp"), lax.axis_size("ctx")
    length = block_len * ctx_size
    offset = lax.axis_index("ctx") * block_len
    back = back_blocks(ctx_size, block_len, length)
    ahead = ahead_blocks(block_len, length, pic_starts.shape[1])
    q_width, kv_width = query_weight.shape[1], key_weight.shape[1]

    joined_w = jnp.concatenate([query_weight, key_weight, value_weight], axis=1)
    gains = jnp.stack([gain_attn, gain_moe]).astype(jnp.float32)
    joined_all, gains_all, docs_all, chosen_all, gates_all = spread(
        [
            joined_w,
            gains,
            documents,
            routes.reshape(block_len * TOP // 128, 128),
            gate_values.reshape(block_len * TOP // 128, 128),
        ],
        [("dp",), ("dp",), ("ctx",), ("dp",), ("dp",)],
        1,
        "spread_weights",
    )
    output_weight, cot, joined_all = lax.optimization_barrier(
        (output_weight, cotangent[0], joined_all)
    )
    output_full = lax.all_gather(output_weight, "dp", axis=1, tiled=True)
    grad_all = lax.all_gather(cot, "dp", axis=0)
    chosen_all = chosen_all.reshape(dp_size, block_len, TOP)
    gates_all = gates_all.reshape(dp_size, block_len, TOP)
    joined_full = joined_all.reshape(model_width, -1)
    gain_rows = gains_all.transpose(1, 0, 2).reshape(2, 1, model_width)
    docs_all = docs_all.reshape(length)

    pictures = picture_of(pic_starts[0], jnp.arange(length, dtype=jnp.int32))
    flags = block_flags(pic_starts[0], documents[0], docs_all, offset)
    kinfo = jnp.stack([docs_all, pictures], axis=1)
    qinfo = jnp.stack([documents[0], lax.dynamic_slice_in_dim(pictures, offset, block_len)])
    tables = rotary_tables(offset + jnp.arange(block_len, dtype=jnp.int32), 1)

    x = tokens[0].astype(jnp.float32)
    normed_one = rms_norm(x, gain_rows[0]).astype(jnp.bfloat16)
    projected = jnp.dot(normed_one, joined_full, preferred_element_type=jnp.float32)
    rotated = rotate(projected[:, : q_width + kv_width], tables, 1.0).astype(jnp.bfloat16)
    query = rotated[:, :q_width] * jnp.bfloat16(HEAD_DIM**-0.5)
    kv = jnp.concatenate(
        [rotated[:, q_width:], projected[:, q_width + kv_width :].astype(jnp.bfloat16)], axis=1
    )
    kv_all = window(kv, back, ahead, 2).reshape(length, 2 * kv_width)
    mixture, mix_full, log_total, attn_part = attend(
        flags, query, kv_all, kinfo, qinfo, output_full
    )
    hidden, rows_all = share_rows(attn_part, tokens[0], gain_rows[1], 3)
    out_part, back_part, weight_part = experts(
        expert_weights, chosen_all, gates_all, rows_all, grad_all
    )
    expert_grad = lax.psum_scatter(weight_part, "ctx", scatter_dimension=2, tiled=True)
    normed_two_grad = return_rows(back_part, 4, "return_grads")
    layer_out = hidden + return_rows(out_part, 5, "return_rows")

    norm_grad, gain_two_grad = norm_back(hidden, gain_rows[1], normed_two_grad)
    hidden_grad = cotangent[0].astype(jnp.float32) + norm_grad
    hidden_low = hidden_grad.astype(jnp.bfloat16)
    output_grad = lax.dot_general(
        hidden_low, mixture, (((0,), (0,)), ((), ())), preferred_element_type=jnp.float32
    )
    mix_grad = lax.dot_general(
        hidden_low, output_full, NT, preferred_element_type=jnp.float32
    ).astype(jnp.bfloat16)
    q_rot_grad, kv_part = attend_back(
        flags, query, kv_all, kinfo, qinfo, log_total, mix_full, mix_grad
    )
    kv_back = window_sum(kv_part.reshape(ctx_size, block_len, 2 * kv_width), back, ahead, 6)
    qk_grad = rotate(jnp.concatenate([q_rot_grad, kv_back[:, :kv_width]], axis=1), tables, -1.0)
    joined_grad = jnp.concatenate([qk_grad, kv_back[:, kv_width:]], axis=1).astype(jnp.bfloat16)
    joined_w_grad = lax.dot_general(
        normed_one, joined_grad, (((0,), (0,)), ((), ())), preferred_element_type=jnp.float32
    )
    normed_part = lax.dot_general(
        joined_grad, joined_full, NT, preferred_element_type=jnp.float32
    ).astype(jnp.bfloat16)
    (both,) = spread([normed_part], [("tp",)], 7, "spread_normed")
    normed_one_grad = both[0].astype(jnp.float32) + both[1].astype(jnp.float32)
    x_norm_grad, gain_one_grad = norm_back(x, gain_rows[0], normed_one_grad)
    input_grad = (hidden_grad + x_norm_grad).astype(jnp.bfloat16)

    sums = jnp.concatenate(
        [
            joined_w_grad,
            output_grad,
            gain_one_grad[:, None],
            gain_two_grad[:, None],
            jnp.zeros((model_width, 126), jnp.float32),
        ],
        axis=1,
    ).astype(jnp.bfloat16)
    width = sums.shape[1]
    part = swap_sum(sums.reshape(dp_size, -1, width), ("dp",), 8, "sum_dp").astype(jnp.bfloat16)
    owned = swap_sum(part.reshape(ctx_size, -1, width), ("ctx",), 9, "sum_ctx")
    v_end = q_width + 2 * kv_width
    return (
        layer_out.astype(jnp.bfloat16)[None],
        input_grad[None],
        owned[:, :q_width],
        owned[:, q_width : q_width + kv_width],
        owned[:, q_width + kv_width : v_end],
        owned[:, v_end : v_end + q_width].T,
        owned[:, v_end + q_width],
        owned[:, v_end + q_width + 1],
        expert_grad.astype(jnp.float32),
    )


def solution(mesh):
    return jax.shard_map(
        body,
        mesh=mesh,
        in_specs=(
            P("dp", "ctx", None),
            P("dp", "tp"),
            P("dp", "tp"),
            P("dp", "tp"),
            P("tp", "dp"),
            P("dp"),
            P("dp"),
            P("dp", None, None, "tp"),
            P("dp", "ctx", None),
            P("dp", "ctx", None),
            P("dp", "ctx"),
            P("dp", None),
            P("dp", "ctx", None),
        ),
        out_specs=(
            P("dp", "ctx", None),
            P("dp", "ctx", None),
            P(("dp", "ctx"), "tp"),
            P(("dp", "ctx"), "tp"),
            P(("dp", "ctx"), "tp"),
            P("tp", ("dp", "ctx")),
            P(("dp", "ctx")),
            P(("dp", "ctx")),
            P("dp", None, "ctx", "tp"),
        ),
        check_vma=False,
    )
```

time: 1140 us -> 630 us (0.55)
  waiting for transfers between devices: 508 us -> 0.73 us
  Pallas kernels: 0 us -> 356 us
  matrix products: 302 us -> 153 us
  blocking collectives: 106 us -> 0 us
  other arithmetic: 90.7 us -> 41.2 us
  loops' own time: 30.9 us -> 0 us
  local copies, waits for them, and re-layouts: 83.9 us -> 55.9 us
    reduce_scatter x11 -> x1, waiting for transfers between devices: 382 us -> 0.01 us  [body(): lax.psum_scatter(weight_part, 'ctx', scatter_dimension=2, tiled=True)]
    pallas_call x0 -> x11, Pallas kernels: none -> 356 us  [the longest x2 86.3 us: swap_sum(): pl.pallas_call(functools.partial(swap_sum_kernel, tuple(axes)), name=name...]
    dot_general x51 -> x17, matrix products: 280 us -> 132 us  [the longest x3 36.1 us: back(): jnp.einsum('ecf,edf->ecd', slots, matrix, preferred_element_type=jnp.floa...]
    all_gather x5 -> x2, waiting for transfers between devices: 92.3 us -> 0.01 us  [the longest x1 0.01 us: body(): output_full = lax.all_gather(output_weight, 'dp', axis=1, tiled=True)]
    all_gather x7 -> x0, blocking collectives: 68.7 us -> none  [the longest x1 12.5 us: body(): lax.all_gather(documents.astype(jnp.bfloat16), 'ctx', axis=1, tiled=True)]
    dynamic_slice x32 -> x1, local copies, waits for them, and re-layouts: 32 us -> 0.08 us  [body(): lax.dynamic_slice_in_dim(pictures, offset, block_len)]
    psum x2 -> x0, waiting for transfers between devices: 31.8 us -> none  [sum_heads(): return lax.psum(partial_sum, 'tp')]
    another operation x4 -> x0, loops' own time: 30.9 us -> none  [the longest x1 8.04 us: body(): lax.scan(delta_step, jnp.zeros(stat_shape, jnp.float32), starts)[0]]
  transfers between devices with their start and end apart: 19 -> 3, of which waited for: 15 -> 0; matrix products, arithmetic and copies ran while one was open for 27% -> 25% of each run, Pallas kernels for 0% -> 52%
where the time goes in v2:
time: 630 us; the launch traced here: 622 us
  Pallas kernels  356 us (57%)
  matrix products  153 us (24%)
  local copies, waits for them, and re-layouts  55.9 us (9%)
  other arithmetic  41.2 us (7%)
  between operations  14.8 us (2%)
    pallas_call x2, Pallas kernels, swap_sum(): pl.pallas_call(functools.partial(swap_sum_kernel, tuple(axes)), name=name...  86.3 us
    pallas_call x1, Pallas kernels, window_sum(): pl.pallas_call(functools.partial(window_sum_kernel, back, ahead), name='w...  75.5 us
    pallas_call x2, Pallas kernels, return_rows(): pl.pallas_call(return_rows_kernel, name=name, in_specs=whole_vmem(1), out...  67.9 us
    pallas_call x1, Pallas kernels, share_rows(): pl.pallas_call(share_rows_kernel, name='share_rows', in_specs=whole_vmem(...  51 us
    pallas_call x2, Pallas kernels, spread(): pl.pallas_call(functools.partial(spread_kernel, tuple(axes_of)), name=nam...  39.8 us
    dot_general x3, matrix products, back(): jnp.einsum('ecf,edf->ecd', slots, matrix, preferred_element_type=jnp.floa...  36.1 us
    dot_general x3, matrix products, outer(): jnp.einsum('ecd,ecf->edf', left, right, preferred_element_type=jnp.float32)  31 us
    dot_general x3, matrix products, into(): jnp.einsum('ecd,edf->ecf', slots, matrix, preferred_element_type=jnp.floa...  30.2 us
  transfers between devices with their start and end apart: 3, of which 0 were waited for; matrix products, arithmetic and copies ran while one was open for 25% of the time, Pallas kernels for 52%

profile of v2, /device:TPU:0, one launch (start us, length us, event | category | flops | bytes accessed | tf_op | source)
XLA Modules:
  0.0 622.2 jit_solution(9493101834903258831)
XLA Ops:
  12.4 1.9 pad_maximum_fusion.7.refs_0_
  14.4 34.6 %spread_weights.1 = (bf16[4,256,1024]{2,1,0:T(8,128)(2,1)}, f32[4,2,256]{2,1,0:T(2,128)}, s32[4,1,512]{2,1,0:T(1,128)}, s32[4,32,128]{2,1,0:T(8,128)}, f32[4,32,128]{2,1,0:T(8,128)}) custom-call(bf16[256,1024]{1,0:T(8,128)(2,1)} %pad_maximum_fusion.7.refs_0_, f32[2,256]{1,0:T(2,128)} %maximum_convert_fusion.refs_1_, s32[1,512]{1,0:T(1,128)} %refs_2_.1, ...), custom_call_target="tpu_custom_call" | custom-call | tf_op jit(solution)/shard_map/spread_weights/pallas_call | solution.py:283
  49.8 1.4 fusion.74
  51.5 2.9 fusion.47
  57.4 12.9 %window.1 = bf16[4,512,512]{2,1,0:T(8,128)(2,1)} custom-call(bf16[512,512]{1,0:T(8,128)(2,1)} %pad_maximum_fusion.8.kv_ref), custom_call_target="tpu_custom_call" | custom-call | tf_op jit(solution)/shard_map/window/pallas_call | solution.py:615
  80.2 10.8 %attend.1 = (bf16[512,512]{1,0:T(8,128)(2,1)}, f32[512,512]{1,0:T(8,128)}, f32[8,512]{1,0:T(8,128)}, bf16[512,1024]{1,0:T(8,128)(2,1)}) custom-call(s32[9]{0:T(128)} %pad_add_fusion.2.flags, bf16[512,512]{1,0:T(8,128)(2,1)} %broadcast_multiply_fusion.q_ref, bf16[2048,512]{1,0:T(8,128)(2,1)} %bitcast.146, s32[2048,2]{1,0:T(8,128)} %copy.108.kinfo_ref, ...), custom_call_target="tpu_custom_call" | custom-call | tf_op jit(solution)/shard_map/attend/pallas_call | solution.py:148
  91.0 51.0 %share_rows.1 = (f32[512,1024]{1,0:T(8,128)}, bf16[4,512,1024]{2,1,0:T(8,128)(2,1)}) custom-call(bf16[512,1024]{1,0:T(8,128)(2,1)} %get-tuple-element.30.part_ref, bf16[512,1024]{1,0:T(8,128)(2,1)} %bitcast.148, f32[1,1024]{1,0:T(1,128)} %bitcast.166), custom_call_target="tpu_custom_call" | custom-call | tf_op jit(solution)/shard_map/share_rows/pallas_call | solution.py:418
  142.0 9.6 %convert_bitcast_fusion = bf16[8,4,144,1024]{3,2,0,1:T(8,128)(2,1)} fusion(s32[4,8,512]{2,1,0:T(8,128)S(1)} %fusion.64, bf16[4,512,1024]{2,1,0:T(8,128)(2,1)} %get-tuple-element.33), kind=kOutput, calls=%fused_computation.10 | convolution fusion | flops 4838916096 | bytes 13697024 | tf_op jit(solution)/shard_map/gesr,grd->egsd/dot_general | solution.py:777
  151.6 9.2 %copy.110 = bf16[8,4,144,1024]{3,2,1,0:T(8,128)(2,1)} copy(bf16[8,4,144,1024]{3,2,0,1:T(8,128)(2,1)} %convert_bitcast_fusion) | data formatting | bytes 18874368 | tf_op jit(solution)/shard_map/convert_element_type | solution.py:798
  160.8 9.8 %fusion.17 = f32[8,576,256]{2,1,0:T(8,128)} fusion(bf16[8,576,1024]{2,1,0:T(8,128)(2,1)} %bitcast.149, bf16[8,3,1024,256]{3,2,1,0:T(8,128)(2,1)} %param.20), kind=kOutput, calls=%fused_computation.30 | convolution fusion | flops 2415919104 | bytes 18350080 | tf_op jit(solution)/shard_map/ecd,edf->ecf/dot_general | solution.py:782
  170.5 6.5 %fusion.21 = f32[8,576,256]{2,1,0:T(8,128)} fusion(bf16[8,576,1024]{2,1,0:T(8,128)(2,1)S(1)} %bitcast.152, bf16[8,3,1024,256]{3,2,1,0:T(8,128)(2,1)} %param.20), kind=kOutput, calls=%fused_computation.34 | convolution fusion | flops 2415919104 | bytes 18350080 | tf_op jit(solution)/shard_map/ecd,edf->ecf/dot_general | solution.py:782
  177.0 11.2 %fusion.7 = f32[8,4,144,1024]{3,2,0,1:T(8,128)} fusion(bf16[4,512,1024,1]{2,1,3,0:T(8,128)(2,1)} %bitcast.178, s32[4,8,512]{2,1,0:T(8,128)S(1)} %fusion.64), kind=kOutput, calls=%fused_computation.16 | convolution fusion | flops 4834197504 | bytes 23134208 | tf_op jit(solution)/shard_map/gesr,grd->egsd/dot_general | solution.py:777
  188.2 7.8 %copy.117 = f32[8,4,144,1024]{3,2,1,0:T(8,128)S(1)} copy(f32[8,4,144,1024]{3,2,0,1:T(8,128)} %fusion.7) | data formatting | bytes 37748736 | tf_op jit(solution)/shard_map/gesr,grd->egsd/transpose | solution.py:777
  196.0 4.7 fusion
  200.8 14.0 %multiply_convert_fusion.1 = (bf16[8,576,256]{2,1,0:T(8,128)(2,1)}, bf16[8,576,256]{2,1,0:T(8,128)(2,1)S(1)}, bf16[8,576,256]{2,1,0:T(8,128)(2,1)}) fusion(f32[8,576,256]{2,1,0:T(8,128)} %fusion.21, f32[8,576,256]{2,1,0:T(8,128)} %fusion.17, bf16[8,576,1024]{2,1,0:T(8,128)(2,1)} %fusion, bf16[8,3,1024,256]{3,2,1,0:T(8,128)(2,1)} %param.20), kind=kOutput, calls=%fused_computation.17 | convolution fusion | flops 2433613824 | bytes 30146560 | tf_op jit(solution)/shard_map/ecd,edf->ecf/dot_general | solution.py:782
  214.8 11.1 %convert_bitcast_fusion.1 = bf16[8,1,1024,256]{3,2,0,1:T(8,128)(2,1)} fusion(bf16[8,576,1024]{2,1,0:T(8,128)(2,1)} %fusion, bf16[8,576,256]{2,1,0:T(8,128)(2,1)} %get-tuple-element.94), kind=kOutput, calls=%fused_computation.37 | convolution fusion | flops 2418016256 | bytes 15990784 | tf_op jit(solution)/shard_map/ecd,ecf->edf/dot_general | solution.py:788
  225.8 10.2 %convert_bitcast_fusion.2 = bf16[8,1,1024,256]{3,2,0,1:T(8,128)(2,1)} fusion(bf16[8,576,1024]{2,1,0:T(8,128)(2,1)} %bitcast.150, bf16[8,576,256]{2,1,0:T(8,128)(2,1)} %get-tuple-element.92), kind=kOutput, calls=%fused_computation.38 | convolution fusion | flops 2418016256 | bytes 15990784 | tf_op jit(solution)/shard_map/ecd,ecf->edf/dot_general | solution.py:788
  236.1 9.7 %convert_bitcast_fusion.3 = bf16[8,1,1024,256]{3,2,0,1:T(8,128)(2,1)} fusion(bf16[8,576,1024]{2,1,0:T(8,128)(2,1)} %bitcast.151, bf16[8,576,256]{2,1,0:T(8,128)(2,1)S(1)} %get-tuple-element.93), kind=kOutput, calls=%fused_computation.39 | convolution fusion | flops 2418016256 | bytes 15990784 | tf_op jit(solution)/shard_map/ecd,ecf->edf/dot_general | solution.py:788
  245.8 10.5 %pad_maximum_fusion = bf16[8,3,1024,256]{3,2,0,1:T(8,128)(2,1)} fusion(bf16[8,1,1024,256]{3,2,0,1:T(8,128)(2,1)} %convert_bitcast_fusion.1, bf16[8,1,1024,256]{3,2,0,1:T(8,128)(2,1)} %convert_bitcast_fusion.2, bf16[8,1,1024,256]{3,2,0,1:T(8,128)(2,1)} %convert_bitcast_fusion.3), kind=kLoop, calls=%fused_computation.4 | loop fusion | flops 12582912 | bytes 25165824 | tf_op jit(solution)/shard_map/stack | solution.py:808
  256.3 1.6 copy-done
  258.1 12.0 %fusion.19 = f32[8,576,1024]{2,1,0:T(8,128)} fusion(bf16[8,576,256]{2,1,0:T(8,128)(2,1)} %copy-done.7, bf16[8,3,1024,256]{3,2,1,0:T(8,128)(2,1)} %param.20), kind=kOutput, calls=%fused_computation.32 | convolution fusion | flops 2415919104 | bytes 25427968 | tf_op jit(solution)/shard_map/ecf,edf->ecd/dot_general | solution.py:785
  270.1 14.8 %add_convert_fusion = bf16[8,576,1024]{2,1,0:T(8,128)(2,1)} fusion(f32[8,576,1024]{2,1,0:T(8,128)} %fusion.19, bf16[8,576,256]{2,1,0:T(8,128)(2,1)} %get-tuple-element.92, bf16[8,3,1024,256]{3,2,1,0:T(8,128)(2,1)} %param.20), kind=kOutput, calls=%fused_computation.2 | convolution fusion | flops 2425356288 | bytes 34865152 | tf_op jit(solution)/shard_map/ecf,edf->ecd/dot_general | solution.py:785
  285.0 11.0 %bitcast_convert_fusion.part_ref = bf16[4,512,1024]{2,1,0:T(8,128)(2,1)} fusion(bf16[8,4,144,1024]{3,2,1,0:T(8,128)(2,1)} %bitcast.153, s32[4,8,512]{2,1,0:T(8,128)S(1)} %fusion.64), kind=kOutput, calls=%fused_computation.14 | convolution fusion | flops 4836294656 | bytes 13697024 | tf_op jit(solution)/shard_map/gesr,egsd->grd/dot_general | solution.py:791
  295.9 33.9 %return_grads.1 = f32[512,1024]{1,0:T(8,128)} custom-call(bf16[4,512,1024]{2,1,0:T(8,128)(2,1)} %bitcast_convert_fusion.part_ref), custom_call_target="tpu_custom_call" | custom-call | tf_op jit(solution)/shard_map/return_grads/pallas_call | solution.py:507
  329.9 9.2 %multiply_convert_fusion = bf16[8,576,1024]{2,1,0:T(8,128)(2,1)} fusion(f32[8,576]{1,0:T(8,128)S(1)} %mul.287, bf16[8,576,256]{2,1,0:T(8,128)(2,1)} %get-tuple-element.94, bf16[8,3,1024,256]{3,2,1,0:T(8,128)(2,1)} %param.20), kind=kOutput, calls=%fused_computation.3 | convolution fusion | flops 2425356288 | bytes 16009216 | tf_op jit(solution)/shard_map/ecf,edf->ecd/dot_general | solution.py:785
  339.1 10.9 %bitcast_convert_fusion.1.part_ref = bf16[4,512,1024]{2,1,0:T(8,128)(2,1)} fusion(bf16[8,4,144,1024]{3,2,1,0:T(8,128)(2,1)} %bitcast.181, s32[4,8,512]{2,1,0:T(8,128)S(1)} %fusion.64), kind=kOutput, calls=%fused_computation.15 | convolution fusion | flops 4836294656 | bytes 13697024 | tf_op jit(solution)/shard_map/gesr,egsd->grd/dot_general | solution.py:791
  349.9 34.0 %return_rows.1 = f32[512,1024]{1,0:T(8,128)} custom-call(bf16[4,512,1024]{2,1,0:T(8,128)(2,1)} %bitcast_convert_fusion.1.part_ref), custom_call_target="tpu_custom_call" | custom-call | tf_op jit(solution)/shard_map/return_rows/pallas_call | solution.py:507
  383.9 2.3 multiply_reduce_fusion
  386.8 3.4 multiply_add_fusion
  390.2 1.6 convolution_convert_fusion.3.grad_ref
  391.8 11.8 %attend_back.1 = (f32[512,512]{1,0:T(8,128)}, bf16[2048,512]{1,0:T(8,128)(2,1)}) custom-call(s32[9]{0:T(128)} %pad_add_fusion.2.flags, bf16[512,512]{1,0:T(8,128)(2,1)} %broadcast_multiply_fusion.q_ref, bf16[2048,512]{1,0:T(8,128)(2,1)} %bitcast.147, s32[2048,2]{1,0:T(8,128)} %copy.108.kinfo_ref, s32[2,512]{1,0:T(2,128)} %pad_add_fusion.1.qinfo_ref, ...), custom_call_target="tpu_custom_call" | custom-call | tf_op jit(solution)/shard_map/attend_back/pallas_call | solution.py:170
  403.6 75.5 %window_sum.1 = f32[512,512]{1,0:T(8,128)} custom-call(bf16[4,512,512]{2,1,0:T(8,128)(2,1)} %bitcast.162), custom_call_target="tpu_custom_call" | custom-call | tf_op jit(solution)/shard_map/window_sum/pallas_call | solution.py:694
  482.6 3.0 copy.120
  485.6 1.6 subtract_convert_fusion
  488.5 4.2 convolution_convert_fusion.1.refs_0_
  492.7 5.2 spread_normed.1
  497.9 2.5 fusion.44
  500.5 2.2 fusion.50
  502.6 1.5 copy.130
  505.7 3.8 convolution_convert_fusion
  510.3 6.1 concatenate.35.x_ref
  516.4 49.2 %sum_dp.1 = f32[256,1664]{1,0:T(8,128)} custom-call(bf16[4,256,1664]{2,1,0:T(8,128)(2,1)} %concatenate.35.x_ref), custom_call_target="tpu_custom_call" | custom-call | tf_op jit(solution)/shard_map/sum_dp/pallas_call | solution.py:329
  565.7 2.4 convert_element_type.136
  568.1 37.0 %sum_ctx.1 = f32[64,1664]{1,0:T(8,128)} custom-call(bf16[4,64,1664]{2,1,0:T(8,128)(2,1)} %bitcast.158), custom_call_target="tpu_custom_call" | custom-call | tf_op jit(solution)/shard_map/sum_ctx/pallas_call | solution.py:329
  605.2 1.5 slice_reduce_fusion
  606.7 1.5 fusion.73
  608.2 1.7 slice_bitcast_fusion
  609.9 5.4 copy.125
  (127 shorter events, 26.8 us)
Async XLA Ops:
  7.2 44.0 %copy-start.4 = (bf16[1,512,1024]{2,1,0:T(8,128)(2,1)S(1)}, bf16[1,512,1024]{2,1,0:T(8,128)(2,1)}, u32[]{:S(2)}) copy-start(bf16[1,512,1024]{2,1,0:T(8,128)(2,1)} %param.13) | copy-start | bytes 3145732
  7.2 73.0 %all-gather.4.cloned.1.call-start = ((), (), s32[]{:S(2)}) async-start(), calls=%async_computation.1 | async-start | bytes 1310720 | tf_op jit(solution)/shard_map/all_gather | solution.py:854
  49.0 128.0 %all-gather.6.cloned.1.call-start = ((), (), s32[]{:S(2)}) async-start(), calls=%async_computation.3 | async-start | bytes 5242880 | tf_op jit(solution)/shard_map/all_gather | solution.py:855
  49.8 560.2 %reduce-scatter.2.cloned.1.call-start = ((), (), s32[]{:S(2)}) async-start(), calls=%async_computation.2 | async-start | bytes 15728640 | tf_op jit(solution)/shard_map/reduce_scatter | solution.py:884
  51.2 3.3 copy-start.19
  51.5 3.0 copy-start.22
  56.0 14.3 %copy-start.11 = (f32[512,32]{0,1:T(8,128)}, f32[512,32]{0,1:T(8,128)S(1)}, u32[]{:S(2)}) copy-start(f32[512,32]{0,1:T(8,128)S(1)} %get-tuple-element.113) | copy-start | bytes 196612
  56.3 14.3 %copy-start.25 = (s32[1,4]{1,0:T(1,128)S(1)}, s32[1,4]{1,0:T(1,128)}, u32[]{:S(2)}) copy-start(s32[1,4]{1,0:T(1,128)} %param.24) | copy-start | bytes 52
  56.3 14.3 %copy-start.21 = (s32[4,1,512]{2,1,0:T(1,128)S(1)}, s32[4,1,512]{2,1,0:T(1,128)}, u32[]{:S(2)}) copy-start(s32[4,1,512]{2,1,0:T(1,128)} %get-tuple-element.25) | copy-start | bytes 24580
  56.4 16.1 %copy-start.17 = (s32[4,32,128]{2,1,0:T(8,128)S(1)}, s32[4,32,128]{2,1,0:T(8,128)}, u32[]{:S(2)}) copy-start(s32[4,32,128]{2,1,0:T(8,128)} %get-tuple-element.32) | copy-start | bytes 196612
  56.6 16.7 %copy-start.16 = (f32[4,32,128]{2,1,0:T(8,128)S(1)}, f32[4,32,128]{2,1,0:T(8,128)}, u32[]{:S(2)}) copy-start(f32[4,32,128]{2,1,0:T(8,128)} %get-tuple-element.34) | copy-start | bytes 196612
  70.3 5.8 copy-start.24
  160.8 9.8 %copy-start.6 = (bf16[8,4,144,1024]{3,2,1,0:T(8,128)(2,1)S(1)}, bf16[8,4,144,1024]{3,2,1,0:T(8,128)(2,1)}, u32[]{:S(2)}) copy-start(bf16[8,4,144,1024]{3,2,1,0:T(8,128)(2,1)} %copy.110) | copy-start | bytes 28311556
  214.8 21.3 %copy-start.7 = (bf16[8,576,256]{2,1,0:T(8,128)(2,1)}, bf16[8,576,256]{2,1,0:T(8,128)(2,1)S(1)}, u32[]{:S(2)}) copy-start(bf16[8,576,256]{2,1,0:T(8,128)(2,1)S(1)} %get-tuple-element.93) | copy-start | bytes 7077892
  256.3 1.6 copy-start
  349.9 34.0 %copy-start.18 = (f32[1,4,256]{2,0,1:T(1,128)S(1)}, f32[1,4,256]{2,0,1:T(1,128)}, u32[]{:S(2)}) copy-start(f32[1,4,256]{2,0,1:T(1,128)} %get-tuple-element.107) | copy-start | bytes 12292
  349.9 36.3 %copy-start.8 = (bf16[1,512,1024]{2,1,0:T(8,128)(2,1)S(1)}, bf16[1,512,1024]{2,1,0:T(8,128)(2,1)}, u32[]{:S(2)}) copy-start(bf16[1,512,1024]{2,1,0:T(8,128)(2,1)} %param.25) | copy-start | bytes 3145732
  383.9 2.4 copy-start.1
  383.9 2.8 copy-start.2
  386.8 3.4 copy-start.9
  403.6 77.7 %copy-start.10 = (f32[512,512]{1,0:T(8,128)S(1)}, f32[512,512]{1,0:T(8,128)}, u32[]{:S(2)}) copy-start(f32[512,512]{1,0:T(8,128)} %get-tuple-element.38) | copy-start | bytes 3145732
  479.1 6.5 %copy-start.12 = (f32[512,32]{0,1:T(8,128)S(1)}, f32[512,32]{0,1:T(8,128)}, u32[]{:S(2)}) copy-start(f32[512,32]{0,1:T(8,128)} %copy-done.11) | copy-start | bytes 196612
  479.1 6.5 %copy-start.14 = (f32[512,32]{0,1:T(8,128)S(1)}, f32[512,32]{0,1:T(8,128)}, u32[]{:S(2)}) copy-start(f32[512,32]{0,1:T(8,128)} %get-tuple-element.111) | copy-start | bytes 196612
  481.3 7.1 %copy-start.15 = (bf16[512,256]{1,0:T(8,128)(2,1)}, bf16[512,256]{1,0:T(8,128)(2,1)S(1)}, u32[]{:S(2)}) copy-start(bf16[512,256]{1,0:T(8,128)(2,1)S(1)} %slice.175) | copy-start | bytes 786436
  488.5 9.4 %copy-start.5 = (bf16[1,512,1024]{2,1,0:T(8,128)(2,1)S(1)}, bf16[1,512,1024]{2,1,0:T(8,128)(2,1)}, u32[]{:S(2)}) copy-start(bf16[1,512,1024]{2,1,0:T(8,128)(2,1)} %param.13) | copy-start | bytes 3145732
  488.5 9.4 %copy-start.20 = (f32[1,4,256]{2,0,1:T(1,128)S(1)}, f32[1,4,256]{2,0,1:T(1,128)}, u32[]{:S(2)}) copy-start(f32[1,4,256]{2,0,1:T(1,128)} %copy-done.19) | copy-start | bytes 12292
  488.5 9.4 %copy-start.23 = (f32[512]{0:T(512)S(1)}, f32[512]{0:T(512)}, u32[]{:S(2)}) copy-start(f32[512]{0:T(512)} %copy-done.22) | copy-start | bytes 6148
  497.9 2.5 copy-start.3
  505.7 3.8 copy-start.13
Sparse Core Ops, SparseCore 0:
  49.1 24.6 all-gather.3
  75.6 68.4 all-gather.5
  256.4 246.0 reduce-scatter.1

commit v3 on v2

--- a/solution.py
+++ b/solution.py
@@ -709,6 +709,149 @@
     )(grad)
 
 
+GROUPS_AT_ONCE = 4
+
+
+def experts_kernel(
+    rows_ref, grads_ref, weights_ref, place_ref, gate_ref, place_col_ref, out_ref, back_ref,
+    weight_grad_ref, slots, slot_grads, outs, backs,
+):
+    e = pl.program_id(1)
+    groups, tok_rows, model_width = rows_ref.shape
+    owners, part = weight_grad_ref.shape[1], weight_grad_ref.shape[5]
+    slot_index = lax.broadcasted_iota(jnp.int32, (CAP, tok_rows), 0)
+    gates = []
+    for g in range(groups):
+        picks = slot_index == place_ref[g, 0]
+        gates.append(jnp.sum(jnp.where(picks, gate_ref[g, 0], 0.0), axis=1, keepdims=True))
+        picks = picks.astype(jnp.float32).astype(jnp.bfloat16)
+        at = slice(g * CAP, (g + 1) * CAP)
+        slots[at, :] = jnp.dot(
+            picks, rows_ref[g], preferred_element_type=jnp.float32
+        ).astype(jnp.bfloat16)
+        slot_grads[at, :] = (
+            jnp.dot(picks, grads_ref[g], preferred_element_type=jnp.float32) * gates[g]
+        ).astype(jnp.bfloat16)
+    gate_w, up_w, down_w = (weights_ref.at[0, i] for i in range(3))
+    gate_pre = jnp.dot(slots[...], gate_w[...], preferred_element_type=jnp.float32)
+    up_pre = jnp.dot(slots[...], up_w[...], preferred_element_type=jnp.float32)
+    act_grad = jnp.dot(slot_grads[...], down_w[...], preferred_element_type=jnp.float32)
+    sig = 1.0 / (1.0 + jnp.exp(-gate_pre))
+    silu = gate_pre * sig
+    act_low = (silu * up_pre).astype(jnp.bfloat16)
+    up_low = (act_grad * silu).astype(jnp.bfloat16)
+    gate_low = (act_grad * up_pre * (sig * (1.0 + gate_pre * (1.0 - sig)))).astype(jnp.bfloat16)
+
+    back = lax.dot_general(
+        gate_low, gate_w[...], NT, preferred_element_type=jnp.float32
+    ) + lax.dot_general(up_low, up_w[...], NT, preferred_element_type=jnp.float32)
+    out = lax.dot_general(act_low, down_w[...], NT, preferred_element_type=jnp.float32)
+    for g in range(groups):
+        at = slice(g * CAP, (g + 1) * CAP)
+        to = pl.ds(pl.multiple_of(e * CAP, CAP), CAP)
+        backs[g, to, :] = back[at].astype(jnp.bfloat16)
+        outs[g, to, :] = (out[at] * gates[g]).astype(jnp.bfloat16)
+
+    for i, (low, source) in enumerate(
+        ((gate_low, slots), (up_low, slots), (act_low, slot_grads))
+    ):
+        turned = jnp.transpose(low.astype(jnp.float32)).astype(jnp.bfloat16)
+        total = jnp.dot(turned, source[...], preferred_element_type=jnp.float32)
+        for c in range(owners):
+            weight_grad_ref[0, c, 0, i] = total[:, c * part : (c + 1) * part].astype(
+                weight_grad_ref.dtype
+            )
+
+    @pl.when(e == pl.num_programs(1) - 1)
+    def _():
+        slot_count = outs.shape[1]
+        for g in range(groups):
+            tiles = []
+            for first in range(0, slot_count, 128):
+                wide = min(128, slot_count - first)
+                lane = first + lax.broadcasted_iota(jnp.int32, (tok_rows, wide), 1)
+                hit = None
+                for n in range(first // CAP, (first + wide - 1) // CAP + 1):
+                    one = place_col_ref[g, :, n : n + 1] == lane - n * CAP
+                    hit = one if hit is None else hit | one
+                tiles.append(hit.astype(jnp.float32).astype(jnp.bfloat16))
+            spread_picks = jnp.concatenate(tiles, axis=1)
+            back_ref[g] = jnp.dot(
+                spread_picks, backs[g], preferred_element_type=jnp.float32
+            ).astype(jnp.bfloat16)
+            out_ref[g] = jnp.dot(
+                spread_picks, outs[g], preferred_element_type=jnp.float32
+            ).astype(jnp.bfloat16)
+
+
+def experts(weights, chosen_all, gates_all, rows_all, grad_all):
+    own, _, model_width, hidden = weights.shape
+    groups, tok_rows, _ = rows_all.shape
+    owners = lax.axis_size("ctx")
+    named = chosen_all[..., None] == lax.axis_index("dp") * own + jnp.arange(own, dtype=jnp.int32)
+    names = jnp.any(named, axis=2)
+    gate_of = jnp.sum(jnp.where(named, gates_all[..., None], 0.0), axis=2)
+    earlier = jnp.tril(jnp.ones((tok_rows, tok_rows), jnp.bfloat16), -1)
+    place = jnp.einsum(
+        "rq,gqe->gre", earlier, names.astype(jnp.bfloat16), preferred_element_type=jnp.float32
+    ).astype(jnp.int32)
+    place = jnp.where(names & (place < CAP), place, -CAP * own)
+    at_once = min(GROUPS_AT_ONCE, groups)
+    chunks = groups // at_once
+    part = model_width // owners
+    rows_spec = pl.BlockSpec(
+        (at_once, tok_rows, model_width), lambda c, e: (c, 0, 0), pipeline_mode=pl.Buffered(1)
+    )
+    line_spec = pl.BlockSpec((at_once, 1, 1, tok_rows), lambda c, e: (c, e, 0, 0))
+    out_shape = jax.ShapeDtypeStruct(rows_all.shape, jnp.bfloat16)
+    flops = own * groups * CAP * model_width * 2 * (9 * hidden + 4 * tok_rows)
+    out_part, back_part, weight_part = pl.pallas_call(
+        experts_kernel,
+        name="experts",
+        grid=(chunks, own),
+        in_specs=[
+            rows_spec,
+            rows_spec,
+            pl.BlockSpec((1, 3, model_width, hidden), lambda c, e: (e, 0, 0, 0)),
+            line_spec,
+            line_spec,
+            pl.BlockSpec((at_once, tok_rows, own), lambda c, e: (c, 0, 0)),
+        ],
+        out_specs=[
+            rows_spec,
+            rows_spec,
+            pl.BlockSpec((1, owners, 1, 3, hidden, part), lambda c, e: (c, 0, e, 0, 0, 0)),
+        ],
+        out_shape=[
+            out_shape,
+            out_shape,
+            jax.ShapeDtypeStruct((chunks, owners, own, 3, hidden, part), jnp.bfloat16),
+        ],
+        scratch_shapes=[
+            pltpu.VMEM((at_once * CAP, model_width), jnp.bfloat16),
+            pltpu.VMEM((at_once * CAP, model_width), jnp.bfloat16),
+            pltpu.VMEM((at_once, own * CAP, model_width), jnp.bfloat16),
+            pltpu.VMEM((at_once, own * CAP, model_width), jnp.bfloat16),
+        ],
+        compiler_params=pltpu.CompilerParams(vmem_limit_bytes=LIMIT),
+        cost_estimate=pl.CostEstimate(
+            flops=flops, bytes_accessed=4 * weights.size, transcendentals=0
+        ),
+    )(
+        rows_all,
+        grad_all,
+        weights,
+        place.transpose(0, 2, 1)[:, :, None],
+        gate_of.transpose(0, 2, 1)[:, :, None],
+        place,
+    )
+    if chunks == 1:
+        return out_part, back_part, weight_part[0]
+    return out_part, back_part, jnp.sum(weight_part.astype(jnp.float32), axis=0).astype(
+        jnp.bfloat16
+    )
+
+
 def rms_norm(tensor, gain_vec):
     return (
         tensor * lax.rsqrt(jnp.mean(tensor * tensor, axis=-1, keepdims=True) + EPSILON) * gain_vec
@@ -749,66 +892,6 @@
     )
     labels = jnp.arange(starts.shape[0], dtype=jnp.int32) + 1
     return jnp.sum(jnp.where(inside, labels[None, :], 0), axis=-1) - 1
-
-
-def silu_parts(gate_pre):
-    sig = jax.nn.sigmoid(gate_pre)
-    return gate_pre * sig, sig * (1.0 + gate_pre * (1.0 - sig))
-
-
-def experts(weights, chosen_all, gates_all, rows_all, grad_all):
-    own, _, model_width, _ = weights.shape
-    groups, tok_rows, _ = rows_all.shape
-    first_own = lax.axis_index("dp") * own
-    named = chosen_all[..., None] == first_own + jnp.arange(own, dtype=jnp.int32)
-    names = jnp.any(named, axis=2)
-    gate_of = jnp.sum(jnp.where(named, gates_all[..., None], 0.0), axis=2)
-    earlier = jnp.tril(jnp.ones((tok_rows, tok_rows), jnp.bfloat16), -1)
-    place = jnp.einsum(
-        "rq,gqe->gre", earlier, names.astype(jnp.bfloat16), preferred_element_type=jnp.float32
-    ).astype(jnp.int32)
-    place = jnp.where(names & (place < CAP), place, -1)
-    picks = place.transpose(0, 2, 1)[:, :, None, :] == jnp.arange(CAP, dtype=jnp.int32)[:, None]
-    slot_gate = jnp.sum(jnp.where(picks, gate_of.transpose(0, 2, 1)[:, :, None, :], 0.0), axis=-1)
-    picks = picks.astype(jnp.bfloat16)
-    gate_col = slot_gate.transpose(1, 0, 2).reshape(own, groups * CAP, 1)
-
-    def take(source):
-        return jnp.einsum(
-            "gesr,grd->egsd", picks, source, preferred_element_type=jnp.float32
-        ).reshape(own, groups * CAP, model_width)
-
-    def into(slots, matrix):
-        return jnp.einsum("ecd,edf->ecf", slots, matrix, preferred_element_type=jnp.float32)
-
-    def back(slots, matrix):
-        return jnp.einsum("ecf,edf->ecd", slots, matrix, preferred_element_type=jnp.float32)
-
-    def outer(left, right):
-        return jnp.einsum("ecd,ecf->edf", left, right, preferred_element_type=jnp.float32)
-
-    def combine(slots):
-        return jnp.einsum(
-            "gesr,egsd->grd",
-            picks,
-            slots.astype(jnp.bfloat16).reshape(own, groups, CAP, model_width),
-            preferred_element_type=jnp.float32,
-        ).astype(jnp.bfloat16)
-
-    slot_rows = take(rows_all).astype(jnp.bfloat16)
-    slot_grads = (take(grad_all) * gate_col).astype(jnp.bfloat16)
-    gate_pre, up_pre = into(slot_rows, weights[:, 0]), into(slot_rows, weights[:, 1])
-    silu, slope = silu_parts(gate_pre)
-    act_grad = into(slot_grads, weights[:, 2])
-    gate_low = (act_grad * up_pre * slope).astype(jnp.bfloat16)
-    up_low = (act_grad * silu).astype(jnp.bfloat16)
-    act_low = (silu * up_pre).astype(jnp.bfloat16)
-    back_part = combine(back(gate_low, weights[:, 0]) + back(up_low, weights[:, 1]))
-    out_part = combine(back(act_low, weights[:, 2]) * gate_col)
-    weight_part = jnp.stack(
-        [outer(slot_rows, gate_low), outer(slot_rows, up_low), outer(slot_grads, act_low)], axis=1
-    ).astype(jnp.bfloat16)
-    return out_part, back_part, weight_part
 
 
 def body(
@@ -881,7 +964,7 @@
     out_part, back_part, weight_part = experts(
         expert_weights, chosen_all, gates_all, rows_all, grad_all
     )
-    expert_grad = lax.psum_scatter(weight_part, "ctx", scatter_dimension=2, tiled=True)
+    expert_grad = lax.psum_scatter(weight_part, "ctx", scatter_dimension=0)
     normed_two_grad = return_rows(back_part, 4, "return_grads")
     layer_out = hidden + return_rows(out_part, 5, "return_rows")
 
@@ -934,7 +1017,7 @@
         owned[:, v_end : v_end + q_width].T,
         owned[:, v_end + q_width],
         owned[:, v_end + q_width + 1],
-        expert_grad.astype(jnp.float32),
+        expert_grad.astype(jnp.float32).transpose(0, 1, 3, 2),
     )
 
 

time: 630 us -> 533 us (0.85)
  matrix products: 153 us -> 13.1 us
  Pallas kernels: 356 us -> 424 us
  local copies, waits for them, and re-layouts: 55.9 us -> 41.5 us
  other arithmetic: 41.2 us -> 29.7 us
    dot_general x13 -> x0, matrix products: 140 us -> none  [the longest x3 36.1 us: back(): jnp.einsum('ecf,edf->ecd', slots, matrix, preferred_element_type=jnp.floa...]
    pallas_call x0 -> x1, Pallas kernels: none -> 69.1 us  [experts(): pl.pallas_call(experts_kernel, name='experts', grid=(chunks, own), in_spe...]
    pallas_call x1, Pallas kernels: 75.5 us -> 95.7 us  [window_sum(): pl.pallas_call(functools.partial(window_sum_kernel, back, ahead), name='w...]
    pallas_call x2, Pallas kernels: 86.3 us -> 66.4 us  [swap_sum(): pl.pallas_call(functools.partial(swap_sum_kernel, tuple(axes)), name=name...]
    another operation x3 -> x2, other arithmetic: 12.3 us -> 1.86 us  [the longest x1 10.5 us: experts(): jnp.stack([outer(slot_rows, gate_low), outer(slot_rows, up_low), outer(sl...]
    convert_element_type x1 -> x0, local copies, waits for them, and re-layouts: 9.2 us -> none  [experts(): slot_rows = take(rows_all).astype(jnp.bfloat16)]
    transpose x2 -> x0, local copies, waits for them, and re-layouts: 7.83 us -> none  [the longest x1 7.82 us: take(): jnp.einsum('gesr,grd->egsd', picks, source, preferred_element_type=jnp.fl...]
  transfers between devices with their start and end apart: 3 -> 3, of which waited for: 0 -> 1; matrix products, arithmetic and copies ran while one was open for 25% -> 12% of each run, Pallas kernels for 52% -> 61%
where the time goes in v3:
time: 533 us; the launch traced here: 527 us
  Pallas kernels  424 us (80%)
  local copies, waits for them, and re-layouts  41.5 us (8%)
  other arithmetic  29.7 us (6%)
  between operations  14.5 us (3%)
  matrix products  13.1 us (2%)
    pallas_call x1, Pallas kernels, window_sum(): pl.pallas_call(functools.partial(window_sum_kernel, back, ahead), name='w...  95.7 us
    pallas_call x1, Pallas kernels, experts(): pl.pallas_call(experts_kernel, name='experts', grid=(chunks, own), in_spe...  69.1 us
    pallas_call x2, Pallas kernels, return_rows(): pl.pallas_call(return_rows_kernel, name=name, in_specs=whole_vmem(1), out...  67.8 us
    pallas_call x2, Pallas kernels, swap_sum(): pl.pallas_call(functools.partial(swap_sum_kernel, tuple(axes)), name=name...  66.4 us
    pallas_call x1, Pallas kernels, share_rows(): pl.pallas_call(share_rows_kernel, name='share_rows', in_specs=whole_vmem(...  50 us
    pallas_call x2, Pallas kernels, spread(): pl.pallas_call(functools.partial(spread_kernel, tuple(axes_of)), name=nam...  39.9 us
    pallas_call x1, Pallas kernels, window(): pl.pallas_call(functools.partial(window_kernel, back, ahead), name='windo...  12.9 us
    pallas_call x1, Pallas kernels, attend_back(): pl.pallas_call(attend_back_kernel, name='attend_back', in_specs=[pl.Block...  12 us
  transfers between devices with their start and end apart: 3, of which 1 were waited for; matrix products, arithmetic and copies ran while one was open for 12% of the time, Pallas kernels for 61%

profile of v3, /device:TPU:0, one launch (start us, length us, event | category | flops | bytes accessed | tf_op | source)
XLA Modules:
  0.0 527.3 jit_solution(5196966689470943542)
XLA Ops:
  7.2 0.9 copy.67
  8.2 0.8 reshape.228.refs_3_
  8.9 0.8 copy.68
  9.8 0.8 reshape.229.refs_4_
  12.4 1.9 pad_maximum_fusion.6.refs_0_
  14.4 34.6 %spread_weights.1 = (bf16[4,256,1024]{2,1,0:T(8,128)(2,1)}, f32[4,2,256]{2,1,0:T(2,128)}, s32[4,1,512]{2,1,0:T(1,128)}, s32[4,32,128]{2,1,0:T(8,128)}, f32[4,32,128]{2,1,0:T(8,128)}) custom-call(bf16[256,1024]{1,0:T(8,128)(2,1)} %pad_maximum_fusion.6.refs_0_, f32[2,256]{1,0:T(2,128)} %maximum_convert_fusion.refs_1_, s32[1,512]{1,0:T(1,128)} %refs_2_.1, ...), custom_call_target="tpu_custom_call" | custom-call | tf_op jit(solution)/shard_map/spread_weights/pallas_call | solution.py:283
  50.8 1.3 fusion.13
  53.6 0.8 pad_maximum_fusion.7.kv_ref
  54.5 12.9 %window.1 = bf16[4,512,512]{2,1,0:T(8,128)(2,1)} custom-call(bf16[512,512]{1,0:T(8,128)(2,1)} %pad_maximum_fusion.7.kv_ref), custom_call_target="tpu_custom_call" | custom-call | tf_op jit(solution)/shard_map/window/pallas_call | solution.py:615
  68.1 1.3 copy.74.kinfo_ref
  71.0 1.6 bitcast_select_fusion
  72.8 0.9 copy.80.place_ref
  76.1 1.3 fusion.32
  78.6 0.8 broadcast_multiply_fusion.q_ref
  79.4 10.4 %attend.1 = (bf16[512,512]{1,0:T(8,128)(2,1)}, f32[512,512]{1,0:T(8,128)}, f32[8,512]{1,0:T(8,128)}, bf16[512,1024]{1,0:T(8,128)(2,1)}) custom-call(s32[9]{0:T(128)} %pad_add_fusion.2.flags, bf16[512,512]{1,0:T(8,128)(2,1)} %broadcast_multiply_fusion.q_ref, bf16[2048,512]{1,0:T(8,128)(2,1)} %bitcast.92, s32[2048,2]{1,0:T(8,128)} %copy.74.kinfo_ref, ...), custom_call_target="tpu_custom_call" | custom-call | tf_op jit(solution)/shard_map/attend/pallas_call | solution.py:148
  89.8 50.0 %share_rows.1 = (f32[512,1024]{1,0:T(8,128)}, bf16[4,512,1024]{2,1,0:T(8,128)(2,1)}) custom-call(bf16[512,1024]{1,0:T(8,128)(2,1)} %get-tuple-element.33.part_ref, bf16[512,1024]{1,0:T(8,128)(2,1)} %bitcast.94, f32[1,1024]{1,0:T(1,128)} %bitcast.107), custom_call_target="tpu_custom_call" | custom-call | tf_op jit(solution)/shard_map/share_rows/pallas_call | solution.py:418
  139.9 3.3 all-gather.6.cloned.1.call-done
  143.2 69.1 %experts.1 = (bf16[4,512,1024]{2,1,0:T(8,128)(2,1)}, bf16[4,512,1024]{2,1,0:T(8,128)(2,1)}, bf16[1,4,8,3,256,256]{5,4,3,2,1,0:T(8,128)(2,1)}) custom-call(bf16[4,512,1024]{2,1,0:T(8,128)(2,1)} %get-tuple-element.35.rows_ref, bf16[4,512,1024]{2,1,0:T(8,128)(2,1)} %bitcast.119, bf16[8,3,1024,256]{3,2,1,0:T(8,128)(2,1)} %weights_ref.1, ...), custom_call_target="tpu_custom_call" | custom-call | flops 41070624768 | bytes 25165824 | tf_op jit(solution)/shard_map/experts/pallas_call | solution.py:808
  212.3 1.6 copy-done
  214.1 33.8 %return_grads.1 = f32[512,1024]{1,0:T(8,128)} custom-call(bf16[4,512,1024]{2,1,0:T(8,128)(2,1)} %get-tuple-element.40.part_ref), custom_call_target="tpu_custom_call" | custom-call | tf_op jit(solution)/shard_map/return_grads/pallas_call | solution.py:507
  247.9 34.0 %return_rows.1 = f32[512,1024]{1,0:T(8,128)} custom-call(bf16[4,512,1024]{2,1,0:T(8,128)(2,1)} %get-tuple-element.39.part_ref), custom_call_target="tpu_custom_call" | custom-call | tf_op jit(solution)/shard_map/return_rows/pallas_call | solution.py:507
  282.0 2.3 multiply_reduce_fusion
  284.8 3.4 multiply_add_fusion
  288.3 1.6 convolution_convert_fusion.4.grad_ref
  289.8 12.0 %attend_back.1 = (f32[512,512]{1,0:T(8,128)}, bf16[2048,512]{1,0:T(8,128)(2,1)}) custom-call(s32[9]{0:T(128)} %pad_add_fusion.2.flags, bf16[512,512]{1,0:T(8,128)(2,1)} %broadcast_multiply_fusion.q_ref, bf16[2048,512]{1,0:T(8,128)(2,1)} %bitcast.93, s32[2048,2]{1,0:T(8,128)} %copy.74.kinfo_ref, s32[2,512]{1,0:T(2,128)} %pad_add_fusion.1.qinfo_ref, ...), custom_call_target="tpu_custom_call" | custom-call | tf_op jit(solution)/shard_map/attend_back/pallas_call | solution.py:170
  301.8 95.7 %window_sum.1 = f32[512,512]{1,0:T(8,128)} custom-call(bf16[4,512,512]{2,1,0:T(8,128)(2,1)} %bitcast.104), custom_call_target="tpu_custom_call" | custom-call | tf_op jit(solution)/shard_map/window_sum/pallas_call | solution.py:694
  397.6 1.1 slice.92
  398.7 1.1 slice.136
  399.8 1.2 pad_maximum_fusion
  401.0 3.0 copy.82
  404.0 1.6 subtract_convert_fusion
  405.7 1.2 copy.83
  406.9 4.1 convolution_convert_fusion.1.refs_0_
  411.0 5.3 %spread_normed.1 = bf16[2,512,1024]{2,1,0:T(8,128)(2,1)} custom-call(bf16[512,1024]{1,0:T(8,128)(2,1)} %convolution_convert_fusion.1.refs_0_), custom_call_target="tpu_custom_call" | custom-call | tf_op jit(solution)/shard_map/spread_normed/pallas_call | solution.py:283
  416.4 2.5 fusion.10
  418.9 2.2 fusion.16
  421.0 1.7 copy.89
  423.2 1.2 concatenate.37
  424.3 3.8 convolution_convert_fusion
  428.9 6.1 %concatenate.35.x_ref = bf16[4,256,1664]{2,1,0:T(8,128)(2,1)} concatenate(bf16[4,256,1024]{2,1,0:T(8,128)(2,1)} %convolution_convert_fusion, bf16[4,256,512]{2,1,0:T(8,128)(2,1)S(1)} %bitcast.98, bf16[4,256,1]{2,1,0:T(8,128)(2,1)S(1)} %concatenate.36, bf16[4,256,1]{2,1,0:T(8,128)(2,1)} %concatenate.37, bf16[4,256,126]{2,1,0:T(8,128)(2,1)S(1)} %broadcast_in_dim.88), dimensions={2} | concatenate | bytes 6815744 | tf_op jit(solution)/shard_map/concatenate | solution.py:997
  435.1 45.9 %sum_dp.1 = f32[256,1664]{1,0:T(8,128)} custom-call(bf16[4,256,1664]{2,1,0:T(8,128)(2,1)} %concatenate.35.x_ref), custom_call_target="tpu_custom_call" | custom-call | tf_op jit(solution)/shard_map/sum_dp/pallas_call | solution.py:329
  481.0 2.4 convert_element_type.95
  483.5 20.4 %sum_ctx.1 = f32[64,1664]{1,0:T(8,128)} custom-call(bf16[4,64,1664]{2,1,0:T(8,128)(2,1)} %bitcast.100), custom_call_target="tpu_custom_call" | custom-call | tf_op jit(solution)/shard_map/sum_ctx/pallas_call | solution.py:329
  503.9 1.5 slice_reduce_fusion
  505.4 1.5 fusion.37
  506.9 1.7 slice_bitcast_fusion
  508.6 5.3 %convert_bitcast_fusion = f32[8,3,256,256]{2,3,1,0:T(8,128)} fusion(bf16[1,8,3,256,256]{4,3,2,1,0:T(8,128)(2,1)} %reduce-scatter.2.cloned.1.call-done), kind=kLoop, calls=%fused_computation | loop fusion | flops 1572864 | bytes 9437184 | tf_op jit(solution)/shard_map/transpose | solution.py:1020
  513.9 6.6 %copy.87 = f32[8,3,256,256]{3,2,1,0:T(8,128)} copy(f32[8,3,256,256]{2,3,1,0:T(8,128)} %convert_bitcast_fusion) | data formatting | bytes 12582912
  (99 shorter events, 13.1 us)
Async XLA Ops:
  7.2 42.7 %copy-start.4 = (bf16[1,512,1024]{2,1,0:T(8,128)(2,1)S(1)}, bf16[1,512,1024]{2,1,0:T(8,128)(2,1)}, u32[]{:S(2)}) copy-start(bf16[1,512,1024]{2,1,0:T(8,128)(2,1)} %param.13) | copy-start | bytes 3145732
  7.2 72.3 %all-gather.4.cloned.1.call-start = ((), (), s32[]{:S(2)}) async-start(), calls=%async_computation.1 | async-start | bytes 1310720 | tf_op jit(solution)/shard_map/all_gather | solution.py:937
  49.0 1.1 copy-start.16
  49.0 1.8 copy-start.18
  49.1 94.1 %all-gather.6.cloned.1.call-start = ((), (), s32[]{:S(2)}) async-start(), calls=%async_computation.3 | async-start | bytes 5242880 | tf_op jit(solution)/shard_map/all_gather | solution.py:938
  49.8 458.8 %reduce-scatter.2.cloned.1.call-start = ((), (), s32[]{:S(2)}) async-start(), calls=%async_computation.2 | async-start | bytes 15728640 | tf_op jit(solution)/shard_map/reduce_scatter | solution.py:967
  54.5 13.2 %copy-start.14 = (s32[4,1,512]{2,1,0:T(1,128)S(1)}, s32[4,1,512]{2,1,0:T(1,128)}, u32[]{:S(2)}) copy-start(s32[4,1,512]{2,1,0:T(1,128)} %get-tuple-element.28) | copy-start | bytes 24580
  54.5 13.4 %copy-start.17 = (s32[1,4]{1,0:T(1,128)S(1)}, s32[1,4]{1,0:T(1,128)}, u32[]{:S(2)}) copy-start(s32[1,4]{1,0:T(1,128)} %param.24) | copy-start | bytes 52
  54.5 15.0 %copy-start.12 = (s32[4,32,128]{2,1,0:T(8,128)S(1)}, s32[4,32,128]{2,1,0:T(8,128)}, u32[]{:S(2)}) copy-start(s32[4,32,128]{2,1,0:T(8,128)} %get-tuple-element.37) | copy-start | bytes 196612
  72.6 1.2 copy-start.11
  72.8 2.6 copy-start.15
  212.3 1.6 copy-start
  247.9 34.1 %copy-start.13 = (f32[1,4,256]{2,0,1:T(1,128)S(1)}, f32[1,4,256]{2,0,1:T(1,128)}, u32[]{:S(2)}) copy-start(f32[1,4,256]{2,0,1:T(1,128)} %get-tuple-element.101) | copy-start | bytes 12292
  247.9 36.4 %copy-start.6 = (bf16[1,512,1024]{2,1,0:T(8,128)(2,1)S(1)}, bf16[1,512,1024]{2,1,0:T(8,128)(2,1)}, u32[]{:S(2)}) copy-start(bf16[1,512,1024]{2,1,0:T(8,128)(2,1)} %param.25) | copy-start | bytes 3145732
  282.0 2.4 copy-start.1
  282.0 2.8 copy-start.2
  284.8 3.4 copy-start.7
  301.8 97.9 %copy-start.8 = (f32[512,512]{1,0:T(8,128)S(1)}, f32[512,512]{1,0:T(8,128)}, u32[]{:S(2)}) copy-start(f32[512,512]{1,0:T(8,128)} %get-tuple-element.43) | copy-start | bytes 3145732
  399.7 7.2 %copy-start.10 = (bf16[512,256]{1,0:T(8,128)(2,1)}, bf16[512,256]{1,0:T(8,128)(2,1)S(1)}, u32[]{:S(2)}) copy-start(bf16[512,256]{1,0:T(8,128)(2,1)S(1)} %slice.136) | copy-start | bytes 786436
  411.0 5.3 %copy-start.5 = (bf16[1,512,1024]{2,1,0:T(8,128)(2,1)S(1)}, bf16[1,512,1024]{2,1,0:T(8,128)(2,1)}, u32[]{:S(2)}) copy-start(bf16[1,512,1024]{2,1,0:T(8,128)(2,1)} %param.13) | copy-start | bytes 3145732
  416.3 2.5 copy-start.3
  424.3 3.8 copy-start.9
Sparse Core Ops, SparseCore 0:
  49.2 24.6 all-gather.3
  75.7 67.4 all-gather.5
  212.4 244.8 reduce-scatter.1

commit v4 on v3

v4 whole, which is shorter than its diff:
```python
import functools

import jax
import jax.numpy as jnp
from jax import lax
from jax.experimental import pallas as pl
from jax.experimental.pallas import tpu as pltpu
from jax.sharding import PartitionSpec as P

HEAD_DIM = 64
TOP = 8
PIC = 256
CAP = 144

EPSILON = 1e-06
THETA = 10000.0
NEG_FILL = -1e30


KEY_ROWS = 256
NT = (((1,), (1,)), ((), ()))
LIMIT = 60 * 1024 * 1024


def seen_bias(flags, j, blocks, kinfo_ref, qinfo_ref):
    rows = pl.ds(pl.multiple_of(j * KEY_ROWS, KEY_ROWS), KEY_ROWS)
    q_doc, q_pic = qinfo_ref[0:1, :], qinfo_ref[1:2, :]
    k_doc, k_pic = kinfo_ref[rows, 0:1], kinfo_ref[rows, 1:2]
    q_place = flags[blocks] + lax.broadcasted_iota(jnp.int32, q_doc.shape, 1)
    k_place = j * KEY_ROWS + lax.broadcasted_iota(jnp.int32, k_doc.shape, 0)
    seen = (k_doc == q_doc) & ((k_place <= q_place) | ((k_pic == q_pic) & (q_pic >= 0)))
    return rows, jnp.where(seen, 0.0, NEG_FILL)


def attend_kernel(
    flags, q_ref, kv_ref, kinfo_ref, qinfo_ref, out_w_ref, mix_ref, full_ref, log_ref, part_ref,
    acc, top, total,
):
    blocks = kv_ref.shape[0] // KEY_ROWS
    kv_width = kv_ref.shape[1] // 2
    heads, kv_heads = q_ref.shape[1] // HEAD_DIM, kv_width // HEAD_DIM
    top[...] = jnp.full(top.shape, NEG_FILL, jnp.float32)
    total[...] = jnp.zeros(total.shape, jnp.float32)
    acc[...] = jnp.zeros(acc.shape, jnp.float32)

    def step(j, carry):
        @pl.when(flags[j] > 0)
        def _():
            rows, bias = seen_bias(flags, j, blocks, kinfo_ref, qinfo_ref)
            for g in range(kv_heads):
                key = kv_ref[rows, g * HEAD_DIM : (g + 1) * HEAD_DIM]
                val = kv_ref[rows, kv_width + g * HEAD_DIM : kv_width + (g + 1) * HEAD_DIM]
                val_t = jnp.transpose(val.astype(jnp.float32)).astype(jnp.bfloat16)
                for h in range(g * heads // kv_heads, (g + 1) * heads // kv_heads):
                    at = slice(h * HEAD_DIM, (h + 1) * HEAD_DIM)
                    scores = bias + lax.dot_general(
                        key, q_ref[:, at], NT, preferred_element_type=jnp.float32
                    )
                    old = top[h : h + 1, :]
                    new = jnp.maximum(old, jnp.max(scores, axis=0, keepdims=True))
                    probs = jnp.exp(scores - new)
                    fade = jnp.exp(old - new)
                    total[h : h + 1, :] = total[h : h + 1, :] * fade + jnp.sum(
                        probs, axis=0, keepdims=True
                    )
                    acc[at, :] = acc[at, :] * fade + jnp.dot(
                        val_t, probs.astype(jnp.bfloat16), preferred_element_type=jnp.float32
                    )
                    top[h : h + 1, :] = new

        return carry

    lax.fori_loop(0, blocks, step, 0)
    log_ref[...] = top[...] + jnp.log(total[...])
    for h in range(heads):
        at = slice(h * HEAD_DIM, (h + 1) * HEAD_DIM)
        acc[at, :] = acc[at, :] / total[h : h + 1, :]
    full = jnp.transpose(acc[...])
    full_ref[...] = full
    mix_ref[...] = full.astype(jnp.bfloat16)
    part_ref[...] = jnp.dot(
        mix_ref[...], out_w_ref[...], preferred_element_type=jnp.float32
    ).astype(jnp.bfloat16)


def attend_back_kernel(
    flags, q_ref, kv_ref, kinfo_ref, qinfo_ref, log_ref, full_ref, grad_ref, dq_ref, dkv_ref,
    acc, delta,
):
    blocks = kv_ref.shape[0] // KEY_ROWS
    kv_width = kv_ref.shape[1] // 2
    heads, kv_heads = q_ref.shape[1] // HEAD_DIM, kv_width // HEAD_DIM
    acc[...] = jnp.transpose(full_ref[...] * grad_ref[...].astype(jnp.float32))
    for h in range(heads):
        delta[h : h + 1, :] = jnp.sum(
            acc[h * HEAD_DIM : (h + 1) * HEAD_DIM, :], axis=0, keepdims=True
        )
    acc[...] = jnp.zeros(acc.shape, jnp.float32)

    def step(j, carry):
        @pl.when(flags[j] > 0)
        def _():
            rows, bias = seen_bias(flags, j, blocks, kinfo_ref, qinfo_ref)
            for g in range(kv_heads):
                k_at = slice(g * HEAD_DIM, (g + 1) * HEAD_DIM)
                v_at = slice(kv_width + g * HEAD_DIM, kv_width + (g + 1) * HEAD_DIM)
                key, val = kv_ref[rows, k_at], kv_ref[rows, v_at]
                key_t = jnp.transpose(key.astype(jnp.float32)).astype(jnp.bfloat16)
                dk = jnp.zeros((KEY_ROWS, HEAD_DIM), jnp.float32)
                dv = jnp.zeros((KEY_ROWS, HEAD_DIM), jnp.float32)
                for h in range(g * heads // kv_heads, (g + 1) * heads // kv_heads):
                    at = slice(h * HEAD_DIM, (h + 1) * HEAD_DIM)
                    q_rows, g_rows = q_ref[:, at], grad_ref[:, at]
                    scores = bias + lax.dot_general(
                        key, q_rows, NT, preferred_element_type=jnp.float32
                    )
                    probs = jnp.exp(scores - log_ref[h : h + 1, :])
                    prob_grad = lax.dot_general(
                        val, g_rows, NT, preferred_element_type=jnp.float32
                    )
                    slope = (probs * (prob_grad - delta[h : h + 1, :])).astype(jnp.bfloat16)
                    dv += jnp.dot(
                        probs.astype(jnp.bfloat16), g_rows, preferred_element_type=jnp.float32
                    )
                    dk += jnp.dot(slope, q_rows, preferred_element_type=jnp.float32)
                    acc[at, :] += jnp.dot(key_t, slope, preferred_element_type=jnp.float32)
                dkv_ref[rows, k_at] = dk.astype(dkv_ref.dtype)
                dkv_ref[rows, v_at] = dv.astype(dkv_ref.dtype)

        @pl.when(flags[j] == 0)
        def _():
            rows = pl.ds(pl.multiple_of(j * KEY_ROWS, KEY_ROWS), KEY_ROWS)
            dkv_ref[rows, :] = jnp.zeros((KEY_ROWS, dkv_ref.shape[1]), dkv_ref.dtype)

        return carry

    lax.fori_loop(0, blocks, step, 0)
    dq_ref[...] = jnp.transpose(acc[...]) * (HEAD_DIM**-0.5)


def whole_vmem(count):
    return [pl.BlockSpec(memory_space=pltpu.VMEM)] * count


def attend(flags, q, kv, kinfo, qinfo, out_w):
    rows, width = q.shape
    heads = width // HEAD_DIM
    return pl.pallas_call(
        attend_kernel,
        name="attend",
        in_specs=[pl.BlockSpec(memory_space=pltpu.SMEM)] + whole_vmem(5),
        out_specs=whole_vmem(4),
        out_shape=[
            jax.ShapeDtypeStruct((rows, width), jnp.bfloat16),
            jax.ShapeDtypeStruct((rows, width), jnp.float32),
            jax.ShapeDtypeStruct((heads, rows), jnp.float32),
            jax.ShapeDtypeStruct((rows, out_w.shape[1]), jnp.bfloat16),
        ],
        scratch_shapes=[
            pltpu.VMEM((width, rows), jnp.float32),
            pltpu.VMEM((heads, rows), jnp.float32),
            pltpu.VMEM((heads, rows), jnp.float32),
        ],
        compiler_params=pltpu.CompilerParams(vmem_limit_bytes=LIMIT),
    )(flags, q, kv, kinfo, qinfo, out_w)


def attend_back(flags, q, kv, kinfo, qinfo, log_total, full, grad):
    rows, width = q.shape
    return pl.pallas_call(
        attend_back_kernel,
        name="attend_back",
        in_specs=[pl.BlockSpec(memory_space=pltpu.SMEM)] + whole_vmem(7),
        out_specs=whole_vmem(2),
        out_shape=[
            jax.ShapeDtypeStruct((rows, width), jnp.float32),
            jax.ShapeDtypeStruct(kv.shape, jnp.bfloat16),
        ],
        scratch_shapes=[
            pltpu.VMEM((width, rows), jnp.float32),
            pltpu.VMEM((width // HEAD_DIM, rows), jnp.float32),
        ],
        compiler_params=pltpu.CompilerParams(vmem_limit_bytes=LIMIT),
    )(flags, q, kv, kinfo, qinfo, log_total, full, grad)


def block_flags(pic_starts, q_docs, k_docs, offset):
    block_len, length = q_docs.shape[0], k_docs.shape[0]
    docs = k_docs.reshape(length // KEY_ROWS, KEY_ROWS)
    first = jnp.arange(length // KEY_ROWS, dtype=jnp.int32) * KEY_ROWS
    same = (docs[:, 0] <= q_docs[-1]) & (docs[:, -1] >= q_docs[0])
    spans = (
        (pic_starts[None, :] < offset + block_len)
        & (pic_starts[None, :] + PIC > offset)
        & (pic_starts[None, :] < first[:, None] + KEY_ROWS)
        & (pic_starts[None, :] + PIC > first[:, None])
    )
    needed = same & ((first < offset + block_len) | jnp.any(spans, axis=1))
    return jnp.concatenate([needed.astype(jnp.int32), offset[None].astype(jnp.int32)])


MESH = pl.DeviceIdType.MESH
TN = (((0,), (0,)), ((), ()))


def place_on(axes):
    index, size = 0, 1
    for axis in axes:
        index = index * lax.axis_size(axis) + lax.axis_index(axis)
        size *= lax.axis_size(axis)
    return index, size


def greet(axes_list, line=False):
    barrier = pltpu.get_barrier_semaphore()
    count = 0
    for axis in axes_list:
        me, size = lax.axis_index(axis), lax.axis_size(axis)

        def signal(k, carry, axis=axis, me=me, size=size):
            pl.semaphore_signal(
                barrier, inc=1, device_id={axis: lax.rem(me + k, size)}, device_id_type=MESH
            )
            return carry

        lax.fori_loop(1, size, signal, 0)
        count += size - 1
    if not line:
        pl.semaphore_wait(barrier, count)
        return
    me, size = lax.axis_index("ctx"), lax.axis_size("ctx")
    for step in (1, -1):
        other = me + step

        @pl.when((other >= 0) & (other < size))
        def _(other=other):
            pl.semaphore_signal(barrier, inc=1, device_id={"ctx": other}, device_id_type=MESH)

    inner = (me > 0) & (me < size - 1)

    @pl.when(inner)
    def _():
        pl.semaphore_wait(barrier, count + 2)

    @pl.when(jnp.logical_not(inner))
    def _():
        pl.semaphore_wait(barrier, count + 1)


def remote(src, dst, sems, k, device_id):
    return pltpu.make_async_remote_copy(
        src_ref=src,
        dst_ref=dst,
        send_sem=sems[0].at[k],
        recv_sem=sems[1].at[k],
        device_id=device_id,
        device_id_type=MESH,
    )


def other_core():
    return {"tp": 1 - lax.axis_index("tp")}


def ahead_on(axis, k):
    return lax.rem(lax.axis_index(axis) + k, lax.axis_size(axis))


def each(count, do, first=1):
    def step(k, carry):
        do(k)
        return carry

    lax.fori_loop(first, count, step, 0)


def sem_pair(count):
    return [pltpu.SemaphoreType.DMA((count,)), pltpu.SemaphoreType.DMA((count,))]


def remote_params(ident):
    return pltpu.CompilerParams(
        collective_id=ident, has_side_effects=True, vmem_limit_bytes=LIMIT
    )


def halves(rows):
    half = rows // 2
    core = lax.axis_index("tp")
    return (
        pl.ds(pl.multiple_of(core * half, half), half),
        pl.ds(pl.multiple_of((1 - core) * half, half), half),
    )


def spread_kernel(axes_of, *refs):
    count = len(axes_of)
    ins, outs, sems = refs[:count], refs[count : 2 * count], refs[2 * count :]
    greet(sorted(set(axes_of)))

    def copy(i, k):
        return remote(
            ins[i],
            outs[i].at[lax.axis_index(axes_of[i])],
            sems[2 * i : 2 * i + 2],
            k,
            {axes_of[i]: ahead_on(axes_of[i], k)},
        )

    for i in range(count):
        each(lax.axis_size(axes_of[i]), lambda k, i=i: copy(i, k).start())
    for i in range(count):
        outs[i][lax.axis_index(axes_of[i])] = ins[i][...]
    for i in range(count):
        each(lax.axis_size(axes_of[i]), lambda k, i=i: copy(i, k).wait())


def spread(arrays, axes_of, ident, name):
    sizes = [lax.axis_size(axis) for axis in axes_of]
    return pl.pallas_call(
        functools.partial(spread_kernel, tuple(axes_of)),
        name=name,
        in_specs=whole_vmem(len(arrays)),
        out_specs=whole_vmem(len(arrays)),
        out_shape=[
            jax.ShapeDtypeStruct((size,) + a.shape, a.dtype) for size, a in zip(sizes, arrays)
        ],
        scratch_shapes=sum([sem_pair(size) for size in sizes], []),
        compiler_params=remote_params(ident),
    )(*arrays)


def turn(tile, cosine, sine):
    lane = lax.broadcasted_iota(jnp.int32, tile.shape, 1)
    half = HEAD_DIM // 2
    swapped = jnp.where(
        lax.rem(lane, HEAD_DIM) < half,
        pltpu.roll(tile, 2 * HEAD_DIM - half, 1),
        pltpu.roll(tile, half, 1),
    )
    return tile * cosine + swapped * sine


def row_scale(x):
    return lax.rsqrt(jnp.mean(x * x, axis=-1, keepdims=True) + EPSILON)


def norm_back(x, gain, grad):
    scale = row_scale(x)
    unit = x * scale
    pull = grad * gain
    return (
        scale * (pull - unit * jnp.mean(pull * unit, axis=-1, keepdims=True)),
        jnp.sum(grad * unit, axis=0, keepdims=True),
    )


def back_blocks(ctx_size, block_len, length):
    return min(ctx_size - 1, -(-(length // 2 - 1) // block_len))


def ahead_blocks(block_len, length, spans):
    return 0 if block_len % (length // spans) == 0 else 1


class RowGather:
    def __init__(self, source, target, dp_sems, tp_sems, first):
        self.source, self.target = source, target
        self.dp_sems, self.tp_sems, self.first = dp_sems, tp_sems, first
        self.mine, _ = halves(source.shape[0])
        self.size = lax.axis_size("dp")

    def copy(self, k):
        at = self.target.at[lax.axis_index("dp"), self.mine]
        return remote(
            self.source.at[self.mine], at, self.dp_sems, k, {"dp": ahead_on("dp", k)}
        )

    def relay(self, k):
        at = self.target.at[ahead_on("dp", self.size - k), self.mine]
        return remote(at, at, self.tp_sems, self.first + k, other_core())

    def start(self):
        each(self.size, lambda k: self.copy(k).start())

    def forward(self):
        def one(k):
            self.copy(k).wait_recv()
            self.relay(k).start()

        each(self.size, one)

    def finish(self):
        def one(k):
            self.copy(k).wait_send()
            self.relay(k).wait()

        each(self.size, one)


def project_kernel(
    back, ahead, q_width, x_ref, w_ref, gain_ref, cos_ref, sin_ref, cot_ref, normed_ref, q_ref,
    all_ref, cot_all_ref, kv_ref, line_send, line_recv, dp_send, dp_recv, tp_send, tp_recv,
):
    me, size = lax.axis_index("ctx"), lax.axis_size("ctx")
    greet(["dp", "tp"], line=True)
    rows_of = RowGather(cot_ref, cot_all_ref, (dp_send, dp_recv), (tp_send, tp_recv), 0)
    rows_of.start()
    x = x_ref[...].astype(jnp.float32)
    normed_ref[...] = (x * row_scale(x) * gain_ref[...]).astype(jnp.bfloat16)
    kv_width = kv_ref.shape[1] // 2
    wide = 2 * HEAD_DIM
    for first in range(q_width, q_width + 2 * kv_width, wide):
        tile = jnp.dot(
            normed_ref[...], w_ref[:, first : first + wide], preferred_element_type=jnp.float32
        )
        if first < q_width + kv_width:
            tile = turn(tile, cos_ref[...], -sin_ref[...])
        kv_ref[:, first - q_width : first - q_width + wide] = tile.astype(jnp.bfloat16)

    sems = (line_send, line_recv)
    right, left = me + 1, me - 1

    def hop(s):
        block = lax.rem(me + size - s, size)
        return remote(
            kv_ref if s == 0 else all_ref.at[block], all_ref.at[block], sems, s, {"ctx": right}
        )

    def arrive(s):
        return remote(kv_ref, all_ref.at[me], sems, s, {"ctx": right})

    def back_hop():
        return remote(kv_ref, all_ref.at[me], sems, back, {"ctx": left})

    if ahead:

        @pl.when(left >= 0)
        def _():
            back_hop().start()

    for s in range(back):

        @pl.when((right < size) & (me - s >= 0))
        def _(s=s):
            hop(s).start()

        if s == 0:
            all_ref[me] = kv_ref[...]
            for first in range(0, q_width, wide):
                tile = jnp.dot(
                    normed_ref[...],
                    w_ref[:, first : first + wide],
                    preferred_element_type=jnp.float32,
                )
                tile = turn(tile, cos_ref[...], -sin_ref[...]).astype(jnp.bfloat16)
                q_ref[:, first : first + wide] = (
                    tile.astype(jnp.float32) * HEAD_DIM**-0.5
                ).astype(jnp.bfloat16)

        @pl.when(me - s - 1 >= 0)
        def _(s=s):
            arrive(s).wait_recv()

    rows_of.forward()
    for s in range(back):

        @pl.when((right < size) & (me - s >= 0))
        def _(s=s):
            hop(s).wait_send()

    if ahead:

        @pl.when(left >= 0)
        def _():
            back_hop().wait_send()

        @pl.when(right < size)
        def _():
            back_hop().wait_recv()

    cot_all_ref[lax.axis_index("dp")] = cot_ref[...]
    rows_of.finish()


def project(x, w, gain, cosine, sine, cot, q_width, back, ahead, ident):
    rows, width = x.shape
    kv_cols = w.shape[1] - q_width
    dp_size, ctx_size = lax.axis_size("dp"), lax.axis_size("ctx")
    low = jnp.bfloat16
    return pl.pallas_call(
        functools.partial(project_kernel, back, ahead, q_width),
        name="project",
        in_specs=whole_vmem(6),
        out_specs=whole_vmem(4),
        out_shape=[
            jax.ShapeDtypeStruct((rows, width), low),
            jax.ShapeDtypeStruct((rows, q_width), low),
            jax.ShapeDtypeStruct((ctx_size, rows, kv_cols), low),
            jax.ShapeDtypeStruct((dp_size, rows, width), low),
        ],
        scratch_shapes=[
            pltpu.VMEM((rows, kv_cols), low),
            *sem_pair(back + 1),
            *sem_pair(dp_size),
            *sem_pair(dp_size),
        ],
        compiler_params=remote_params(ident),
    )(x, w, gain, cosine, sine, cot)


def share_rows_kernel(
    part_ref, x_ref, gain_ref, hidden_ref, all_ref, held, normed, dp_send, dp_recv, tp_send,
    tp_recv,
):
    mine, theirs = halves(part_ref.shape[0])
    greet(["dp", "tp"])
    size = lax.axis_size("dp")
    rows_of = RowGather(normed, all_ref, (dp_send, dp_recv), (tp_send, tp_recv), 1)
    first = remote(part_ref.at[theirs], held.at[theirs], (tp_send, tp_recv), 0, other_core())
    second = remote(part_ref.at[mine], held.at[mine], (tp_send, tp_recv), 1, other_core())
    first.start()
    second.start()

    def norm(rows):
        total = x_ref[rows, :].astype(jnp.float32) + (
            part_ref[rows, :].astype(jnp.float32) + held[rows, :].astype(jnp.float32)
        )
        hidden_ref[rows, :] = total
        normed[rows, :] = (total * row_scale(total) * gain_ref[...]).astype(jnp.bfloat16)

    first.wait()
    norm(mine)
    rows_of.start()
    second.wait()
    norm(theirs)
    all_ref[lax.axis_index("dp")] = normed[...]
    rows_of.forward()
    rows_of.finish()


def share_rows(part, x, gain, ident):
    size = lax.axis_size("dp")
    rows, width = part.shape
    return pl.pallas_call(
        share_rows_kernel,
        name="share_rows",
        in_specs=whole_vmem(3),
        out_specs=whole_vmem(2),
        out_shape=[
            jax.ShapeDtypeStruct((rows, width), jnp.float32),
            jax.ShapeDtypeStruct((size, rows, width), jnp.bfloat16),
        ],
        scratch_shapes=[
            pltpu.VMEM((rows, width), jnp.bfloat16),
            pltpu.VMEM((rows, width), jnp.bfloat16),
            *sem_pair(size),
            *sem_pair(size + 1),
        ],
        compiler_params=remote_params(ident),
    )(part, x, gain)


class RowReturn:
    def __init__(self, part, held, landed, total, sent, came, dp_sems, tp_sems):
        self.part, self.held, self.landed, self.total = part, held, landed, total
        self.sent, self.came, self.dp_sems, self.tp_sems = sent, came, dp_sems, tp_sems
        self.size = lax.axis_size("dp")
        self.mine, self.theirs = halves(part.shape[1])

    def swap(self, k):
        group = ahead_on("dp", k)
        return remote(
            self.part.at[group, self.theirs], self.held.at[k], self.tp_sems, k, other_core()
        )

    def copy(self, k):
        return remote(
            self.held.at[k], self.landed.at[k], self.dp_sems, k, {"dp": ahead_on("dp", k)}
        )

    def last(self):
        return remote(self.sent, self.came, self.tp_sems, self.size, other_core())

    def both(self, k):
        group = ahead_on("dp", k)
        return self.part[group, self.mine].astype(jnp.float32) + self.held[k].astype(jnp.float32)

    def start(self):
        each(self.size + 1, lambda k: self.swap(lax.rem(k, self.size)).start())

    def forward(self):
        def one(k):
            self.swap(k).wait_recv()
            self.held[k] = self.both(k).astype(jnp.bfloat16)
            self.copy(k).start()

        each(self.size, one)
        self.swap(0).wait()
        self.total[...] = self.both(0)

    def gather(self):
        def one(k):
            self.copy(k).wait_recv()
            self.total[...] += self.landed[k].astype(jnp.float32)

        each(self.size, one)
        self.sent[...] = self.total[...].astype(jnp.bfloat16)
        self.last().start()

    def finish(self):
        def one(k):
            self.swap(k).wait_send()
            self.copy(k).wait_send()

        each(self.size, one)
        self.last().wait()


def return_scratch(size, rows, width):
    low = jnp.bfloat16
    return [
        pltpu.VMEM((size, rows // 2, width), low),
        pltpu.VMEM((size, rows // 2, width), low),
        pltpu.VMEM((rows // 2, width), jnp.float32),
        pltpu.VMEM((rows // 2, width), low),
        pltpu.VMEM((rows // 2, width), low),
        *sem_pair(size),
        *sem_pair(size + 1),
    ]


def return_grads_kernel(
    part_ref, hidden_ref, cot_ref, gain_ref, out_w_ref, grad_ref, low_ref, mix_ref, gain_grad_ref,
    held, landed, total, sent, came, dp_send, dp_recv, tp_send, tp_recv,
):
    greet(["dp", "tp"])
    rows = RowReturn(
        part_ref, held, landed, total, sent, came, (dp_send, dp_recv), (tp_send, tp_recv)
    )
    rows.start()
    rows.forward()
    rows.gather()

    def turn_back(at, grads):
        x_grad, gain_grad = norm_back(
            hidden_ref[at, :], gain_ref[...], grads.astype(jnp.float32)
        )
        hidden_grad = cot_ref[at, :].astype(jnp.float32) + x_grad
        grad_ref[at, :] = hidden_grad
        low_ref[at, :] = hidden_grad.astype(jnp.bfloat16)
        mix_ref[at, :] = lax.dot_general(
            low_ref[at, :], out_w_ref[...], NT, preferred_element_type=jnp.float32
        ).astype(jnp.bfloat16)
        return gain_grad

    gain_mine = turn_back(rows.mine, sent[...])
    rows.finish()
    gain_theirs = turn_back(rows.theirs, came[...])
    gain_grad_ref[...] = gain_mine + gain_theirs


def return_grads(part, hidden, cot, gain, out_w, ident):
    size, rows, width = part.shape
    return pl.pallas_call(
        return_grads_kernel,
        name="return_grads",
        in_specs=whole_vmem(5),
        out_specs=whole_vmem(4),
        out_shape=[
            jax.ShapeDtypeStruct((rows, width), jnp.float32),
            jax.ShapeDtypeStruct((rows, width), jnp.bfloat16),
            jax.ShapeDtypeStruct((rows, out_w.shape[0]), jnp.bfloat16),
            jax.ShapeDtypeStruct((1, width), jnp.float32),
        ],
        scratch_shapes=return_scratch(size, rows, width),
        compiler_params=remote_params(ident),
    )(part, hidden, cot, gain, out_w)


def trade_kernel(
    back, ahead, kv_grad_ref, part_ref, hidden_ref, low_ref, mix_ref, kv_ref, out_ref, out_w_ref,
    going, came_kv, line_send, line_recv, held, landed, total, sent, came, dp_send, dp_recv,
    tp_send, tp_recv,
):
    me, size = lax.axis_index("ctx"), lax.axis_size("ctx")
    greet(["dp", "tp"], line=True)
    right, left = me + 1, me - 1
    sems = (line_send, line_recv)

    def hop(s, src):
        return remote(src, came_kv.at[s], sems, s, {"ctx": left})

    def forth():
        return remote(
            kv_grad_ref.at[lax.rem(me + 1, size)], came_kv.at[0], sems, 0, {"ctx": right}
        )

    def own_piece(s):
        return kv_grad_ref.at[lax.rem(me + size - s, size)]

    if ahead:

        @pl.when(right < size)
        def _():
            forth().start()

    @pl.when(me - back >= 0)
    def _():
        hop(back, own_piece(back)).start()

    rows = RowReturn(
        part_ref, held, landed, total, sent, came, (dp_send, dp_recv), (tp_send, tp_recv)
    )
    rows.start()
    rows.forward()
    turned = jnp.transpose(low_ref[...].astype(jnp.float32)).astype(jnp.bfloat16)
    grad = jnp.dot(turned, mix_ref[...], preferred_element_type=jnp.float32)
    piece = out_w_ref.shape[1]
    for i in range(out_w_ref.shape[0]):
        out_w_ref[i] = grad[i * piece : (i + 1) * piece].astype(jnp.bfloat16)

    for s in range(back - 1, 0, -1):

        @pl.when((me - s >= 0) & (right < size))
        def _(s=s):
            hop(s + 1, going.at[s]).wait_recv()
            going[s] = (
                own_piece(s)[...].astype(jnp.float32) + came_kv[s + 1].astype(jnp.float32)
            ).astype(going.dtype)
            hop(s, going.at[s]).start()

        @pl.when((me - s >= 0) & (right >= size))
        def _(s=s):
            hop(s, own_piece(s)).start()

    rows.gather()
    kv_ref[...] = kv_grad_ref[me].astype(jnp.float32)

    @pl.when(right < size)
    def _():
        hop(1, going.at[0]).wait_recv()
        kv_ref[...] += came_kv[1].astype(jnp.float32)

    if ahead:

        @pl.when(left >= 0)
        def _():
            forth().wait_recv()
            kv_ref[...] += came_kv[0].astype(jnp.float32)

        @pl.when(right < size)
        def _():
            forth().wait_send()

    for s in range(back, 0, -1):

        @pl.when(me - s >= 0)
        def _(s=s):
            hop(s, going.at[0]).wait_send()

    rows.finish()
    mine, theirs = rows.mine, rows.theirs
    out_ref[mine, :] = (hidden_ref[mine, :] + sent[...].astype(jnp.float32)).astype(jnp.bfloat16)
    out_ref[theirs, :] = (hidden_ref[theirs, :] + came[...].astype(jnp.float32)).astype(
        jnp.bfloat16
    )


def trade(kv_grad, part, hidden, low, mix, back, ahead, ident):
    size, rows, width = part.shape
    kv_shape = kv_grad.shape[1:]
    held = pltpu.VMEM((back + 1,) + kv_shape, kv_grad.dtype)
    return pl.pallas_call(
        functools.partial(trade_kernel, back, ahead),
        name="trade",
        in_specs=whole_vmem(5),
        out_specs=whole_vmem(3),
        out_shape=[
            jax.ShapeDtypeStruct(kv_shape, jnp.float32),
            jax.ShapeDtypeStruct((rows, width), jnp.bfloat16),
            jax.ShapeDtypeStruct((size, width // size, mix.shape[1]), jnp.bfloat16),
        ],
        scratch_shapes=[
            held, held, *sem_pair(back + 1), *return_scratch(size, rows, width)
        ],
        compiler_params=remote_params(ident),
    )(kv_grad, part, hidden, low, mix)


class PieceSum:
    def __init__(self, axis, source, landed, sems):
        self.axis, self.source, self.landed, self.sems = axis, source, landed, sems
        self.size = lax.axis_size(axis)

    def copy(self, k):
        peer = ahead_on(self.axis, k)
        return remote(
            self.source.at[peer], self.landed.at[k], self.sems, k, {self.axis: peer}
        )

    def send(self, k):
        self.copy(k).start()

    def total(self):
        each(self.size, lambda k: self.copy(k).wait_recv())
        whole = self.source[lax.axis_index(self.axis)].astype(jnp.float32)
        for k in range(1, self.size):
            whole += self.landed[k].astype(jnp.float32)
        return whole

    def finish(self):
        each(self.size, lambda k: self.copy(k).wait_send())


class WholeSum:
    def __init__(self, axis, source, landed, sems):
        self.axis, self.source, self.landed, self.sems = axis, source, landed, sems
        self.size = lax.axis_size(axis)

    def copy(self, k):
        return remote(
            self.source, self.landed.at[k], self.sems, k, {self.axis: ahead_on(self.axis, k)}
        )

    def start(self):
        each(self.size, lambda k: self.copy(k).start())

    def total(self):
        each(self.size, lambda k: self.copy(k).wait())
        whole = self.source[...]
        for k in range(1, self.size):
            whole += self.landed[k]
        return whole


def finish_kernel(
    dq_ref, dkv_ref, cos_ref, sin_ref, normed_ref, w_ref, x_ref, gain_ref, hidden_ref, out_w_ref,
    gain_two_ref, in_ref, own_ref, gains_ref, joined, turned, part, held, pieces, landed,
    out_landed, low, low_landed, gain_rows, gain_landed, gain_more, gain_more_landed, *sems,
):
    greet(["dp", "ctx", "tp"])
    pairs = [sems[2 * i : 2 * i + 2] for i in range(len(sems) // 2)]
    out_sum = PieceSum("dp", out_w_ref, out_landed, pairs[0])
    each(out_sum.size, out_sum.send)
    wide = 2 * HEAD_DIM
    q_width, kv_width = dq_ref.shape[1], dkv_ref.shape[1] // 2
    for first in range(0, q_width, wide):
        joined[:, first : first + wide] = turn(
            dq_ref[:, first : first + wide], cos_ref[...], sin_ref[...]
        ).astype(jnp.bfloat16)
    for first in range(0, kv_width, wide):
        joined[:, q_width + first : q_width + first + wide] = turn(
            dkv_ref[:, first : first + wide], cos_ref[...], sin_ref[...]
        ).astype(jnp.bfloat16)
    joined[:, q_width + kv_width :] = dkv_ref[:, kv_width:].astype(jnp.bfloat16)

    turned[...] = jnp.transpose(normed_ref[...].astype(jnp.float32)).astype(jnp.bfloat16)
    w_sum = PieceSum("dp", pieces, landed, pairs[1])
    rows = pieces.shape[1]

    def piece(k):
        peer = ahead_on("dp", k)
        at = pl.ds(pl.multiple_of(peer * rows, rows), rows)
        pieces[peer] = jnp.dot(
            turned[at, :], joined[...], preferred_element_type=jnp.float32
        ).astype(jnp.bfloat16)
        w_sum.send(k)

    each(w_sum.size, piece)
    part[...] = lax.dot_general(
        joined[...], w_ref[...], NT, preferred_element_type=jnp.float32
    ).astype(jnp.bfloat16)
    swap = remote(part, held, pairs[2], 0, other_core())
    swap.start()
    me = lax.axis_index("dp")
    own = pl.ds(pl.multiple_of(me * rows, rows), rows)
    pieces[me] = jnp.dot(
        turned[own, :], joined[...], preferred_element_type=jnp.float32
    ).astype(jnp.bfloat16)
    swap.wait()
    x_grad, gain_grad = norm_back(
        x_ref[...].astype(jnp.float32),
        gain_ref[...],
        part[...].astype(jnp.float32) + held[...].astype(jnp.float32),
    )
    in_ref[...] = (hidden_ref[...] + x_grad).astype(jnp.bfloat16)
    gain_rows[...] = jnp.zeros(gain_rows.shape, jnp.float32)
    gain_rows[0:1, :] = gain_grad
    gain_rows[1:2, :] = gain_two_ref[...]
    gain_sum = WholeSum("dp", gain_rows, gain_landed, pairs[3])
    gain_sum.start()

    out_total = out_sum.total()
    w_total = w_sum.total()
    cols = w_total.shape[1]
    few = low.shape[1]
    for c in range(low.shape[0]):
        low[c, :, :cols] = w_total[c * few : (c + 1) * few].astype(jnp.bfloat16)
        low[c, :, cols:] = out_total[c * few : (c + 1) * few].astype(jnp.bfloat16)
    low_sum = PieceSum("ctx", low, low_landed, pairs[4])
    each(low_sum.size, low_sum.send)
    gain_more[...] = gain_sum.total()
    more_sum = WholeSum("ctx", gain_more, gain_more_landed, pairs[5])
    more_sum.start()
    out_sum.finish()
    w_sum.finish()
    own_ref[...] = low_sum.total()
    low_sum.finish()
    gains_ref[...] = more_sum.total()


def finish(dq, dkv, cosine, sine, normed, w, x, gain, hidden_grad, out_w, gain_two, ident):
    rows, width = x.shape
    dp_size, ctx_size = lax.axis_size("dp"), lax.axis_size("ctx")
    cols, out_cols = w.shape[1], out_w.shape[2]
    few = width // dp_size // ctx_size
    low, high = jnp.bfloat16, jnp.float32
    return pl.pallas_call(
        finish_kernel,
        name="finish",
        in_specs=whole_vmem(11),
        out_specs=whole_vmem(3),
        out_shape=[
            jax.ShapeDtypeStruct((rows, width), low),
            jax.ShapeDtypeStruct((few, cols + out_cols), high),
            jax.ShapeDtypeStruct((8, width), high),
        ],
        scratch_shapes=[
            pltpu.VMEM((rows, cols), low),
            pltpu.VMEM((width, rows), low),
            pltpu.VMEM((rows, width), low),
            pltpu.VMEM((rows, width), low),
            pltpu.VMEM((dp_size, width // dp_size, cols), low),
            pltpu.VMEM((dp_size, width // dp_size, cols), low),
            pltpu.VMEM(out_w.shape, low),
            pltpu.VMEM((ctx_size, few, cols + out_cols), low),
            pltpu.VMEM((ctx_size, few, cols + out_cols), low),
            pltpu.VMEM((8, width), high),
            pltpu.VMEM((dp_size, 8, width), high),
            pltpu.VMEM((8, width), high),
            pltpu.VMEM((ctx_size, 8, width), high),
            *sem_pair(dp_size),
            *sem_pair(dp_size),
            *sem_pair(1),
            *sem_pair(dp_size),
            *sem_pair(ctx_size),
            *sem_pair(ctx_size),
        ],
        compiler_params=remote_params(ident),
    )(dq, dkv, cosine, sine, normed, w, x, gain, hidden_grad, out_w, gain_two)


GROUPS_AT_ONCE = 4


def experts_kernel(
    more, rows_ref, grads_ref, weights_ref, place_ref, gate_ref, place_col_ref, *refs
):
    before, refs = (refs[:2], refs[2:]) if more else (None, refs)
    out_ref, back_ref, weight_grad_ref, slots, slot_grads, outs, backs = refs
    e = pl.program_id(1)
    groups, tok_rows, model_width = rows_ref.shape
    owners, part = weight_grad_ref.shape[1], weight_grad_ref.shape[5]
    slot_index = lax.broadcasted_iota(jnp.int32, (CAP, tok_rows), 0)
    gates = []
    for g in range(groups):
        picks = slot_index == place_ref[g, 0]
        gates.append(jnp.sum(jnp.where(picks, gate_ref[g, 0], 0.0), axis=1, keepdims=True))
        picks = picks.astype(jnp.float32).astype(jnp.bfloat16)
        at = slice(g * CAP, (g + 1) * CAP)
        slots[at, :] = jnp.dot(
            picks, rows_ref[g], preferred_element_type=jnp.float32
        ).astype(jnp.bfloat16)
        slot_grads[at, :] = (
            jnp.dot(picks, grads_ref[g], preferred_element_type=jnp.float32) * gates[g]
        ).astype(jnp.bfloat16)
    gate_w, up_w, down_w = (weights_ref.at[0, i] for i in range(3))
    gate_pre = jnp.dot(slots[...], gate_w[...], preferred_element_type=jnp.float32)
    up_pre = jnp.dot(slots[...], up_w[...], preferred_element_type=jnp.float32)
    act_grad = jnp.dot(slot_grads[...], down_w[...], preferred_element_type=jnp.float32)
    sig = 1.0 / (1.0 + jnp.exp(-gate_pre))
    silu = gate_pre * sig
    act_low = (silu * up_pre).astype(jnp.bfloat16)
    up_low = (act_grad * silu).astype(jnp.bfloat16)
    gate_low = (act_grad * up_pre * (sig * (1.0 + gate_pre * (1.0 - sig)))).astype(jnp.bfloat16)

    back = lax.dot_general(
        gate_low, gate_w[...], NT, preferred_element_type=jnp.float32
    ) + lax.dot_general(up_low, up_w[...], NT, preferred_element_type=jnp.float32)
    out = lax.dot_general(act_low, down_w[...], NT, preferred_element_type=jnp.float32)
    for g in range(groups):
        at = slice(g * CAP, (g + 1) * CAP)
        to = pl.ds(pl.multiple_of(e * CAP, CAP), CAP)
        backs[g, to, :] = back[at].astype(jnp.bfloat16)
        outs[g, to, :] = (out[at] * gates[g]).astype(jnp.bfloat16)

    for i, (low, source) in enumerate(
        ((gate_low, slots), (up_low, slots), (act_low, slot_grads))
    ):
        turned = jnp.transpose(low.astype(jnp.float32)).astype(jnp.bfloat16)
        total = jnp.dot(turned, source[...], preferred_element_type=jnp.float32)
        for c in range(owners):
            weight_grad_ref[0, c, 0, i] = total[:, c * part : (c + 1) * part].astype(
                weight_grad_ref.dtype
            )

    @pl.when(e == pl.num_programs(1) - 1)
    def _():
        slot_count = outs.shape[1]
        for g in range(groups):
            tiles = []
            for first in range(0, slot_count, 128):
                wide = min(128, slot_count - first)
                lane = first + lax.broadcasted_iota(jnp.int32, (tok_rows, wide), 1)
                hit = None
                for n in range(first // CAP, (first + wide - 1) // CAP + 1):
                    one = place_col_ref[g, :, n : n + 1] == lane - n * CAP
                    hit = one if hit is None else hit | one
                tiles.append(hit.astype(jnp.float32).astype(jnp.bfloat16))
            spread_picks = jnp.concatenate(tiles, axis=1)
            for i, (to_ref, source) in enumerate(((back_ref, backs), (out_ref, outs))):
                total = jnp.dot(spread_picks, source[g], preferred_element_type=jnp.float32)
                if more:
                    total += before[1 - i][g].astype(jnp.float32)
                to_ref[g] = total.astype(jnp.bfloat16)


def expert_places(chosen_all, gates_all, own):
    tok_rows = chosen_all.shape[1]
    named = chosen_all[..., None] == lax.axis_index("dp") * own + jnp.arange(own, dtype=jnp.int32)
    names = jnp.any(named, axis=2)
    gate_of = jnp.sum(jnp.where(named, gates_all[..., None], 0.0), axis=2)
    earlier = jnp.tril(jnp.ones((tok_rows, tok_rows), jnp.bfloat16), -1)
    place = jnp.einsum(
        "rq,gqe->gre", earlier, names.astype(jnp.bfloat16), preferred_element_type=jnp.float32
    ).astype(jnp.int32)
    place = jnp.where(names & (place < CAP), place, -CAP * own)
    return (
        place,
        place.transpose(0, 2, 1)[:, :, None],
        gate_of.transpose(0, 2, 1)[:, :, None],
    )


def experts(weights, places, rows_all, grad_all, first, count, before):
    _, _, model_width, hidden = weights.shape
    place_cols, place_rows, gate_rows = places
    groups, tok_rows, _ = rows_all.shape
    owners = lax.axis_size("ctx")
    at_once = min(GROUPS_AT_ONCE, groups)
    chunks = groups // at_once
    part = model_width // owners
    rows_spec = pl.BlockSpec(
        (at_once, tok_rows, model_width), lambda c, e: (c, 0, 0), pipeline_mode=pl.Buffered(1)
    )
    line_spec = pl.BlockSpec((at_once, 1, 1, tok_rows), lambda c, e: (c, e + first, 0, 0))
    out_shape = jax.ShapeDtypeStruct(rows_all.shape, jnp.bfloat16)
    flops = count * groups * CAP * model_width * 2 * (9 * hidden + 4 * tok_rows)
    more = before is not None
    out_part, back_part, weight_part = pl.pallas_call(
        functools.partial(experts_kernel, more),
        name="experts",
        grid=(chunks, count),
        in_specs=[
            rows_spec,
            rows_spec,
            pl.BlockSpec((1, 3, model_width, hidden), lambda c, e: (e + first, 0, 0, 0)),
            line_spec,
            line_spec,
            pl.BlockSpec((at_once, tok_rows, count), lambda c, e: (c, 0, 0)),
        ]
        + [rows_spec] * (2 * more),
        out_specs=[
            rows_spec,
            rows_spec,
            pl.BlockSpec((1, owners, 1, 3, hidden, part), lambda c, e: (c, 0, e, 0, 0, 0)),
        ],
        out_shape=[
            out_shape,
            out_shape,
            jax.ShapeDtypeStruct((chunks, owners, count, 3, hidden, part), jnp.bfloat16),
        ],
        scratch_shapes=[
            pltpu.VMEM((at_once * CAP, model_width), jnp.bfloat16),
            pltpu.VMEM((at_once * CAP, model_width), jnp.bfloat16),
            pltpu.VMEM((at_once, count * CAP, model_width), jnp.bfloat16),
            pltpu.VMEM((at_once, count * CAP, model_width), jnp.bfloat16),
        ],
        compiler_params=pltpu.CompilerParams(vmem_limit_bytes=LIMIT),
        cost_estimate=pl.CostEstimate(
            flops=flops, bytes_accessed=4 * weights.size, transcendentals=0
        ),
    )(
        rows_all,
        grad_all,
        weights,
        place_rows,
        gate_rows,
        place_cols[:, :, first : first + count],
        *(before if more else ()),
    )
    if chunks == 1:
        return (out_part, back_part), weight_part[0]
    return (out_part, back_part), jnp.sum(weight_part.astype(jnp.float32), axis=0).astype(
        jnp.bfloat16
    )


def picture_of(starts, token_positions):
    inside = (token_positions[:, None] >= starts[None, :]) & (
        token_positions[:, None] < starts[None, :] + PIC
    )
    labels = jnp.arange(starts.shape[0], dtype=jnp.int32) + 1
    return jnp.sum(jnp.where(inside, labels[None, :], 0), axis=-1) - 1


def rotary_tables(token_positions):
    half_dim = HEAD_DIM // 2
    inverse = THETA ** (-(jnp.arange(half_dim, dtype=jnp.float32) * 2.0 / HEAD_DIM))
    angles = token_positions.astype(jnp.float32)[:, None] * inverse[None, :]
    cosine, sine = jnp.cos(angles), jnp.sin(angles)
    return jnp.concatenate([cosine] * 4, axis=1), jnp.concatenate([sine, -sine] * 2, axis=1)


def body(
    tokens,
    query_weight,
    key_weight,
    value_weight,
    output_weight,
    gain_attn,
    gain_moe,
    expert_weights,
    routes,
    gate_values,
    documents,
    pic_starts,
    cotangent,
):
    _, block_len, model_width = tokens.shape
    dp_size, ctx_size = lax.axis_size("dp"), lax.axis_size("ctx")
    length = block_len * ctx_size
    offset = lax.axis_index("ctx") * block_len
    back = back_blocks(ctx_size, block_len, length)
    ahead = ahead_blocks(block_len, length, pic_starts.shape[1])
    q_width, kv_width = query_weight.shape[1], key_weight.shape[1]
    own = expert_weights.shape[0]
    x, cot = tokens[0], cotangent[0]

    joined_w = jnp.concatenate([query_weight, key_weight, value_weight], axis=1)
    gains = jnp.stack([gain_attn, gain_moe]).astype(jnp.float32)
    joined_all, gains_all, docs_all, chosen_all, gates_all = spread(
        [
            joined_w,
            gains,
            documents,
            routes.reshape(block_len * TOP // 128, 128),
            gate_values.reshape(block_len * TOP // 128, 128),
        ],
        ["dp", "dp", "ctx", "dp", "dp"],
        1,
        "spread_weights",
    )
    output_weight, joined_all = lax.optimization_barrier((output_weight, joined_all))
    output_full = lax.all_gather(output_weight, "dp", axis=1, tiled=True)
    joined_full = joined_all.reshape(model_width, -1)
    gain_rows = gains_all.transpose(1, 0, 2).reshape(2, 1, model_width)
    docs_all = docs_all.reshape(length)
    cosine, sine = rotary_tables(offset + jnp.arange(block_len, dtype=jnp.int32))
    normed_one, query, kv_all, grad_all = project(
        x, joined_full, gain_rows[0], cosine, sine, cot, q_width, back, ahead, 2
    )
    kv_all = kv_all.reshape(length, 2 * kv_width)

    pictures = picture_of(pic_starts[0], jnp.arange(length, dtype=jnp.int32))
    flags = block_flags(pic_starts[0], documents[0], docs_all, offset)
    kinfo = jnp.stack([docs_all, pictures], axis=1)
    qinfo = jnp.stack([documents[0], lax.dynamic_slice_in_dim(pictures, offset, block_len)])
    places = expert_places(
        chosen_all.reshape(dp_size, block_len, TOP), gates_all.reshape(dp_size, block_len, TOP), own
    )
    mixture, mix_full, log_total, attn_part = attend(
        flags, query, kv_all, kinfo, qinfo, output_full
    )
    hidden, rows_all = share_rows(attn_part, x, gain_rows[1], 3)
    half = own // 2
    parts, grads_one = experts(expert_weights, places, rows_all, grad_all, 0, half, None)
    expert_one = lax.psum_scatter(grads_one, "ctx", scatter_dimension=0)
    (out_part, back_part), grads_two = experts(
        expert_weights, places, rows_all, grad_all, half, own - half, parts
    )
    hidden_grad, hidden_low, mix_grad, gain_two_grad = return_grads(
        back_part, hidden, cot, gain_rows[1], output_full, 4
    )
    q_rot_grad, kv_part = attend_back(
        flags, query, kv_all, kinfo, qinfo, log_total, mix_full, mix_grad
    )
    kv_back, layer_out, output_grad = trade(
        kv_part.reshape(ctx_size, block_len, 2 * kv_width),
        out_part,
        hidden,
        hidden_low,
        mixture,
        back,
        ahead,
        5,
    )
    grads_two, kv_back = lax.optimization_barrier((grads_two, kv_back))
    expert_two = lax.psum_scatter(grads_two, "ctx", scatter_dimension=0)
    input_grad, owned, gain_sums = finish(
        q_rot_grad,
        kv_back,
        cosine,
        sine,
        normed_one,
        joined_full,
        x,
        gain_rows[0],
        hidden_grad,
        output_grad,
        gain_two_grad,
        6,
    )
    few = owned.shape[0]
    here = (lax.axis_index("dp") * ctx_size + lax.axis_index("ctx")) * few
    gain_sums = lax.dynamic_slice_in_dim(gain_sums, here, few, 1)
    expert_grad = jnp.concatenate([expert_one, expert_two], axis=0)
    v_end = q_width + 2 * kv_width
    return (
        layer_out[None],
        input_grad[None],
        owned[:, :q_width],
        owned[:, q_width : q_width + kv_width],
        owned[:, q_width + kv_width : v_end],
        owned[:, v_end:].T,
        gain_sums[0],
        gain_sums[1],
        expert_grad.astype(jnp.float32).transpose(0, 1, 3, 2),
    )


def solution(mesh):
    return jax.shard_map(
        body,
        mesh=mesh,
        in_specs=(
            P("dp", "ctx", None),
            P("dp", "tp"),
            P("dp", "tp"),
            P("dp", "tp"),
            P("tp", "dp"),
            P("dp"),
            P("dp"),
            P("dp", None, None, "tp"),
            P("dp", "ctx", None),
            P("dp", "ctx", None),
            P("dp", "ctx"),
            P("dp", None),
            P("dp", "ctx", None),
        ),
        out_specs=(
            P("dp", "ctx", None),
            P("dp", "ctx", None),
            P(("dp", "ctx"), "tp"),
            P(("dp", "ctx"), "tp"),
            P(("dp", "ctx"), "tp"),
            P("tp", ("dp", "ctx")),
            P(("dp", "ctx")),
            P(("dp", "ctx")),
            P("dp", None, "ctx", "tp"),
        ),
        check_vma=False,
    )
```

time: 533 us -> 598 us (1.12)
  waiting for transfers between devices: 4.05 us -> 149 us
  Pallas kernels: 424 us -> 382 us
  other arithmetic: 29.7 us -> 15 us
  local copies, waits for them, and re-layouts: 41.5 us -> 27.7 us
  matrix products: 13.1 us -> 0.63 us
    reduce_scatter x1 -> x2, waiting for transfers between devices: 0.01 us -> 148 us  [the longest x1 118 us: body(): expert_one = lax.psum_scatter(grads_one, 'ctx', scatter_dimension=0)]
    pallas_call x7 -> x6, Pallas kernels: 312 us -> 291 us  [the longest x1 90.4 us: finish(): pl.pallas_call(finish_kernel, name='finish', in_specs=whole_vmem(11), out...]
    pallas_call x1, Pallas kernels: 50 us -> 34.5 us  [share_rows(): pl.pallas_call(share_rows_kernel, name='share_rows', in_specs=whole_vmem(...]
    dot_general x6 -> x1, matrix products: 13.1 us -> 0.63 us  [expert_places(): jnp.einsum('rq,gqe->gre', earlier, names.astype(jnp.bfloat16), preferred_...]
    concatenate x4 -> x0, local copies, waits for them, and re-layouts: 10.7 us -> none  [the longest x3 7.7 us: body(): jnp.concatenate([joined_w_grad, output_grad, gain_one_grad[:, None], gain...]
    pallas_call x2 -> x1, Pallas kernels: 39.9 us -> 34.6 us  [spread(): pl.pallas_call(functools.partial(spread_kernel, tuple(axes_of)), name=nam...]
  transfers between devices with their start and end apart: 3 -> 3, of which waited for: 1 -> 2; matrix products, arithmetic and copies ran while one was open for 12% -> 4% of each run, Pallas kernels for 61% -> 22%
where the time goes in v4:
time: 598 us; the launch traced here: 589 us
  Pallas kernels  382 us (64%)
  waiting for transfers between devices  149 us (25%)
  local copies, waits for them, and re-layouts  27.7 us (5%)
  other arithmetic  15 us (3%)
  between operations  14.5 us (2%)
    reduce_scatter x1, waiting for transfers between devices, body(): expert_one = lax.psum_scatter(grads_one, 'ctx', scatter_dimension=0)  118 us
    pallas_call x1, Pallas kernels, finish(): pl.pallas_call(finish_kernel, name='finish', in_specs=whole_vmem(11), out...  90.4 us
    pallas_call x2, Pallas kernels, experts(): pl.pallas_call(functools.partial(experts_kernel, more), name='experts', g...  73.6 us
    pallas_call x1, Pallas kernels, trade(): pl.pallas_call(functools.partial(trade_kernel, back, ahead), name='trade'...  52.4 us
    pallas_call x1, Pallas kernels, project(): pl.pallas_call(functools.partial(project_kernel, back, ahead, q_width), n...  38.7 us
    pallas_call x1, Pallas kernels, return_grads(): pl.pallas_call(return_grads_kernel, name='return_grads', in_specs=whole_v...  36 us
    pallas_call x1, Pallas kernels, spread(): pl.pallas_call(functools.partial(spread_kernel, tuple(axes_of)), name=nam...  34.6 us
    pallas_call x1, Pallas kernels, share_rows(): pl.pallas_call(share_rows_kernel, name='share_rows', in_specs=whole_vmem(...  34.5 us
  transfers between devices with their start and end apart: 3, of which 2 were waited for; matrix products, arithmetic and copies ran while one was open for 4% of the time, Pallas kernels for 22%

profile of v4, /device:TPU:0, one launch (start us, length us, event | category | flops | bytes accessed | tf_op | source)
XLA Modules:
  0.0 589.3 jit_solution(3395156943984096989)
XLA Ops:
  7.2 0.7 stack.19
  7.9 0.7 stack.20
  8.5 0.8 copy.67
  9.4 0.8 reshape.85.refs_3_
  10.1 0.8 copy.68
  11.0 0.8 reshape.86.refs_4_
  11.7 0.6 maximum_convert_fusion.refs_1_
  12.3 1.9 pad_maximum_fusion.refs_0_
  14.3 34.6 %spread_weights.1 = (bf16[4,256,1024]{2,1,0:T(8,128)(2,1)}, f32[4,2,256]{2,1,0:T(2,128)}, s32[4,1,512]{2,1,0:T(1,128)}, s32[4,32,128]{2,1,0:T(8,128)}, f32[4,32,128]{2,1,0:T(8,128)}) custom-call(bf16[256,1024]{1,0:T(8,128)(2,1)} %pad_maximum_fusion.refs_0_, f32[2,256]{1,0:T(2,128)} %maximum_convert_fusion.refs_1_, s32[1,512]{1,0:T(1,128)} %refs_2_.1, ...), custom_call_target="tpu_custom_call" | custom-call | tf_op jit(solution)/shard_map/spread_weights/pallas_call | solution.py:320
  49.0 0.7 add_bitcast_fusion
  49.6 0.8 select_reduce_fusion
  50.4 0.7 reduce
  51.2 1.4 eq.15
  52.6 0.3 copy.73
  53.1 0.4 copy.74
  53.5 1.4 broadcast_in_dim.69
  55.4 0.6 bitcast_select_fusion
  56.3 1.0 multiply_sine_fusion
  57.3 1.3 pad_maximum_fusion.1
  58.8 1.3 copy.80.kinfo_ref
  60.2 0.7 broadcast_in_dim.72.gate_ref
  60.9 0.9 copy.79.place_ref
  61.8 0.6 fusion.15
  62.4 38.7 %project.1 = (bf16[512,1024]{1,0:T(8,128)(2,1)}, bf16[512,512]{1,0:T(8,128)(2,1)}, bf16[4,512,512]{2,1,0:T(8,128)(2,1)}, bf16[4,512,1024]{2,1,0:T(8,128)(2,1)}) custom-call(bf16[512,1024]{1,0:T(8,128)(2,1)} %bitcast.57, bf16[1024,1024]{1,0:T(8,128)(2,1)} %bitcast.62, f32[1,1024]{1,0:T(1,128)} %bitcast.77, f32[512,128]{1,0:T(8,128)} %get-tuple-element.149.cos_ref, ...), custom_call_target="tpu_custom_call" | custom-call | tf_op jit(solution)/shard_map/project/pallas_call | solution.py:491
  101.1 0.6 fusion.17
  101.8 1.3 fusion.10
  103.1 0.6 pad_add_fusion.2.flags
  103.7 0.6 pad_add_fusion.1.qinfo_ref
  104.3 1.7 fusion.13
  106.0 10.4 %attend.1 = (bf16[512,512]{1,0:T(8,128)(2,1)}, f32[512,512]{1,0:T(8,128)}, f32[8,512]{1,0:T(8,128)}, bf16[512,1024]{1,0:T(8,128)(2,1)}) custom-call(s32[9]{0:T(128)} %pad_add_fusion.2.flags, bf16[512,512]{1,0:T(8,128)(2,1)} %get-tuple-element.50.q_ref, bf16[2048,512]{1,0:T(8,128)(2,1)} %bitcast.60, s32[2048,2]{1,0:T(8,128)} %copy.80.kinfo_ref, ...), custom_call_target="tpu_custom_call" | custom-call | tf_op jit(solution)/shard_map/attend/pallas_call | solution.py:148
  116.4 34.5 %share_rows.1 = (f32[512,1024]{1,0:T(8,128)}, bf16[4,512,1024]{2,1,0:T(8,128)(2,1)}) custom-call(bf16[512,1024]{1,0:T(8,128)(2,1)} %get-tuple-element.55.part_ref, bf16[512,1024]{1,0:T(8,128)(2,1)} %bitcast.58, f32[1,1024]{1,0:T(1,128)} %bitcast.75), custom_call_target="tpu_custom_call" | custom-call | tf_op jit(solution)/shard_map/share_rows/pallas_call | solution.py:545
  150.9 35.6 %experts.2 = (bf16[4,512,1024]{2,1,0:T(8,128)(2,1)}, bf16[4,512,1024]{2,1,0:T(8,128)(2,1)}, bf16[1,4,4,3,256,256]{5,4,3,2,1,0:T(8,128)(2,1)}) custom-call(bf16[4,512,1024]{2,1,0:T(8,128)(2,1)} %get-tuple-element.56.rows_ref, bf16[4,512,1024]{2,1,0:T(8,128)(2,1)} %get-tuple-element.57.grads_ref, bf16[8,3,1024,256]{3,2,1,0:T(8,128)(2,1)} %weights_ref.3, ...), custom_call_target="tpu_custom_call" | custom-call | flops 20535312384 | bytes 25165824 | tf_op jit(solution)/shard_map/experts/pallas_call | solution.py:1061
  186.5 38.0 %experts.3 = (bf16[4,512,1024]{2,1,0:T(8,128)(2,1)}, bf16[4,512,1024]{2,1,0:T(8,128)(2,1)}, bf16[1,4,4,3,256,256]{5,4,3,2,1,0:T(8,128)(2,1)}) custom-call(bf16[4,512,1024]{2,1,0:T(8,128)(2,1)} %get-tuple-element.56.rows_ref, bf16[4,512,1024]{2,1,0:T(8,128)(2,1)} %get-tuple-element.57.grads_ref, bf16[8,3,1024,256]{3,2,1,0:T(8,128)(2,1)} %weights_ref.3, ...), custom_call_target="tpu_custom_call" | custom-call | flops 20535312384 | bytes 25165824 | tf_op jit(solution)/shard_map/experts/pallas_call | solution.py:1061
  224.6 36.0 %return_grads.1 = (f32[512,1024]{1,0:T(8,128)}, bf16[512,1024]{1,0:T(8,128)(2,1)}, bf16[512,512]{1,0:T(8,128)(2,1)}, f32[1,1024]{1,0:T(1,128)}) custom-call(bf16[4,512,1024]{2,1,0:T(8,128)(2,1)} %get-tuple-element.62.part_ref, f32[512,1024]{1,0:T(8,128)} %get-tuple-element.63.hidden_ref, bf16[512,1024]{1,0:T(8,128)(2,1)} %bitcast.67, f32[1,1024]{1,0:T(1,128)} %bitcast.76, ...), custom_call_target="tpu_custom_call" | custom-call | tf_op jit(solution)/shard_map/return_grads/pallas_call | solution.py:665
  260.5 11.8 %attend_back.1 = (f32[512,512]{1,0:T(8,128)}, bf16[2048,512]{1,0:T(8,128)(2,1)}) custom-call(s32[9]{0:T(128)} %pad_add_fusion.2.flags, bf16[512,512]{1,0:T(8,128)(2,1)} %get-tuple-element.50.q_ref, bf16[2048,512]{1,0:T(8,128)(2,1)} %bitcast.61, s32[2048,2]{1,0:T(8,128)} %copy.80.kinfo_ref, s32[2,512]{1,0:T(2,128)} %pad_add_fusion.1.qinfo_ref, ...), custom_call_target="tpu_custom_call" | custom-call | tf_op jit(solution)/shard_map/attend_back/pallas_call | solution.py:170
  272.4 52.4 %trade.1 = (f32[512,512]{1,0:T(8,128)}, bf16[512,1024]{1,0:T(8,128)(2,1)}, bf16[4,256,512]{2,1,0:T(8,128)(2,1)}) custom-call(bf16[4,512,512]{2,1,0:T(8,128)(2,1)} %bitcast.68, bf16[4,512,1024]{2,1,0:T(8,128)(2,1)} %get-tuple-element.66.part_ref, f32[512,1024]{1,0:T(8,128)} %get-tuple-element.63.hidden_ref, bf16[512,1024]{1,0:T(8,128)(2,1)} %get-tuple-element.67.low_ref, ...), custom_call_target="tpu_custom_call" | custom-call | tf_op jit(solution)/shard_map/trade/pallas_call | solution.py:774
  324.8 0.7 reduce-scatter.3.cloned.1.call-update
  325.5 90.4 %finish.1 = (bf16[512,1024]{1,0:T(8,128)(2,1)}, f32[64,1536]{1,0:T(8,128)}, f32[8,1024]{1,0:T(8,128)}) custom-call(f32[512,512]{1,0:T(8,128)} %get-tuple-element.70.dq_ref, f32[512,512]{1,0:T(8,128)} %get-tuple-element.73.dkv_ref, f32[512,128]{1,0:T(8,128)} %get-tuple-element.149.cos_ref, f32[512,128]{1,0:T(8,128)} %get-tuple-element.150.sin_ref, ...), custom_call_target="tpu_custom_call" | custom-call | tf_op jit(solution)/shard_map/finish/pallas_call | solution.py:919
  415.9 0.8 constant_dynamic-slice_fusion
  416.6 0.5 slice_bitcast_fusion.1
  417.1 1.5 fusion.14
  418.7 1.7 slice_bitcast_fusion
  420.4 30.7 %reduce-scatter.5.cloned.1.call-done = bf16[1,4,3,256,256]{4,3,2,1,0:T(8,128)(2,1)} async-done(((bf16[4,4,3,256,256]{4,3,2,1,0:T(8,128)(2,1)}), bf16[1,4,3,256,256]{4,3,2,1,0:T(8,128)(2,1)}) %reduce-scatter.5.cloned.1.call-update) | async-done | bytes 1572880 | tf_op jit(solution)/shard_map/reduce_scatter | solution.py:1210
  451.0 117.7 %reduce-scatter.3.cloned.1.call-done = bf16[1,4,3,256,256]{4,3,2,1,0:T(8,128)(2,1)} async-done(((bf16[4,4,3,256,256]{4,3,2,1,0:T(8,128)(2,1)}), bf16[1,4,3,256,256]{4,3,2,1,0:T(8,128)(2,1)}) %reduce-scatter.3.cloned.1.call-update) | async-done | bytes 1572880 | tf_op jit(solution)/shard_map/reduce_scatter | solution.py:1189
  568.7 4.9 convert_bitcast_fusion
  573.7 6.7 %copy.81 = f32[8,3,256,256]{3,2,1,0:T(8,128)} copy(f32[8,3,256,256]{2,3,1,0:T(8,128)} %convert_bitcast_fusion) | data formatting | bytes 12582912
  580.4 1.0 copy.87
  581.3 1.0 copy.88
  (37 shorter events, 1.4 us)
Async XLA Ops:
  7.2 98.8 %all-gather.2.cloned.1.call-start = ((), (), s32[]{:S(2)}) async-start(), calls=%async_computation.2 | async-start | bytes 1310720 | tf_op jit(solution)/shard_map/all_gather | solution.py:1166
  48.9 402.2 %reduce-scatter.5.cloned.1.call-start = ((), (), s32[]{:S(2)}) async-start(), calls=%async_computation.4 | async-start | bytes 7864320 | tf_op jit(solution)/shard_map/reduce_scatter | solution.py:1210
  53.5 3.7 copy-start.2
  56.0 5.8 copy-start.4
  57.3 43.8 %copy-start.3 = (s32[1,512]{1,0:T(1,128)S(1)}, s32[1,512]{1,0:T(1,128)}, u32[]{:S(2)}) copy-start(s32[1,512]{1,0:T(1,128)} %refs_2_.1) | copy-start | bytes 6148
  57.3 44.4 %copy-start.5 = (s32[1,4]{1,0:T(1,128)S(1)}, s32[1,4]{1,0:T(1,128)}, u32[]{:S(2)}) copy-start(s32[1,4]{1,0:T(1,128)} %param.24) | copy-start | bytes 52
  324.8 243.9 %reduce-scatter.3.cloned.1.call-start = ((), (), s32[]{:S(2)}) async-start(), calls=%async_computation.3 | async-start | bytes 7864320 | tf_op jit(solution)/shard_map/reduce_scatter | solution.py:1189
  573.7 6.7 %copy-start = (bf16[512,1024]{1,0:T(8,128)(2,1)S(1)}, bf16[512,1024]{1,0:T(8,128)(2,1)}, u32[]{:S(2)}) copy-start(bf16[512,1024]{1,0:T(8,128)(2,1)} %get-tuple-element.69) | copy-start | bytes 3145732
  573.7 7.7 %copy-start.1 = (bf16[512,1024]{1,0:T(8,128)(2,1)S(1)}, bf16[512,1024]{1,0:T(8,128)(2,1)}, u32[]{:S(2)}) copy-start(bf16[512,1024]{1,0:T(8,128)(2,1)} %get-tuple-element.78) | copy-start | bytes 3145732
Sparse Core Ops, SparseCore 0:
  49.0 41.0 all-gather.1
  324.9 126.1 reduce-scatter.4
  453.9 114.7 reduce-scatter.2

commit v5 on v4

--- a/solution.py
+++ b/solution.py
@@ -200,15 +200,6 @@
 
 
 MESH = pl.DeviceIdType.MESH
-TN = (((0,), (0,)), ((), ()))
-
-
-def place_on(axes):
-    index, size = 0, 1
-    for axis in axes:
-        index = index * lax.axis_size(axis) + lax.axis_index(axis)
-        size *= lax.axis_size(axis)
-    return index, size
 
 
 def greet(axes_list, line=False):
@@ -315,11 +306,10 @@
         each(lax.axis_size(axes_of[i]), lambda k, i=i: copy(i, k).wait())
 
 
-def spread(arrays, axes_of, ident, name):
+def spread(arrays, axes_of, ident):
     sizes = [lax.axis_size(axis) for axis in axes_of]
     return pl.pallas_call(
         functools.partial(spread_kernel, tuple(axes_of)),
-        name=name,
         in_specs=whole_vmem(len(arrays)),
         out_specs=whole_vmem(len(arrays)),
         out_shape=[
@@ -515,7 +505,6 @@
 ):
     mine, theirs = halves(part_ref.shape[0])
     greet(["dp", "tp"])
-    size = lax.axis_size("dp")
     rows_of = RowGather(normed, all_ref, (dp_send, dp_recv), (tp_send, tp_recv), 1)
     first = remote(part_ref.at[theirs], held.at[theirs], (tp_send, tp_recv), 0, other_core())
     second = remote(part_ref.at[mine], held.at[mine], (tp_send, tp_recv), 1, other_core())
@@ -960,7 +949,7 @@
     before, refs = (refs[:2], refs[2:]) if more else (None, refs)
     out_ref, back_ref, weight_grad_ref, slots, slot_grads, outs, backs = refs
     e = pl.program_id(1)
-    groups, tok_rows, model_width = rows_ref.shape
+    groups, tok_rows, _ = rows_ref.shape
     owners, part = weight_grad_ref.shape[1], weight_grad_ref.shape[5]
     slot_index = lax.broadcasted_iota(jnp.int32, (CAP, tok_rows), 0)
     gates = []
@@ -1160,7 +1149,6 @@
         ],
         ["dp", "dp", "ctx", "dp", "dp"],
         1,
-        "spread_weights",
     )
     output_weight, joined_all = lax.optimization_barrier((output_weight, joined_all))
     output_full = lax.all_gather(output_weight, "dp", axis=1, tiled=True)

time: 598 us -> 594 us (level)
  no operation moved by 1% of the time
where the time goes in v5:
time: 594 us; the launch traced here: 589 us
  Pallas kernels  383 us (64%)
  waiting for transfers between devices  149 us (25%)
  local copies, waits for them, and re-layouts  27.7 us (5%)
  other arithmetic  15 us (3%)
  between operations  14.3 us (2%)
    reduce_scatter x1, waiting for transfers between devices, body(): expert_one = lax.psum_scatter(grads_one, 'ctx', scatter_dimension=0)  118 us
    pallas_call x1, Pallas kernels, finish(): pl.pallas_call(finish_kernel, name='finish', in_specs=whole_vmem(11), out...  91.2 us
    pallas_call x2, Pallas kernels, experts(): pl.pallas_call(functools.partial(experts_kernel, more), name='experts', g...  74 us
    pallas_call x1, Pallas kernels, trade(): pl.pallas_call(functools.partial(trade_kernel, back, ahead), name='trade'...  51.6 us
    pallas_call x1, Pallas kernels, project(): pl.pallas_call(functools.partial(project_kernel, back, ahead, q_width), n...  38.4 us
    pallas_call x1, Pallas kernels, return_grads(): pl.pallas_call(return_grads_kernel, name='return_grads', in_specs=whole_v...  36 us
    pallas_call x1, Pallas kernels, spread(): pl.pallas_call(functools.partial(spread_kernel, tuple(axes_of)), in_specs...  34.6 us
    pallas_call x1, Pallas kernels, share_rows(): pl.pallas_call(share_rows_kernel, name='share_rows', in_specs=whole_vmem(...  34.5 us
  transfers between devices with their start and end apart: 3, of which 2 were waited for; matrix products, arithmetic and copies ran while one was open for 4% of the time, Pallas kernels for 22%

profile of v5, /device:TPU:0, one launch (start us, length us, event | category | flops | bytes accessed | tf_op | source)
XLA Modules:
  0.0 589.4 jit_solution(3395156943984096989)
XLA Ops:
  7.2 0.7 stack.19
  7.9 0.7 stack.20
  8.5 0.8 copy.67
  9.4 0.8 reshape.85.refs_3_
  10.1 0.8 copy.68
  11.0 0.8 reshape.86.refs_4_
  11.7 0.6 maximum_convert_fusion.refs_1_
  12.3 1.9 pad_maximum_fusion.refs_0_
  14.3 34.6 %shard_map.196 = (bf16[4,256,1024]{2,1,0:T(8,128)(2,1)}, f32[4,2,256]{2,1,0:T(2,128)}, s32[4,1,512]{2,1,0:T(1,128)}, s32[4,32,128]{2,1,0:T(8,128)}, f32[4,32,128]{2,1,0:T(8,128)}) custom-call(bf16[256,1024]{1,0:T(8,128)(2,1)} %pad_maximum_fusion.refs_0_, f32[2,256]{1,0:T(2,128)} %maximum_convert_fusion.refs_1_, s32[1,512]{1,0:T(1,128)} %refs_2_.1, ...), custom_call_target="tpu_custom_call" | custom-call | tf_op jit(solution)/shard_map/pallas_call | solution.py:311
  49.0 0.7 add_bitcast_fusion
  49.6 0.8 select_reduce_fusion
  50.4 0.7 reduce
  51.2 1.4 eq.15
  52.6 0.3 copy.73
  53.1 0.4 copy.74
  53.5 1.4 broadcast_in_dim.69
  55.4 0.6 bitcast_select_fusion
  56.3 1.0 multiply_sine_fusion
  57.3 1.3 pad_maximum_fusion.1
  58.8 1.3 copy.80.kinfo_ref
  60.2 0.7 broadcast_in_dim.72.gate_ref
  60.9 0.9 copy.79.place_ref
  61.8 0.6 fusion.15
  62.4 38.4 %project.1 = (bf16[512,1024]{1,0:T(8,128)(2,1)}, bf16[512,512]{1,0:T(8,128)(2,1)}, bf16[4,512,512]{2,1,0:T(8,128)(2,1)}, bf16[4,512,1024]{2,1,0:T(8,128)(2,1)}) custom-call(bf16[512,1024]{1,0:T(8,128)(2,1)} %bitcast.57, bf16[1024,1024]{1,0:T(8,128)(2,1)} %bitcast.62, f32[1,1024]{1,0:T(1,128)} %bitcast.77, f32[512,128]{1,0:T(8,128)} %get-tuple-element.149.cos_ref, ...), custom_call_target="tpu_custom_call" | custom-call | tf_op jit(solution)/shard_map/project/pallas_call | solution.py:481
  100.8 0.6 fusion.17
  101.5 1.3 fusion.10
  102.8 0.6 pad_add_fusion.2.flags
  103.4 0.6 pad_add_fusion.1.qinfo_ref
  104.0 1.7 fusion.13
  105.7 10.4 %attend.1 = (bf16[512,512]{1,0:T(8,128)(2,1)}, f32[512,512]{1,0:T(8,128)}, f32[8,512]{1,0:T(8,128)}, bf16[512,1024]{1,0:T(8,128)(2,1)}) custom-call(s32[9]{0:T(128)} %pad_add_fusion.2.flags, bf16[512,512]{1,0:T(8,128)(2,1)} %get-tuple-element.50.q_ref, bf16[2048,512]{1,0:T(8,128)(2,1)} %bitcast.60, s32[2048,2]{1,0:T(8,128)} %copy.80.kinfo_ref, ...), custom_call_target="tpu_custom_call" | custom-call | tf_op jit(solution)/shard_map/attend/pallas_call | solution.py:148
  116.1 34.5 %share_rows.1 = (f32[512,1024]{1,0:T(8,128)}, bf16[4,512,1024]{2,1,0:T(8,128)(2,1)}) custom-call(bf16[512,1024]{1,0:T(8,128)(2,1)} %get-tuple-element.55.part_ref, bf16[512,1024]{1,0:T(8,128)(2,1)} %bitcast.58, f32[1,1024]{1,0:T(1,128)} %bitcast.75), custom_call_target="tpu_custom_call" | custom-call | tf_op jit(solution)/shard_map/share_rows/pallas_call | solution.py:534
  150.7 36.0 %experts.2 = (bf16[4,512,1024]{2,1,0:T(8,128)(2,1)}, bf16[4,512,1024]{2,1,0:T(8,128)(2,1)}, bf16[1,4,4,3,256,256]{5,4,3,2,1,0:T(8,128)(2,1)}) custom-call(bf16[4,512,1024]{2,1,0:T(8,128)(2,1)} %get-tuple-element.56.rows_ref, bf16[4,512,1024]{2,1,0:T(8,128)(2,1)} %get-tuple-element.57.grads_ref, bf16[8,3,1024,256]{3,2,1,0:T(8,128)(2,1)} %weights_ref.3, ...), custom_call_target="tpu_custom_call" | custom-call | flops 20535312384 | bytes 25165824 | tf_op jit(solution)/shard_map/experts/pallas_call | solution.py:1050
  186.7 38.0 %experts.3 = (bf16[4,512,1024]{2,1,0:T(8,128)(2,1)}, bf16[4,512,1024]{2,1,0:T(8,128)(2,1)}, bf16[1,4,4,3,256,256]{5,4,3,2,1,0:T(8,128)(2,1)}) custom-call(bf16[4,512,1024]{2,1,0:T(8,128)(2,1)} %get-tuple-element.56.rows_ref, bf16[4,512,1024]{2,1,0:T(8,128)(2,1)} %get-tuple-element.57.grads_ref, bf16[8,3,1024,256]{3,2,1,0:T(8,128)(2,1)} %weights_ref.3, ...), custom_call_target="tpu_custom_call" | custom-call | flops 20535312384 | bytes 25165824 | tf_op jit(solution)/shard_map/experts/pallas_call | solution.py:1050
  224.7 36.0 %return_grads.1 = (f32[512,1024]{1,0:T(8,128)}, bf16[512,1024]{1,0:T(8,128)(2,1)}, bf16[512,512]{1,0:T(8,128)(2,1)}, f32[1,1024]{1,0:T(1,128)}) custom-call(bf16[4,512,1024]{2,1,0:T(8,128)(2,1)} %get-tuple-element.62.part_ref, f32[512,1024]{1,0:T(8,128)} %get-tuple-element.63.hidden_ref, bf16[512,1024]{1,0:T(8,128)(2,1)} %bitcast.67, f32[1,1024]{1,0:T(1,128)} %bitcast.76, ...), custom_call_target="tpu_custom_call" | custom-call | tf_op jit(solution)/shard_map/return_grads/pallas_call | solution.py:654
  260.6 11.8 %attend_back.1 = (f32[512,512]{1,0:T(8,128)}, bf16[2048,512]{1,0:T(8,128)(2,1)}) custom-call(s32[9]{0:T(128)} %pad_add_fusion.2.flags, bf16[512,512]{1,0:T(8,128)(2,1)} %get-tuple-element.50.q_ref, bf16[2048,512]{1,0:T(8,128)(2,1)} %bitcast.61, s32[2048,2]{1,0:T(8,128)} %copy.80.kinfo_ref, s32[2,512]{1,0:T(2,128)} %pad_add_fusion.1.qinfo_ref, ...), custom_call_target="tpu_custom_call" | custom-call | tf_op jit(solution)/shard_map/attend_back/pallas_call | solution.py:170
  272.5 51.6 %trade.1 = (f32[512,512]{1,0:T(8,128)}, bf16[512,1024]{1,0:T(8,128)(2,1)}, bf16[4,256,512]{2,1,0:T(8,128)(2,1)}) custom-call(bf16[4,512,512]{2,1,0:T(8,128)(2,1)} %bitcast.68, bf16[4,512,1024]{2,1,0:T(8,128)(2,1)} %get-tuple-element.66.part_ref, f32[512,1024]{1,0:T(8,128)} %get-tuple-element.63.hidden_ref, bf16[512,1024]{1,0:T(8,128)(2,1)} %get-tuple-element.67.low_ref, ...), custom_call_target="tpu_custom_call" | custom-call | tf_op jit(solution)/shard_map/trade/pallas_call | solution.py:763
  324.2 0.7 reduce-scatter.3.cloned.1.call-update
  324.9 91.2 %finish.1 = (bf16[512,1024]{1,0:T(8,128)(2,1)}, f32[64,1536]{1,0:T(8,128)}, f32[8,1024]{1,0:T(8,128)}) custom-call(f32[512,512]{1,0:T(8,128)} %get-tuple-element.70.dq_ref, f32[512,512]{1,0:T(8,128)} %get-tuple-element.73.dkv_ref, f32[512,128]{1,0:T(8,128)} %get-tuple-element.149.cos_ref, f32[512,128]{1,0:T(8,128)} %get-tuple-element.150.sin_ref, ...), custom_call_target="tpu_custom_call" | custom-call | tf_op jit(solution)/shard_map/finish/pallas_call | solution.py:908
  416.1 0.8 constant_dynamic-slice_fusion
  416.9 0.5 slice_bitcast_fusion.1
  417.4 1.5 fusion.14
  418.9 1.7 slice_bitcast_fusion
  420.6 30.7 %reduce-scatter.5.cloned.1.call-done = bf16[1,4,3,256,256]{4,3,2,1,0:T(8,128)(2,1)} async-done(((bf16[4,4,3,256,256]{4,3,2,1,0:T(8,128)(2,1)}), bf16[1,4,3,256,256]{4,3,2,1,0:T(8,128)(2,1)}) %reduce-scatter.5.cloned.1.call-update) | async-done | bytes 1572880 | tf_op jit(solution)/shard_map/reduce_scatter | solution.py:1198
  451.3 117.7 %reduce-scatter.3.cloned.1.call-done = bf16[1,4,3,256,256]{4,3,2,1,0:T(8,128)(2,1)} async-done(((bf16[4,4,3,256,256]{4,3,2,1,0:T(8,128)(2,1)}), bf16[1,4,3,256,256]{4,3,2,1,0:T(8,128)(2,1)}) %reduce-scatter.3.cloned.1.call-update) | async-done | bytes 1572880 | tf_op jit(solution)/shard_map/reduce_scatter | solution.py:1177
  569.0 4.9 convert_bitcast_fusion
  573.9 6.7 %copy.81 = f32[8,3,256,256]{3,2,1,0:T(8,128)} copy(f32[8,3,256,256]{2,3,1,0:T(8,128)} %convert_bitcast_fusion) | data formatting | bytes 12582912
  580.6 1.0 copy.87
  581.6 1.0 copy.88
  (37 shorter events, 1.4 us)
Async XLA Ops:
  7.2 98.6 %all-gather.2.cloned.1.call-start = ((), (), s32[]{:S(2)}) async-start(), calls=%async_computation.2 | async-start | bytes 1310720 | tf_op jit(solution)/shard_map/all_gather | solution.py:1154
  48.9 402.4 %reduce-scatter.5.cloned.1.call-start = ((), (), s32[]{:S(2)}) async-start(), calls=%async_computation.4 | async-start | bytes 7864320 | tf_op jit(solution)/shard_map/reduce_scatter | solution.py:1198
  53.5 3.7 copy-start.2
  56.0 5.8 copy-start.4
  57.3 43.5 %copy-start.3 = (s32[1,512]{1,0:T(1,128)S(1)}, s32[1,512]{1,0:T(1,128)}, u32[]{:S(2)}) copy-start(s32[1,512]{1,0:T(1,128)} %refs_2_.1) | copy-start | bytes 6148
  57.3 44.1 %copy-start.5 = (s32[1,4]{1,0:T(1,128)S(1)}, s32[1,4]{1,0:T(1,128)}, u32[]{:S(2)}) copy-start(s32[1,4]{1,0:T(1,128)} %param.24) | copy-start | bytes 52
  324.1 244.8 %reduce-scatter.3.cloned.1.call-start = ((), (), s32[]{:S(2)}) async-start(), calls=%async_computation.3 | async-start | bytes 7864320 | tf_op jit(solution)/shard_map/reduce_scatter | solution.py:1177
  573.9 6.7 %copy-start = (bf16[512,1024]{1,0:T(8,128)(2,1)S(1)}, bf16[512,1024]{1,0:T(8,128)(2,1)}, u32[]{:S(2)}) copy-start(bf16[512,1024]{1,0:T(8,128)(2,1)} %get-tuple-element.69) | copy-start | bytes 3145732
  573.9 7.7 %copy-start.1 = (bf16[512,1024]{1,0:T(8,128)(2,1)S(1)}, bf16[512,1024]{1,0:T(8,128)(2,1)}, u32[]{:S(2)}) copy-start(bf16[512,1024]{1,0:T(8,128)(2,1)} %get-tuple-element.78) | copy-start | bytes 3145732
Sparse Core Ops, SparseCore 0:
  49.0 40.8 all-gather.1
  324.3 127.0 reduce-scatter.4
  454.2 114.7 reduce-scatter.2

commit v6 on v5

--- a/solution.py
+++ b/solution.py
@@ -8,7 +8,6 @@
 from jax.sharding import PartitionSpec as P
 
 HEAD_DIM = 64
-TOP = 8
 PIC = 256
 CAP = 144
 
@@ -19,158 +18,156 @@
 
 KEY_ROWS = 256
 NT = (((1,), (1,)), ((), ()))
-LIMIT = 60 * 1024 * 1024
-
-
-def seen_bias(flags, j, blocks, kinfo_ref, qinfo_ref):
-    rows = pl.ds(pl.multiple_of(j * KEY_ROWS, KEY_ROWS), KEY_ROWS)
-    q_doc, q_pic = qinfo_ref[0:1, :], qinfo_ref[1:2, :]
-    k_doc, k_pic = kinfo_ref[rows, 0:1], kinfo_ref[rows, 1:2]
-    q_place = flags[blocks] + lax.broadcasted_iota(jnp.int32, q_doc.shape, 1)
-    k_place = j * KEY_ROWS + lax.broadcasted_iota(jnp.int32, k_doc.shape, 0)
-    seen = (k_doc == q_doc) & ((k_place <= q_place) | ((k_pic == q_pic) & (q_pic >= 0)))
-    return rows, jnp.where(seen, 0.0, NEG_FILL)
-
-
-def attend_kernel(
-    flags, q_ref, kv_ref, kinfo_ref, qinfo_ref, out_w_ref, mix_ref, full_ref, log_ref, part_ref,
-    acc, top, total,
-):
-    blocks = kv_ref.shape[0] // KEY_ROWS
+LIMIT = 63 * 1024 * 1024
+
+
+def whole_vmem(count):
+    return [pl.BlockSpec(memory_space=pltpu.VMEM)] * count
+
+
+def picture_ids(starts_ref, places):
+    ids = jnp.full(places.shape, -1, jnp.int32)
+    for j in range(starts_ref.shape[1]):
+        start = starts_ref[0, j]
+        ids += jnp.where((places >= start) & (places < start + PIC), j + 1, 0)
+    return ids
+
+
+def as_column(row):
+    tall = jnp.broadcast_to(row.astype(jnp.float32), (8, row.shape[1]))
+    return jnp.transpose(tall)[:, 0:1].astype(jnp.int32)
+
+
+class Masks:
+    def __init__(self, docs_ref, starts_ref, column):
+        self.docs_ref, self.starts_ref, self.column = docs_ref, starts_ref, column
+        self.rows = docs_ref.shape[2]
+        me = lax.axis_index("ctx")
+        self.q_doc = docs_ref[me]
+        self.q_place = me * self.rows + lax.broadcasted_iota(jnp.int32, (1, self.rows), 1)
+        self.q_pic = picture_ids(starts_ref, self.q_place)
+
+    def open(self, block):
+        self.column[...] = jnp.broadcast_to(
+            as_column(self.docs_ref[block]), self.column.shape
+        )
+
+    def bias(self, block, rows, first):
+        k_doc = self.column[rows, 0:1]
+        k_place = block * self.rows + first + lax.broadcasted_iota(jnp.int32, k_doc.shape, 0)
+        k_pic = picture_ids(self.starts_ref, k_place)
+        seen = (k_doc == self.q_doc) & (
+            (k_place <= self.q_place) | ((k_pic == self.q_pic) & (self.q_pic >= 0))
+        )
+        return jnp.where(seen, 0.0, NEG_FILL)
+
+
+def attend_block(masks, block, q_ref, kv_ref, acc, top, total):
     kv_width = kv_ref.shape[1] // 2
     heads, kv_heads = q_ref.shape[1] // HEAD_DIM, kv_width // HEAD_DIM
-    top[...] = jnp.full(top.shape, NEG_FILL, jnp.float32)
-    total[...] = jnp.zeros(total.shape, jnp.float32)
-    acc[...] = jnp.zeros(acc.shape, jnp.float32)
+    masks.open(block)
 
     def step(j, carry):
-        @pl.when(flags[j] > 0)
-        def _():
-            rows, bias = seen_bias(flags, j, blocks, kinfo_ref, qinfo_ref)
-            for g in range(kv_heads):
-                key = kv_ref[rows, g * HEAD_DIM : (g + 1) * HEAD_DIM]
-                val = kv_ref[rows, kv_width + g * HEAD_DIM : kv_width + (g + 1) * HEAD_DIM]
-                val_t = jnp.transpose(val.astype(jnp.float32)).astype(jnp.bfloat16)
-                for h in range(g * heads // kv_heads, (g + 1) * heads // kv_heads):
-                    at = slice(h * HEAD_DIM, (h + 1) * HEAD_DIM)
-                    scores = bias + lax.dot_general(
-                        key, q_ref[:, at], NT, preferred_element_type=jnp.float32
-                    )
-                    old = top[h : h + 1, :]
-                    new = jnp.maximum(old, jnp.max(scores, axis=0, keepdims=True))
-                    probs = jnp.exp(scores - new)
-                    fade = jnp.exp(old - new)
-                    total[h : h + 1, :] = total[h : h + 1, :] * fade + jnp.sum(
-                        probs, axis=0, keepdims=True
-                    )
-                    acc[at, :] = acc[at, :] * fade + jnp.dot(
-                        val_t, probs.astype(jnp.bfloat16), preferred_element_type=jnp.float32
-                    )
-                    top[h : h + 1, :] = new
-
+        first = pl.multiple_of(j * KEY_ROWS, KEY_ROWS)
+        rows = pl.ds(first, KEY_ROWS)
+        bias = masks.bias(block, rows, first)
+        for g in range(kv_heads):
+            key = kv_ref[rows, g * HEAD_DIM : (g + 1) * HEAD_DIM]
+            val = kv_ref[rows, kv_width + g * HEAD_DIM : kv_width + (g + 1) * HEAD_DIM]
+            val_t = jnp.transpose(val.astype(jnp.float32)).astype(jnp.bfloat16)
+            for h in range(g * heads // kv_heads, (g + 1) * heads // kv_heads):
+                at = slice(h * HEAD_DIM, (h + 1) * HEAD_DIM)
+                scores = bias + lax.dot_general(
+                    key, q_ref[:, at], NT, preferred_element_type=jnp.float32
+                )
+                old = top[h : h + 1, :]
+                new = jnp.maximum(old, jnp.max(scores, axis=0, keepdims=True))
+                probs = jnp.exp(scores - new)
+                fade = jnp.exp(old - new)
+                total[h : h + 1, :] = total[h : h + 1, :] * fade + jnp.sum(
+                    probs, axis=0, keepdims=True
+                )
+                acc[at, :] = acc[at, :] * fade + jnp.dot(
+                    val_t, probs.astype(jnp.bfloat16), preferred_element_type=jnp.float32
+                )
+                top[h : h + 1, :] = new
         return carry
 
-    lax.fori_loop(0, blocks, step, 0)
-    log_ref[...] = top[...] + jnp.log(total[...])
-    for h in range(heads):
-        at = slice(h * HEAD_DIM, (h + 1) * HEAD_DIM)
-        acc[at, :] = acc[at, :] / total[h : h + 1, :]
-    full = jnp.transpose(acc[...])
-    full_ref[...] = full
-    mix_ref[...] = full.astype(jnp.bfloat16)
-    part_ref[...] = jnp.dot(
-        mix_ref[...], out_w_ref[...], preferred_element_type=jnp.float32
-    ).astype(jnp.bfloat16)
-
-
-def attend_back_kernel(
-    flags, q_ref, kv_ref, kinfo_ref, qinfo_ref, log_ref, full_ref, grad_ref, dq_ref, dkv_ref,
-    acc, delta,
-):
-    blocks = kv_ref.shape[0] // KEY_ROWS
+    lax.fori_loop(0, kv_ref.shape[0] // KEY_ROWS, step, 0)
+
+
+def attend_back_block(masks, block, q_ref, kv_ref, log_ref, delta, grad_ref, acc, dkv_ref):
     kv_width = kv_ref.shape[1] // 2
     heads, kv_heads = q_ref.shape[1] // HEAD_DIM, kv_width // HEAD_DIM
+    masks.open(block)
+
+    def step(j, carry):
+        first = pl.multiple_of(j * KEY_ROWS, KEY_ROWS)
+        rows = pl.ds(first, KEY_ROWS)
+        bias = masks.bias(block, rows, first)
+        for g in range(kv_heads):
+            k_at = slice(g * HEAD_DIM, (g + 1) * HEAD_DIM)
+            v_at = slice(kv_width + g * HEAD_DIM, kv_width + (g + 1) * HEAD_DIM)
+            key, val = kv_ref[rows, k_at], kv_ref[rows, v_at]
+            key_t = jnp.transpose(key.astype(jnp.float32)).astype(jnp.bfloat16)
+            dk = jnp.zeros((KEY_ROWS, HEAD_DIM), jnp.float32)
+            dv = jnp.zeros((KEY_ROWS, HEAD_DIM), jnp.float32)
+            for h in range(g * heads // kv_heads, (g + 1) * heads // kv_heads):
+                at = slice(h * HEAD_DIM, (h + 1) * HEAD_DIM)
+                q_rows, g_rows = q_ref[:, at], grad_ref[:, at]
+                scores = bias + lax.dot_general(
+                    key, q_rows, NT, preferred_element_type=jnp.float32
+                )
+                probs = jnp.exp(scores - log_ref[h : h + 1, :])
+                prob_grad = lax.dot_general(val, g_rows, NT, preferred_element_type=jnp.float32)
+                slope = (probs * (prob_grad - delta[h : h + 1, :])).astype(jnp.bfloat16)
+                dv += jnp.dot(
+                    probs.astype(jnp.bfloat16), g_rows, preferred_element_type=jnp.float32
+                )
+                dk += jnp.dot(slope, q_rows, preferred_element_type=jnp.float32)
+                acc[at, :] += jnp.dot(key_t, slope, preferred_element_type=jnp.float32)
+            dkv_ref[rows, k_at] = dk.astype(dkv_ref.dtype)
+            dkv_ref[rows, v_at] = dv.astype(dkv_ref.dtype)
+        return carry
+
+    lax.fori_loop(0, kv_ref.shape[0] // KEY_ROWS, step, 0)
+
+
+def attend_back_kernel(
+    back, ahead, starts_ref, q_ref, kv_ref, docs_ref, log_ref, full_ref, grad_ref, dq_ref,
+    dkv_ref, acc, delta, column,
+):
+    me, size = lax.axis_index("ctx"), lax.axis_size("ctx")
     acc[...] = jnp.transpose(full_ref[...] * grad_ref[...].astype(jnp.float32))
-    for h in range(heads):
+    for h in range(delta.shape[0]):
         delta[h : h + 1, :] = jnp.sum(
             acc[h * HEAD_DIM : (h + 1) * HEAD_DIM, :], axis=0, keepdims=True
         )
     acc[...] = jnp.zeros(acc.shape, jnp.float32)
-
-    def step(j, carry):
-        @pl.when(flags[j] > 0)
+    masks = Masks(docs_ref, starts_ref, column)
+
+    def step(s, carry):
+        block = me + ahead - s
+
+        @pl.when((block >= 0) & (block < size))
         def _():
-            rows, bias = seen_bias(flags, j, blocks, kinfo_ref, qinfo_ref)
-            for g in range(kv_heads):
-                k_at = slice(g * HEAD_DIM, (g + 1) * HEAD_DIM)
-                v_at = slice(kv_width + g * HEAD_DIM, kv_width + (g + 1) * HEAD_DIM)
-                key, val = kv_ref[rows, k_at], kv_ref[rows, v_at]
-                key_t = jnp.transpose(key.astype(jnp.float32)).astype(jnp.bfloat16)
-                dk = jnp.zeros((KEY_ROWS, HEAD_DIM), jnp.float32)
-                dv = jnp.zeros((KEY_ROWS, HEAD_DIM), jnp.float32)
-                for h in range(g * heads // kv_heads, (g + 1) * heads // kv_heads):
-                    at = slice(h * HEAD_DIM, (h + 1) * HEAD_DIM)
-                    q_rows, g_rows = q_ref[:, at], grad_ref[:, at]
-                    scores = bias + lax.dot_general(
-                        key, q_rows, NT, preferred_element_type=jnp.float32
-                    )
-                    probs = jnp.exp(scores - log_ref[h : h + 1, :])
-                    prob_grad = lax.dot_general(
-                        val, g_rows, NT, preferred_element_type=jnp.float32
-                    )
-                    slope = (probs * (prob_grad - delta[h : h + 1, :])).astype(jnp.bfloat16)
-                    dv += jnp.dot(
-                        probs.astype(jnp.bfloat16), g_rows, preferred_element_type=jnp.float32
-                    )
-                    dk += jnp.dot(slope, q_rows, preferred_element_type=jnp.float32)
-                    acc[at, :] += jnp.dot(key_t, slope, preferred_element_type=jnp.float32)
-                dkv_ref[rows, k_at] = dk.astype(dkv_ref.dtype)
-                dkv_ref[rows, v_at] = dv.astype(dkv_ref.dtype)
-
-        @pl.when(flags[j] == 0)
-        def _():
-            rows = pl.ds(pl.multiple_of(j * KEY_ROWS, KEY_ROWS), KEY_ROWS)
-            dkv_ref[rows, :] = jnp.zeros((KEY_ROWS, dkv_ref.shape[1]), dkv_ref.dtype)
+            attend_back_block(
+                masks, block, q_ref, kv_ref.at[block], log_ref, delta, grad_ref, acc,
+                dkv_ref.at[block],
+            )
 
         return carry
 
-    lax.fori_loop(0, blocks, step, 0)
+    lax.fori_loop(0, back + ahead + 1, step, 0)
     dq_ref[...] = jnp.transpose(acc[...]) * (HEAD_DIM**-0.5)
 
 
-def whole_vmem(count):
-    return [pl.BlockSpec(memory_space=pltpu.VMEM)] * count
-
-
-def attend(flags, q, kv, kinfo, qinfo, out_w):
-    rows, width = q.shape
-    heads = width // HEAD_DIM
-    return pl.pallas_call(
-        attend_kernel,
-        name="attend",
-        in_specs=[pl.BlockSpec(memory_space=pltpu.SMEM)] + whole_vmem(5),
-        out_specs=whole_vmem(4),
-        out_shape=[
-            jax.ShapeDtypeStruct((rows, width), jnp.bfloat16),
-            jax.ShapeDtypeStruct((rows, width), jnp.float32),
-            jax.ShapeDtypeStruct((heads, rows), jnp.float32),
-            jax.ShapeDtypeStruct((rows, out_w.shape[1]), jnp.bfloat16),
-        ],
-        scratch_shapes=[
-            pltpu.VMEM((width, rows), jnp.float32),
-            pltpu.VMEM((heads, rows), jnp.float32),
-            pltpu.VMEM((heads, rows), jnp.float32),
-        ],
-        compiler_params=pltpu.CompilerParams(vmem_limit_bytes=LIMIT),
-    )(flags, q, kv, kinfo, qinfo, out_w)
-
-
-def attend_back(flags, q, kv, kinfo, qinfo, log_total, full, grad):
+def attend_back(starts, q, kv, docs, log_total, full, grad, back, ahead):
     rows, width = q.shape
     return pl.pallas_call(
-        attend_back_kernel,
+        functools.partial(attend_back_kernel, back, ahead),
         name="attend_back",
-        in_specs=[pl.BlockSpec(memory_space=pltpu.SMEM)] + whole_vmem(7),
+        in_specs=[pl.BlockSpec(memory_space=pltpu.SMEM)] + whole_vmem(6),
         out_specs=whole_vmem(2),
         out_shape=[
             jax.ShapeDtypeStruct((rows, width), jnp.float32),
@@ -179,24 +176,10 @@
         scratch_shapes=[
             pltpu.VMEM((width, rows), jnp.float32),
             pltpu.VMEM((width // HEAD_DIM, rows), jnp.float32),
+            pltpu.VMEM((rows, 8), jnp.int32),
         ],
         compiler_params=pltpu.CompilerParams(vmem_limit_bytes=LIMIT),
-    )(flags, q, kv, kinfo, qinfo, log_total, full, grad)
-
-
-def block_flags(pic_starts, q_docs, k_docs, offset):
-    block_len, length = q_docs.shape[0], k_docs.shape[0]
-    docs = k_docs.reshape(length // KEY_ROWS, KEY_ROWS)
-    first = jnp.arange(length // KEY_ROWS, dtype=jnp.int32) * KEY_ROWS
-    same = (docs[:, 0] <= q_docs[-1]) & (docs[:, -1] >= q_docs[0])
-    spans = (
-        (pic_starts[None, :] < offset + block_len)
-        & (pic_starts[None, :] + PIC > offset)
-        & (pic_starts[None, :] < first[:, None] + KEY_ROWS)
-        & (pic_starts[None, :] + PIC > first[:, None])
-    )
-    needed = same & ((first < offset + block_len) | jnp.any(spans, axis=1))
-    return jnp.concatenate([needed.astype(jnp.int32), offset[None].astype(jnp.int32)])
+    )(starts, q, kv, docs, log_total, full, grad)
 
 
 MESH = pl.DeviceIdType.MESH
@@ -284,42 +267,6 @@
     )
 
 
-def spread_kernel(axes_of, *refs):
-    count = len(axes_of)
-    ins, outs, sems = refs[:count], refs[count : 2 * count], refs[2 * count :]
-    greet(sorted(set(axes_of)))
-
-    def copy(i, k):
-        return remote(
-            ins[i],
-            outs[i].at[lax.axis_index(axes_of[i])],
-            sems[2 * i : 2 * i + 2],
-            k,
-            {axes_of[i]: ahead_on(axes_of[i], k)},
-        )
-
-    for i in range(count):
-        each(lax.axis_size(axes_of[i]), lambda k, i=i: copy(i, k).start())
-    for i in range(count):
-        outs[i][lax.axis_index(axes_of[i])] = ins[i][...]
-    for i in range(count):
-        each(lax.axis_size(axes_of[i]), lambda k, i=i: copy(i, k).wait())
-
-
-def spread(arrays, axes_of, ident):
-    sizes = [lax.axis_size(axis) for axis in axes_of]
-    return pl.pallas_call(
-        functools.partial(spread_kernel, tuple(axes_of)),
-        in_specs=whole_vmem(len(arrays)),
-        out_specs=whole_vmem(len(arrays)),
-        out_shape=[
-            jax.ShapeDtypeStruct((size,) + a.shape, a.dtype) for size, a in zip(sizes, arrays)
-        ],
-        scratch_shapes=sum([sem_pair(size) for size in sizes], []),
-        compiler_params=remote_params(ident),
-    )(*arrays)
-
-
 def turn(tile, cosine, sine):
     lane = lax.broadcasted_iota(jnp.int32, tile.shape, 1)
     half = HEAD_DIM // 2
@@ -386,168 +333,6 @@
             self.relay(k).wait()
 
         each(self.size, one)
-
-
-def project_kernel(
-    back, ahead, q_width, x_ref, w_ref, gain_ref, cos_ref, sin_ref, cot_ref, normed_ref, q_ref,
-    all_ref, cot_all_ref, kv_ref, line_send, line_recv, dp_send, dp_recv, tp_send, tp_recv,
-):
-    me, size = lax.axis_index("ctx"), lax.axis_size("ctx")
-    greet(["dp", "tp"], line=True)
-    rows_of = RowGather(cot_ref, cot_all_ref, (dp_send, dp_recv), (tp_send, tp_recv), 0)
-    rows_of.start()
-    x = x_ref[...].astype(jnp.float32)
-    normed_ref[...] = (x * row_scale(x) * gain_ref[...]).astype(jnp.bfloat16)
-    kv_width = kv_ref.shape[1] // 2
-    wide = 2 * HEAD_DIM
-    for first in range(q_width, q_width + 2 * kv_width, wide):
-        tile = jnp.dot(
-            normed_ref[...], w_ref[:, first : first + wide], preferred_element_type=jnp.float32
-        )
-        if first < q_width + kv_width:
-            tile = turn(tile, cos_ref[...], -sin_ref[...])
-        kv_ref[:, first - q_width : first - q_width + wide] = tile.astype(jnp.bfloat16)
-
-    sems = (line_send, line_recv)
-    right, left = me + 1, me - 1
-
-    def hop(s):
-        block = lax.rem(me + size - s, size)
-        return remote(
-            kv_ref if s == 0 else all_ref.at[block], all_ref.at[block], sems, s, {"ctx": right}
-        )
-
-    def arrive(s):
-        return remote(kv_ref, all_ref.at[me], sems, s, {"ctx": right})
-
-    def back_hop():
-        return remote(kv_ref, all_ref.at[me], sems, back, {"ctx": left})
-
-    if ahead:
-
-        @pl.when(left >= 0)
-        def _():
-            back_hop().start()
-
-    for s in range(back):
-
-        @pl.when((right < size) & (me - s >= 0))
-        def _(s=s):
-            hop(s).start()
-
-        if s == 0:
-            all_ref[me] = kv_ref[...]
-            for first in range(0, q_width, wide):
-                tile = jnp.dot(
-                    normed_ref[...],
-                    w_ref[:, first : first + wide],
-                    preferred_element_type=jnp.float32,
-                )
-                tile = turn(tile, cos_ref[...], -sin_ref[...]).astype(jnp.bfloat16)
-                q_ref[:, first : first + wide] = (
-                    tile.astype(jnp.float32) * HEAD_DIM**-0.5
-                ).astype(jnp.bfloat16)
-
-        @pl.when(me - s - 1 >= 0)
-        def _(s=s):
-            arrive(s).wait_recv()
-
-    rows_of.forward()
-    for s in range(back):
-
-        @pl.when((right < size) & (me - s >= 0))
-        def _(s=s):
-            hop(s).wait_send()
-
-    if ahead:
-
-        @pl.when(left >= 0)
-        def _():
-            back_hop().wait_send()
-
-        @pl.when(right < size)
-        def _():
-            back_hop().wait_recv()
-
-    cot_all_ref[lax.axis_index("dp")] = cot_ref[...]
-    rows_of.finish()
-
-
-def project(x, w, gain, cosine, sine, cot, q_width, back, ahead, ident):
-    rows, width = x.shape
-    kv_cols = w.shape[1] - q_width
-    dp_size, ctx_size = lax.axis_size("dp"), lax.axis_size("ctx")
-    low = jnp.bfloat16
-    return pl.pallas_call(
-        functools.partial(project_kernel, back, ahead, q_width),
-        name="project",
-        in_specs=whole_vmem(6),
-        out_specs=whole_vmem(4),
-        out_shape=[
-            jax.ShapeDtypeStruct((rows, width), low),
-            jax.ShapeDtypeStruct((rows, q_width), low),
-            jax.ShapeDtypeStruct((ctx_size, rows, kv_cols), low),
-            jax.ShapeDtypeStruct((dp_size, rows, width), low),
-        ],
-        scratch_shapes=[
-            pltpu.VMEM((rows, kv_cols), low),
-            *sem_pair(back + 1),
-            *sem_pair(dp_size),
-            *sem_pair(dp_size),
-        ],
-        compiler_params=remote_params(ident),
-    )(x, w, gain, cosine, sine, cot)
-
-
-def share_rows_kernel(
-    part_ref, x_ref, gain_ref, hidden_ref, all_ref, held, normed, dp_send, dp_recv, tp_send,
-    tp_recv,
-):
-    mine, theirs = halves(part_ref.shape[0])
-    greet(["dp", "tp"])
-    rows_of = RowGather(normed, all_ref, (dp_send, dp_recv), (tp_send, tp_recv), 1)
-    first = remote(part_ref.at[theirs], held.at[theirs], (tp_send, tp_recv), 0, other_core())
-    second = remote(part_ref.at[mine], held.at[mine], (tp_send, tp_recv), 1, other_core())
-    first.start()
-    second.start()
-
-    def norm(rows):
-        total = x_ref[rows, :].astype(jnp.float32) + (
-            part_ref[rows, :].astype(jnp.float32) + held[rows, :].astype(jnp.float32)
-        )
-        hidden_ref[rows, :] = total
-        normed[rows, :] = (total * row_scale(total) * gain_ref[...]).astype(jnp.bfloat16)
-
-    first.wait()
-    norm(mine)
-    rows_of.start()
-    second.wait()
-    norm(theirs)
-    all_ref[lax.axis_index("dp")] = normed[...]
-    rows_of.forward()
-    rows_of.finish()
-
-
-def share_rows(part, x, gain, ident):
-    size = lax.axis_size("dp")
-    rows, width = part.shape
-    return pl.pallas_call(
-        share_rows_kernel,
-        name="share_rows",
-        in_specs=whole_vmem(3),
-        out_specs=whole_vmem(2),
-        out_shape=[
-            jax.ShapeDtypeStruct((rows, width), jnp.float32),
-            jax.ShapeDtypeStruct((size, rows, width), jnp.bfloat16),
-        ],
-        scratch_shapes=[
-            pltpu.VMEM((rows, width), jnp.bfloat16),
-            pltpu.VMEM((rows, width), jnp.bfloat16),
-            *sem_pair(size),
-            *sem_pair(size + 1),
-        ],
-        compiler_params=remote_params(ident),
-    )(part, x, gain)
 
 
 class RowReturn:
@@ -633,14 +418,22 @@
 
     def turn_back(at, grads):
         x_grad, gain_grad = norm_back(
-            hidden_ref[at, :], gain_ref[...], grads.astype(jnp.float32)
+            hidden_ref[at, :], gain_ref[1:2, :], grads.astype(jnp.float32)
         )
         hidden_grad = cot_ref[at, :].astype(jnp.float32) + x_grad
         grad_ref[at, :] = hidden_grad
         low_ref[at, :] = hidden_grad.astype(jnp.bfloat16)
-        mix_ref[at, :] = lax.dot_general(
-            low_ref[at, :], out_w_ref[...], NT, preferred_element_type=jnp.float32
-        ).astype(jnp.bfloat16)
+        piece = out_w_ref.shape[2]
+        mix = None
+        for i in range(out_w_ref.shape[0]):
+            one = lax.dot_general(
+                low_ref[at, i * piece : (i + 1) * piece],
+                out_w_ref[i],
+                NT,
+                preferred_element_type=jnp.float32,
+            )
+            mix = one if mix is None else mix + one
+        mix_ref[at, :] = mix.astype(jnp.bfloat16)
         return gain_grad
 
     gain_mine = turn_back(rows.mine, sent[...])
@@ -659,7 +452,7 @@
         out_shape=[
             jax.ShapeDtypeStruct((rows, width), jnp.float32),
             jax.ShapeDtypeStruct((rows, width), jnp.bfloat16),
-            jax.ShapeDtypeStruct((rows, out_w.shape[0]), jnp.bfloat16),
+            jax.ShapeDtypeStruct((rows, out_w.shape[1]), jnp.bfloat16),
             jax.ShapeDtypeStruct((1, width), jnp.float32),
         ],
         scratch_shapes=return_scratch(size, rows, width),
@@ -857,9 +650,10 @@
         w_sum.send(k)
 
     each(w_sum.size, piece)
-    part[...] = lax.dot_general(
-        joined[...], w_ref[...], NT, preferred_element_type=jnp.float32
-    ).astype(jnp.bfloat16)
+    for i in range(w_ref.shape[0]):
+        part[:, i * rows : (i + 1) * rows] = lax.dot_general(
+            joined[...], w_ref[i], NT, preferred_element_type=jnp.float32
+        ).astype(jnp.bfloat16)
     swap = remote(part, held, pairs[2], 0, other_core())
     swap.start()
     me = lax.axis_index("dp")
@@ -870,7 +664,7 @@
     swap.wait()
     x_grad, gain_grad = norm_back(
         x_ref[...].astype(jnp.float32),
-        gain_ref[...],
+        gain_ref[0:1, :],
         part[...].astype(jnp.float32) + held[...].astype(jnp.float32),
     )
     in_ref[...] = (hidden_ref[...] + x_grad).astype(jnp.bfloat16)
@@ -902,7 +696,7 @@
 def finish(dq, dkv, cosine, sine, normed, w, x, gain, hidden_grad, out_w, gain_two, ident):
     rows, width = x.shape
     dp_size, ctx_size = lax.axis_size("dp"), lax.axis_size("ctx")
-    cols, out_cols = w.shape[1], out_w.shape[2]
+    cols, out_cols = w.shape[2], out_w.shape[2]
     few = width // dp_size // ctx_size
     low, high = jnp.bfloat16, jnp.float32
     return pl.pallas_call(
@@ -940,6 +734,291 @@
     )(dq, dkv, cosine, sine, normed, w, x, gain, hidden_grad, out_w, gain_two)
 
 
+class Everyone:
+    def __init__(self, axis, target, sems):
+        self.axis, self.target, self.sems = axis, target, sems
+        self.size = lax.axis_size(axis)
+
+    def copy(self, k):
+        at = self.target.at[lax.axis_index(self.axis)]
+        return remote(at, at, self.sems, k, {self.axis: ahead_on(self.axis, k)})
+
+    def start(self):
+        each(self.size, lambda k: self.copy(k).start())
+
+    def arrive(self):
+        each(self.size, lambda k: self.copy(k).wait_recv())
+
+    def finish(self):
+        each(self.size, lambda k: self.copy(k).wait_send())
+
+
+def find_places(first, own, routes_ref, gates_ref, earlier, place_ref, gate_ref, column_ref):
+    _, tokens = routes_ref.shape[1:]
+
+    def group(g, carry):
+        routes, gates = routes_ref[g], gates_ref[g]
+        names, values = [], []
+        for e in range(own):
+            named = routes == first + e
+            names.append(jnp.max(named.astype(jnp.float32), axis=0, keepdims=True))
+            values.append(jnp.sum(jnp.where(named, gates, 0.0), axis=0, keepdims=True))
+        spare = jnp.zeros((8 - own % 8 if own % 8 else 0, tokens), jnp.float32)
+        names = jnp.concatenate(names + ([spare] if spare.shape[0] else []), axis=0)
+        place = jnp.dot(
+            names.astype(jnp.bfloat16), earlier[...], preferred_element_type=jnp.float32
+        )
+        place = jnp.where((names > 0.0) & (place < CAP), place, -float(CAP * own))
+        for e in range(own):
+            place_ref[g, e] = place[e : e + 1].astype(jnp.int32)
+            gate_ref[g, e] = values[e]
+        column_ref[g] = jnp.transpose(place)[:, :own].astype(jnp.int32)
+        return carry
+
+    lax.fori_loop(0, routes_ref.shape[0], group, 0)
+
+
+def front_kernel(
+    back, ahead, own, starts_ref, x_ref, cot_ref, q_w_ref, k_w_ref, v_w_ref, out_w_ref, gains_ref,
+    docs_ref, routes_ref, gates_ref, cos_ref, sin_ref, w_all, out_w_all, gain_rows, docs_all,
+    normed_ref, q_ref, kv_all, mix_ref, full_ref, log_ref, hidden_ref, rows_all, cot_all,
+    place_ref, gate_ref, column_ref, gains_all, routes_all, gates_all, acc, top, total, column,
+    part, held, normed_two, earlier, *sems,
+):
+    me, size = lax.axis_index("ctx"), lax.axis_size("ctx")
+    dp = lax.axis_index("dp")
+    pairs = [sems[2 * i : 2 * i + 2] for i in range(len(sems) // 2)]
+    q_width, kv_width = q_w_ref.shape[1], k_w_ref.shape[1]
+    dp_size, piece = w_all.shape[:2]
+    w_all[dp, :, :q_width] = q_w_ref[...]
+    w_all[dp, :, q_width : q_width + kv_width] = k_w_ref[...]
+    w_all[dp, :, q_width + kv_width :] = v_w_ref[...]
+    gains_all[dp] = gains_ref[...]
+    docs_all[me] = docs_ref[...]
+    routes_all[dp] = routes_ref[...]
+    gates_all[dp] = gates_ref[...]
+    out_w_all[dp] = out_w_ref[...]
+    greet(["dp", "ctx", "tp"])
+    gains = Everyone("dp", gains_all, pairs[0])
+    weights = Everyone("dp", w_all, pairs[1])
+    docs = Everyone("ctx", docs_all, pairs[2])
+    routes = Everyone("dp", routes_all, pairs[3])
+    gates = Everyone("dp", gates_all, pairs[4])
+    out_w = Everyone("dp", out_w_all, pairs[5])
+    for one in (gains, weights, docs, routes, gates):
+        one.start()
+
+    token = lax.broadcasted_iota(jnp.int32, earlier.shape, 0)
+    later = lax.broadcasted_iota(jnp.int32, earlier.shape, 1)
+    earlier[...] = (token < later).astype(jnp.float32).astype(jnp.bfloat16)
+    top[...] = jnp.full(top.shape, NEG_FILL, jnp.float32)
+    total[...] = jnp.zeros(total.shape, jnp.float32)
+    acc[...] = jnp.zeros(acc.shape, jnp.float32)
+    gains.arrive()
+    for i in range(dp_size):
+        gain_rows[:, i * piece : (i + 1) * piece] = gains_all[i]
+    x = x_ref[...].astype(jnp.float32)
+    normed_ref[...] = (x * row_scale(x) * gain_rows[0:1, :]).astype(jnp.bfloat16)
+    routes.arrive()
+    gates.arrive()
+    docs.arrive()
+    find_places(dp * own, own, routes_all, gates_all, earlier, place_ref, gate_ref, column_ref)
+    weights.arrive()
+    out_w.start()
+    cot_rows = RowGather(cot_ref, cot_all, pairs[6], pairs[7], 0)
+    cot_rows.start()
+
+    wide, tile = 4 * HEAD_DIM, 2 * HEAD_DIM
+
+    def project(first):
+        whole = jnp.dot(
+            normed_ref[:, :piece], w_all[0, :, first : first + wide],
+            preferred_element_type=jnp.float32,
+        )
+        for i in range(1, dp_size):
+            whole += jnp.dot(
+                normed_ref[:, i * piece : (i + 1) * piece], w_all[i, :, first : first + wide],
+                preferred_element_type=jnp.float32,
+            )
+        return [whole[:, :tile], whole[:, tile:]]
+
+    for first in range(q_width, q_width + 2 * kv_width, wide):
+        for i, part_of in enumerate(project(first)):
+            if first < q_width + kv_width:
+                part_of = turn(part_of, cos_ref[...], -sin_ref[...])
+            at = first - q_width + i * tile
+            kv_all[me, :, at : at + tile] = part_of.astype(jnp.bfloat16)
+
+    right, left = me + 1, me - 1
+    line = pairs[8]
+
+    def hop(s):
+        at = kv_all.at[lax.rem(me + size - s, size)]
+        return remote(at, at, line, s, {"ctx": right})
+
+    def back_hop():
+        return remote(kv_all.at[me], kv_all.at[me], line, back, {"ctx": left})
+
+    if back:
+
+        @pl.when(right < size)
+        def _():
+            hop(0).start()
+
+    if ahead:
+
+        @pl.when(left >= 0)
+        def _():
+            back_hop().start()
+
+    for first in range(0, q_width, wide):
+        for i, part_of in enumerate(project(first)):
+            turned = turn(part_of, cos_ref[...], -sin_ref[...]).astype(jnp.bfloat16)
+            at = first + i * tile
+            q_ref[:, at : at + tile] = (turned.astype(jnp.float32) * HEAD_DIM**-0.5).astype(
+                jnp.bfloat16
+            )
+    masks = Masks(docs_all, starts_ref, column)
+
+    def visit(s):
+        @pl.when(me - s >= 0)
+        def _():
+            block = lax.rem(me + size - s, size)
+
+            @pl.when(s > 0)
+            def _():
+                hop(s - 1).wait_recv()
+
+            @pl.when((s > 0) & (s < back) & (right < size))
+            def _():
+                hop(s).start()
+
+            attend_block(masks, block, q_ref, kv_all.at[block], acc, top, total)
+
+    each(back + 1, visit, 0)
+    if ahead:
+
+        @pl.when(right < size)
+        def _():
+            block = lax.rem(me + 1, size)
+            back_hop().wait_recv()
+            attend_block(masks, block, q_ref, kv_all.at[block], acc, top, total)
+
+    log_ref[...] = top[...] + jnp.log(total[...])
+    for h in range(total.shape[0]):
+        at = slice(h * HEAD_DIM, (h + 1) * HEAD_DIM)
+        acc[at, :] = acc[at, :] / total[h : h + 1, :]
+    full_ref[...] = jnp.transpose(acc[...])
+    mix_ref[...] = full_ref[...].astype(jnp.bfloat16)
+    out_w.arrive()
+    for i in range(dp_size):
+        part[:, i * piece : (i + 1) * piece] = jnp.dot(
+            mix_ref[...], out_w_all[i], preferred_element_type=jnp.float32
+        ).astype(jnp.bfloat16)
+
+    mine, theirs = halves(part.shape[0])
+    rows = RowGather(normed_two, rows_all, pairs[9], pairs[10], 1)
+    first = remote(part.at[theirs], held.at[theirs], pairs[10], 0, other_core())
+    second = remote(part.at[mine], held.at[mine], pairs[10], 1, other_core())
+    first.start()
+    second.start()
+
+    def norm(at):
+        whole = x_ref[at, :].astype(jnp.float32) + (
+            part[at, :].astype(jnp.float32) + held[at, :].astype(jnp.float32)
+        )
+        hidden_ref[at, :] = whole
+        normed_two[at, :] = (whole * row_scale(whole) * gain_rows[1:2, :]).astype(jnp.bfloat16)
+
+    first.wait()
+    norm(mine)
+    rows.start()
+    second.wait()
+    norm(theirs)
+    rows_all[dp] = normed_two[...]
+    cot_all[dp] = cot_ref[...]
+    cot_rows.forward()
+    rows.forward()
+    for one in (gains, weights, docs, routes, gates, out_w):
+        one.finish()
+
+    def sent(s):
+        @pl.when((right < size) & (me - s >= 0))
+        def _():
+            hop(s).wait_send()
+
+    each(back, sent, 0)
+    if ahead:
+
+        @pl.when(left >= 0)
+        def _():
+            back_hop().wait_send()
+
+    cot_rows.finish()
+    rows.finish()
+
+
+def front(
+    starts, x, cot, q_w, k_w, v_w, out_w, gains, docs, routes, gates, cosine, sine, own, back,
+    ahead, ident,
+):
+    rows, width = x.shape
+    dp_size, ctx_size = lax.axis_size("dp"), lax.axis_size("ctx")
+    q_width, kv_cols = q_w.shape[1], 2 * k_w.shape[1]
+    piece, heads = q_w.shape[0], q_width // HEAD_DIM
+    low, high, whole = jnp.bfloat16, jnp.float32, jnp.int32
+    shapes = [
+        ((dp_size, piece, q_width + kv_cols), low),
+        ((dp_size,) + out_w.shape, low),
+        ((2, width), high),
+        ((ctx_size, 1, rows), whole),
+        ((rows, width), low),
+        ((rows, q_width), low),
+        ((ctx_size, rows, kv_cols), low),
+        ((rows, q_width), low),
+        ((rows, q_width), high),
+        ((heads, rows), high),
+        ((rows, width), high),
+        ((dp_size, rows, width), low),
+        ((dp_size, rows, width), low),
+        ((dp_size, own, 1, rows), whole),
+        ((dp_size, own, 1, rows), high),
+        ((dp_size, rows, own), whole),
+    ]
+    return pl.pallas_call(
+        functools.partial(front_kernel, back, ahead, own),
+        name="front",
+        in_specs=[pl.BlockSpec(memory_space=pltpu.SMEM)] + whole_vmem(12),
+        out_specs=whole_vmem(len(shapes)),
+        out_shape=[jax.ShapeDtypeStruct(*shape) for shape in shapes],
+        scratch_shapes=[
+            pltpu.VMEM((dp_size,) + gains.shape, high),
+            pltpu.VMEM((dp_size,) + routes.shape, whole),
+            pltpu.VMEM((dp_size,) + gates.shape, high),
+            pltpu.VMEM((q_width, rows), high),
+            pltpu.VMEM((heads, rows), high),
+            pltpu.VMEM((heads, rows), high),
+            pltpu.VMEM((rows, 8), whole),
+            pltpu.VMEM((rows, width), low),
+            pltpu.VMEM((rows, width), low),
+            pltpu.VMEM((rows, width), low),
+            pltpu.VMEM((rows, rows), low),
+            *sem_pair(dp_size),
+            *sem_pair(dp_size),
+            *sem_pair(ctx_size),
+            *sem_pair(dp_size),
+            *sem_pair(dp_size),
+            *sem_pair(dp_size),
+            *sem_pair(dp_size),
+            *sem_pair(dp_size),
+            *sem_pair(back + 1),
+            *sem_pair(dp_size),
+            *sem_pair(dp_size + 1),
+        ],
+        compiler_params=remote_params(ident),
+    )(starts, x, cot, q_w, k_w, v_w, out_w, gains, docs, routes, gates, cosine, sine)
+
+
 GROUPS_AT_ONCE = 4
 
 
@@ -1015,26 +1094,9 @@
                 to_ref[g] = total.astype(jnp.bfloat16)
 
 
-def expert_places(chosen_all, gates_all, own):
-    tok_rows = chosen_all.shape[1]
-    named = chosen_all[..., None] == lax.axis_index("dp") * own + jnp.arange(own, dtype=jnp.int32)
-    names = jnp.any(named, axis=2)
-    gate_of = jnp.sum(jnp.where(named, gates_all[..., None], 0.0), axis=2)
-    earlier = jnp.tril(jnp.ones((tok_rows, tok_rows), jnp.bfloat16), -1)
-    place = jnp.einsum(
-        "rq,gqe->gre", earlier, names.astype(jnp.bfloat16), preferred_element_type=jnp.float32
-    ).astype(jnp.int32)
-    place = jnp.where(names & (place < CAP), place, -CAP * own)
-    return (
-        place,
-        place.transpose(0, 2, 1)[:, :, None],
-        gate_of.transpose(0, 2, 1)[:, :, None],
-    )
-
-
 def experts(weights, places, rows_all, grad_all, first, count, before):
     _, _, model_width, hidden = weights.shape
-    place_cols, place_rows, gate_rows = places
+    place_rows, gate_rows, place_cols = places
     groups, tok_rows, _ = rows_all.shape
     owners = lax.axis_size("ctx")
     at_once = min(GROUPS_AT_ONCE, groups)
@@ -1096,14 +1158,6 @@
     )
 
 
-def picture_of(starts, token_positions):
-    inside = (token_positions[:, None] >= starts[None, :]) & (
-        token_positions[:, None] < starts[None, :] + PIC
-    )
-    labels = jnp.arange(starts.shape[0], dtype=jnp.int32) + 1
-    return jnp.sum(jnp.where(inside, labels[None, :], 0), axis=-1) - 1
-
-
 def rotary_tables(token_positions):
     half_dim = HEAD_DIM // 2
     inverse = THETA ** (-(jnp.arange(half_dim, dtype=jnp.float32) * 2.0 / HEAD_DIM))
@@ -1127,8 +1181,8 @@
     pic_starts,
     cotangent,
 ):
-    _, block_len, model_width = tokens.shape
-    dp_size, ctx_size = lax.axis_size("dp"), lax.axis_size("ctx")
+    block_len = tokens.shape[1]
+    ctx_size = lax.axis_size("ctx")
     length = block_len * ctx_size
     offset = lax.axis_index("ctx") * block_len
     back = back_blocks(ctx_size, block_len, length)
@@ -1137,41 +1191,41 @@
     own = expert_weights.shape[0]
     x, cot = tokens[0], cotangent[0]
 
-    joined_w = jnp.concatenate([query_weight, key_weight, value_weight], axis=1)
-    gains = jnp.stack([gain_attn, gain_moe]).astype(jnp.float32)
-    joined_all, gains_all, docs_all, chosen_all, gates_all = spread(
-        [
-            joined_w,
-            gains,
-            documents,
-            routes.reshape(block_len * TOP // 128, 128),
-            gate_values.reshape(block_len * TOP // 128, 128),
-        ],
-        ["dp", "dp", "ctx", "dp", "dp"],
+    cosine, sine = rotary_tables(offset + jnp.arange(block_len, dtype=jnp.int32))
+    (
+        w_all,
+        out_w_all,
+        gain_rows,
+        docs_all,
+        normed_one,
+        query,
+        kv_all,
+        mixture,
+        mix_full,
+        log_total,
+        hidden,
+        rows_all,
+        grad_all,
+        *places,
+    ) = front(
+        pic_starts,
+        x,
+        cot,
+        query_weight,
+        key_weight,
+        value_weight,
+        output_weight,
+        jnp.stack([gain_attn, gain_moe]).astype(jnp.float32),
+        documents,
+        routes[0].T,
+        gate_values[0].T,
+        cosine,
+        sine,
+        own,
+        back,
+        ahead,
         1,
     )
-    output_weight, joined_all = lax.optimization_barrier((output_weight, joined_all))
-    output_full = lax.all_gather(output_weight, "dp", axis=1, tiled=True)
-    joined_full = joined_all.reshape(model_width, -1)
-    gain_rows = gains_all.transpose(1, 0, 2).reshape(2, 1, model_width)
-    docs_all = docs_all.reshape(length)
-    cosine, sine = rotary_tables(offset + jnp.arange(block_len, dtype=jnp.int32))
-    normed_one, query, kv_all, grad_all = project(
-        x, joined_full, gain_rows[0], cosine, sine, cot, q_width, back, ahead, 2
-    )
-    kv_all = kv_all.reshape(length, 2 * kv_width)
-
-    pictures = picture_of(pic_starts[0], jnp.arange(length, dtype=jnp.int32))
-    flags = block_flags(pic_starts[0], documents[0], docs_all, offset)
-    kinfo = jnp.stack([docs_all, pictures], axis=1)
-    qinfo = jnp.stack([documents[0], lax.dynamic_slice_in_dim(pictures, offset, block_len)])
-    places = expert_places(
-        chosen_all.reshape(dp_size, block_len, TOP), gates_all.reshape(dp_size, block_len, TOP), own
-    )
-    mixture, mix_full, log_total, attn_part = attend(
-        flags, query, kv_all, kinfo, qinfo, output_full
-    )
-    hidden, rows_all = share_rows(attn_part, x, gain_rows[1], 3)
     half = own // 2
     parts, grads_one = experts(expert_weights, places, rows_all, grad_all, 0, half, None)
     expert_one = lax.psum_scatter(grads_one, "ctx", scatter_dimension=0)
@@ -1179,20 +1233,20 @@
         expert_weights, places, rows_all, grad_all, half, own - half, parts
     )
     hidden_grad, hidden_low, mix_grad, gain_two_grad = return_grads(
-        back_part, hidden, cot, gain_rows[1], output_full, 4
+        back_part, hidden, cot, gain_rows, out_w_all, 2
     )
     q_rot_grad, kv_part = attend_back(
-        flags, query, kv_all, kinfo, qinfo, log_total, mix_full, mix_grad
+        pic_starts, query, kv_all, docs_all, log_total, mix_full, mix_grad, back, ahead
     )
     kv_back, layer_out, output_grad = trade(
-        kv_part.reshape(ctx_size, block_len, 2 * kv_width),
+        kv_part,
         out_part,
         hidden,
         hidden_low,
         mixture,
         back,
         ahead,
-        5,
+        3,
     )
     grads_two, kv_back = lax.optimization_barrier((grads_two, kv_back))
     expert_two = lax.psum_scatter(grads_two, "ctx", scatter_dimension=0)
@@ -1202,13 +1256,13 @@
         cosine,
         sine,
         normed_one,
-        joined_full,
+        w_all,
         x,
-        gain_rows[0],
+        gain_rows,
         hidden_grad,
         output_grad,
         gain_two_grad,
-        6,
+        4,
     )
     few = owned.shape[0]
     here = (lax.axis_index("dp") * ctx_size + lax.axis_index("ctx")) * few

time: 594 us -> 560 us (0.943)
  Pallas kernels: 383 us -> 364 us
  local copies, waits for them, and re-layouts: 27.7 us -> 17.6 us
  other arithmetic: 15 us -> 7.8 us
    pallas_call x5 -> x2, Pallas kernels: 130 us -> 113 us  [the longest x1 102 us: front(): pl.pallas_call(functools.partial(front_kernel, back, ahead, own), name='f...]
  transfers between devices with their start and end apart: 3 -> 2, of which waited for: 2 -> 2; matrix products, arithmetic and copies ran while one was open for 4% -> 1% of each run, Pallas kernels for 22% -> 16%
where the time goes in v6:
time: 560 us; the launch traced here: 553 us
  Pallas kernels  364 us (65%)
  waiting for transfers between devices  149 us (27%)
  local copies, waits for them, and re-layouts  17.6 us (3%)
  between operations  14.4 us (3%)
  other arithmetic  7.8 us (1%)
    reduce_scatter x1, waiting for transfers between devices, body(): expert_one = lax.psum_scatter(grads_one, 'ctx', scatter_dimension=0)  118 us
    pallas_call x1, Pallas kernels, front(): pl.pallas_call(functools.partial(front_kernel, back, ahead, own), name='f...  102 us
    pallas_call x1, Pallas kernels, finish(): pl.pallas_call(finish_kernel, name='finish', in_specs=whole_vmem(11), out...  91 us
    pallas_call x2, Pallas kernels, experts(): pl.pallas_call(functools.partial(experts_kernel, more), name='experts', g...  74.1 us
    pallas_call x1, Pallas kernels, trade(): pl.pallas_call(functools.partial(trade_kernel, back, ahead), name='trade'...  49.6 us
    pallas_call x1, Pallas kernels, return_grads(): pl.pallas_call(return_grads_kernel, name='return_grads', in_specs=whole_v...  36 us
    reduce_scatter x1, waiting for transfers between devices, body(): expert_two = lax.psum_scatter(grads_two, 'ctx', scatter_dimension=0)  30.7 us
    pallas_call x1, Pallas kernels, attend_back(): pl.pallas_call(functools.partial(attend_back_kernel, back, ahead), name='...  11.7 us
  transfers between devices with their start and end apart: 2, of which 2 were waited for; matrix products, arithmetic and copies ran while one was open for 1% of the time, Pallas kernels for 16%

profile of v6, /device:TPU:0, one launch (start us, length us, event | category | flops | bytes accessed | tf_op | source)
XLA Modules:
  0.0 553.1 jit_solution(16620656998376642280)
XLA Ops:
  7.2 0.0 reduce-scatter.5.cloned.1.call-start
  7.2 0.7 stack.9
  7.9 0.7 stack.10
  8.6 0.6 maximum_convert_fusion.gains_ref
  9.2 1.0 multiply_sine_fusion
  10.1 1.3 pad_maximum_fusion
  11.4 101.8 %front.1 = (bf16[4,256,1024]{2,1,0:T(8,128)(2,1)}, bf16[4,512,256]{2,1,0:T(8,128)(2,1)}, f32[2,1024]{1,0:T(2,128)}, s32[4,1,512]{2,1,0:T(1,128)}, bf16[512,1024]...) custom-call(s32[1,4]{1,0:T(1,128)} %starts_ref.3, ...), custom_call_target="tpu_custom_call" | custom-call | tf_op jit(solution)/shard_map/front/pallas_call | solution.py:988
  113.2 3.2 fusion.1
  116.4 35.9 %experts.2 = (bf16[4,512,1024]{2,1,0:T(8,128)(2,1)}, bf16[4,512,1024]{2,1,0:T(8,128)(2,1)}, bf16[1,4,4,3,256,256]{5,4,3,2,1,0:T(8,128)(2,1)}) custom-call(bf16[4,512,1024]{2,1,0:T(8,128)(2,1)} %get-tuple-element.50.rows_ref, bf16[4,512,1024]{2,1,0:T(8,128)(2,1)} %get-tuple-element.51.grads_ref, bf16[8,3,1024,256]{3,2,1,0:T(8,128)(2,1)} %weights_ref.3, ...), custom_call_target="tpu_custom_call" | custom-call | flops 20535312384 | bytes 25165824 | tf_op jit(solution)/shard_map/experts/pallas_call | solution.py:1112
  152.3 38.2 %experts.3 = (bf16[4,512,1024]{2,1,0:T(8,128)(2,1)}, bf16[4,512,1024]{2,1,0:T(8,128)(2,1)}, bf16[1,4,4,3,256,256]{5,4,3,2,1,0:T(8,128)(2,1)}) custom-call(bf16[4,512,1024]{2,1,0:T(8,128)(2,1)} %get-tuple-element.50.rows_ref, bf16[4,512,1024]{2,1,0:T(8,128)(2,1)} %get-tuple-element.51.grads_ref, bf16[8,3,1024,256]{3,2,1,0:T(8,128)(2,1)} %weights_ref.3, ...), custom_call_target="tpu_custom_call" | custom-call | flops 20535312384 | bytes 25165824 | tf_op jit(solution)/shard_map/experts/pallas_call | solution.py:1112
  190.5 36.0 %return_grads.1 = (f32[512,1024]{1,0:T(8,128)}, bf16[512,1024]{1,0:T(8,128)(2,1)}, bf16[512,512]{1,0:T(8,128)(2,1)}, f32[1,1024]{1,0:T(1,128)}) custom-call(bf16[4,512,1024]{2,1,0:T(8,128)(2,1)} %get-tuple-element.57.part_ref, f32[512,1024]{1,0:T(8,128)} %get-tuple-element.58.hidden_ref, bf16[512,1024]{1,0:T(8,128)(2,1)} %bitcast.25, ...), custom_call_target="tpu_custom_call" | custom-call | tf_op jit(solution)/shard_map/return_grads/pallas_call | solution.py:447
  226.5 11.7 %attend_back.1 = (f32[512,512]{1,0:T(8,128)}, bf16[4,512,512]{2,1,0:T(8,128)(2,1)}) custom-call(s32[1,4]{1,0:T(1,128)} %starts_ref.3, bf16[512,512]{1,0:T(8,128)(2,1)} %get-tuple-element.45.q_ref, bf16[4,512,512]{2,1,0:T(8,128)(2,1)} %get-tuple-element.46.kv_ref, s32[4,1,512]{2,1,0:T(1,128)} %get-tuple-element.47.docs_ref, ...), custom_call_target="tpu_custom_call" | custom-call | tf_op jit(solution)/shard_map/attend_back/pallas_call | solution.py:167
  238.2 49.6 %trade.1 = (f32[512,512]{1,0:T(8,128)}, bf16[512,1024]{1,0:T(8,128)(2,1)}, bf16[4,256,512]{2,1,0:T(8,128)(2,1)}) custom-call(bf16[4,512,512]{2,1,0:T(8,128)(2,1)} %get-tuple-element.62.kv_grad_ref, bf16[4,512,1024]{2,1,0:T(8,128)(2,1)} %get-tuple-element.63.part_ref, f32[512,1024]{1,0:T(8,128)} %get-tuple-element.58.hidden_ref, ...), custom_call_target="tpu_custom_call" | custom-call | tf_op jit(solution)/shard_map/trade/pallas_call | solution.py:556
  287.7 0.0 reduce-scatter.5.cloned.1.call-update
  287.8 0.0 reduce-scatter.3.cloned.1.call-start
  287.8 0.7 reduce-scatter.3.cloned.1.call-update
  288.5 91.0 %finish.1 = (bf16[512,1024]{1,0:T(8,128)(2,1)}, f32[64,1536]{1,0:T(8,128)}, f32[8,1024]{1,0:T(8,128)}) custom-call(f32[512,512]{1,0:T(8,128)} %get-tuple-element.67.dq_ref, f32[512,512]{1,0:T(8,128)} %get-tuple-element.70.dkv_ref, f32[512,128]{1,0:T(8,128)} %get-tuple-element.110.cos_ref, f32[512,128]{1,0:T(8,128)} %get-tuple-element.111.sin_ref, ...), custom_call_target="tpu_custom_call" | custom-call | tf_op jit(solution)/shard_map/finish/pallas_call | solution.py:702
  379.6 0.8 constant_dynamic-slice_fusion
  380.3 0.5 slice_bitcast_fusion.1
  380.8 1.5 fusion.2
  382.4 1.7 slice_bitcast_fusion
  384.1 30.7 %reduce-scatter.5.cloned.1.call-done = bf16[1,4,3,256,256]{4,3,2,1,0:T(8,128)(2,1)} async-done(((bf16[4,4,3,256,256]{4,3,2,1,0:T(8,128)(2,1)}), bf16[1,4,3,256,256]{4,3,2,1,0:T(8,128)(2,1)}) %reduce-scatter.5.cloned.1.call-update) | async-done | bytes 1572880 | tf_op jit(solution)/shard_map/reduce_scatter | solution.py:1252
  414.8 117.7 %reduce-scatter.3.cloned.1.call-done = bf16[1,4,3,256,256]{4,3,2,1,0:T(8,128)(2,1)} async-done(((bf16[4,4,3,256,256]{4,3,2,1,0:T(8,128)(2,1)}), bf16[1,4,3,256,256]{4,3,2,1,0:T(8,128)(2,1)}) %reduce-scatter.3.cloned.1.call-update) | async-done | bytes 1572880 | tf_op jit(solution)/shard_map/reduce_scatter | solution.py:1231
  532.4 4.9 convert_bitcast_fusion
  537.4 0.0 copy-start
  537.4 0.0 copy-start.1
  537.4 6.7 %copy.24 = f32[8,3,256,256]{3,2,1,0:T(8,128)} copy(f32[8,3,256,256]{2,3,1,0:T(8,128)} %convert_bitcast_fusion) | data formatting | bytes 12582912
  544.1 0.0 copy-done
  544.1 1.0 copy.27
  545.1 0.0 copy-done.1
  545.1 1.0 copy.28
  (2 shorter events, 0.0 us)
Async XLA Ops:
  7.2 407.6 %reduce-scatter.5.cloned.1.call-start = ((), (), s32[]{:S(2)}) async-start(), calls=%async_computation.3 | async-start | bytes 7864320 | tf_op jit(solution)/shard_map/reduce_scatter | solution.py:1252
  287.8 244.7 %reduce-scatter.3.cloned.1.call-start = ((), (), s32[]{:S(2)}) async-start(), calls=%async_computation.2 | async-start | bytes 7864320 | tf_op jit(solution)/shard_map/reduce_scatter | solution.py:1231
  537.4 6.7 %copy-start = (bf16[512,1024]{1,0:T(8,128)(2,1)S(1)}, bf16[512,1024]{1,0:T(8,128)(2,1)}, u32[]{:S(2)}) copy-start(bf16[512,1024]{1,0:T(8,128)(2,1)} %get-tuple-element.66) | copy-start | bytes 3145732
  537.4 7.7 %copy-start.1 = (bf16[512,1024]{1,0:T(8,128)(2,1)S(1)}, bf16[512,1024]{1,0:T(8,128)(2,1)}, u32[]{:S(2)}) copy-start(bf16[512,1024]{1,0:T(8,128)(2,1)} %get-tuple-element.76) | copy-start | bytes 3145732
Sparse Core Ops, SparseCore 0:
  287.9 126.8 reduce-scatter.4
  417.6 114.7 reduce-scatter.2
